TPU v7x, 8 devices: a whole 2x2x1 slice. The times are simulated.
8 devices in a mesh: rep: 2 (over y, z), dp: 4 (over x, core).
Axes of the slice: x: 2, y: 2, z: 1, core: 2. Of those that a mesh axis runs over, the one named last changes fastest.
Arguments:
- x: bfloat16 [8, 2048, 1152], P(('rep', 'dp')), parts along dimension 0
- dy: bfloat16 [8, 2048, 1152], P(('rep', 'dp')), parts along dimension 0
- w_gate: bfloat16 [2, 1152, 4608], replicated
- w_up: bfloat16 [2, 1152, 4608], replicated
- w_down: bfloat16 [2, 4608, 1152], replicated
- m_w_gate: float32 [2, 1152, 4608], P(None, 'dp')
- m_w_up: float32 [2, 1152, 4608], P(None, 'dp')
- m_w_down: float32 [2, 4608, 1152], P(None, 'dp')
- v_w_gate: float32 [2, 1152, 4608], P(None, 'dp')
- v_w_up: float32 [2, 1152, 4608], P(None, 'dp')
- v_w_down: float32 [2, 4608, 1152], P(None, 'dp')
Outputs:
- output 1: bfloat16 [4, 1152, 4608], P('rep'), parts along dimension 0
- output 2: bfloat16 [4, 1152, 4608], P('rep'), parts along dimension 0
- output 3: bfloat16 [4, 4608, 1152], P('rep'), parts along dimension 0
- output 4: float32 [4, 1152, 4608], P('rep', 'dp'), parts along dimension 0
- output 5: float32 [4, 1152, 4608], P('rep', 'dp'), parts along dimension 0
- output 6: float32 [4, 4608, 1152], P('rep', 'dp'), parts along dimension 0
- output 7: float32 [4, 1152, 4608], P('rep', 'dp'), parts along dimension 0
- output 8: float32 [4, 1152, 4608], P('rep', 'dp'), parts along dimension 0
- output 9: float32 [4, 4608, 1152], P('rep', 'dp'), parts along dimension 0
There are 2 independent parts. A program takes and returns all parts, laid end to end along the dimension named above; an argument that names none is the same for every part.
All inputs are finite; a program needn't handle non-finite values.
Results may differ from a plain program's by a relative error of at most 0.022.
Values are sent between devices in bfloat16 or wider.
A program may use at most 2 GiB of HBM per device.

v0:
```python
import jax
import jax.numpy as jnp
from jax import lax

NAMES = ("w_gate", "w_up", "w_down")


def matmul(a, w):
    return jnp.dot(a, w, preferred_element_type=jnp.float32).astype(jnp.bfloat16)


def normed(h):
    wide = h.astype(jnp.float32)
    scale = lax.rsqrt(jnp.mean(wide**2, -1, keepdims=True) + 1e-6)
    return (wide * scale).astype(jnp.bfloat16)


def layer(h, w):
    a = normed(h)
    gate = jnp.dot(a, w["w_gate"], preferred_element_type=jnp.float32)
    up = jnp.dot(a, w["w_up"], preferred_element_type=jnp.float32)
    return h + matmul((jax.nn.silu(gate) * up).astype(jnp.bfloat16), w["w_down"])


def adamw(w, m, v, g):
    m = 0.9 * m + 0.1 * g
    v = 0.95 * v + 0.05 * g * g
    step = m * lax.rsqrt(v + 1e-8) + 0.1 * w
    return (w - 0.02 * step).astype(jnp.bfloat16), m, v


def stack(weights, h):
    for number in range(weights["w_gate"].shape[0]):
        h = layer(h, {name: w[number] for name, w in weights.items()})
    return h


def solution(mesh):
    groups = mesh.shape["rep"]

    def step(x, dy, *arrays):
        weights, m, v = (arrays[i : i + 3] for i in (0, 3, 6))
        x, dy = (t.reshape(groups, -1, *t.shape[1:]) for t in (x, dy))

        def of_a_group(x, dy):
            _, back = jax.vjp(lambda w: stack(w, x), dict(zip(NAMES, weights, strict=True)))
            by_weights = back(dy)[0]
            gradients = [by_weights[name].astype(jnp.float32) for name in NAMES]
            new = [adamw(w.astype(jnp.float32), m, v, g) for w, m, v, g in zip(weights, m, v, gradients, strict=True)]
            return tuple(one[which] for which in range(3) for one in new)

        return tuple(t.reshape(-1, *t.shape[2:]) for t in jax.vmap(of_a_group)(x, dy))

    return step
```

profile of v0, /device:TPU:0, one launch (start us, length us, event | category | flops | bytes accessed | tf_op | source)
XLA Modules:
  0.0 1623.6 jit_solution(14990791911749619705)
XLA Ops:
  17.3 32.0 %fusion.77 = f32[2048,4608]{1,0:T(8,128)} fusion(bf16[2,1152,4608]{2,1,0:T(8,128)(2,1)} %param, bf16[1,2048,1152]{2,1,0:T(8,128)(2,1)} %param.2, f32[2048]{0:T(1024)S(1)} %add_rsqrt_fusion), kind=kOutput, calls=%fused_computation.103 | convolution fusion | flops 21750349824 | bytes 53092352 | tf_op jit(solution)/vmap(jvp())/dot_general | solution.py:20
  49.3 30.2 %fusion.75 = f32[2048,4608]{1,0:T(8,128)} fusion(bf16[2,1152,4608]{2,1,0:T(8,128)(2,1)} %param.3, bf16[1,2048,1152]{2,1,0:T(8,128)(2,1)S(1)} %bitcast.354, f32[2048]{0:T(1024)S(1)} %add_rsqrt_fusion), kind=kOutput, calls=%fused_computation.101 | convolution fusion | flops 21750349824 | bytes 53092352 | tf_op jit(solution)/vmap(jvp())/dot_general | solution.py:21
  79.5 31.8 %fusion.35 = bf16[2048,4608]{1,0:T(8,128)(2,1)} fusion(f32[2048,4608]{1,0:T(8,128)} %fusion.75, f32[2048,4608]{1,0:T(8,128)} %fusion.77), kind=kLoop, calls=%fused_computation.43 | loop fusion | flops 56623104 | bytes 94371840
  111.3 30.7 %fusion.86 = (f32[2048]{0:T(1024)S(1)}, bf16[1,1,2048,1152]{2,3,1,0:T(8,128)(2,1)}) fusion(bf16[2048,4608]{1,0:T(8,128)(2,1)} %fusion.35, bf16[2,4608,1152]{2,1,0:T(8,128)(2,1)} %param.4, bf16[1,2048,1152]{1,2,0:T(8,128)(2,1)} %copy), kind=kOutput, calls=%fused_computation.112 | convolution fusion | flops 21755066368 | bytes 38936576 | tf_op jit(solution)/vmap(jvp())/dot_general | solution.py:9
  142.6 32.4 %fusion.64 = f32[2048,4608]{1,0:T(8,128)} fusion(bf16[2,1152,4608]{2,1,0:T(8,128)(2,1)} %param, bf16[1,1,2048,1152]{2,3,1,0:T(8,128)(2,1)} %get-tuple-element.10, f32[2048]{0:T(1024)S(1)} %bitcast.358), kind=kOutput, calls=%fused_computation.90 | convolution fusion | flops 21750349824 | bytes 53092352 | tf_op jit(solution)/vmap(jvp())/dot_general | solution.py:20
  175.0 31.3 %fusion.68 = f32[2048,4608]{1,0:T(8,128)} fusion(bf16[2,1152,4608]{2,1,0:T(8,128)(2,1)} %param.3, bf16[1,1,2048,1152]{2,3,1,0:T(8,128)(2,1)S(1)} %copy-done.1, f32[2048]{0:T(1024)S(1)} %bitcast.359), kind=kOutput, calls=%fused_computation.94 | convolution fusion | flops 21750349824 | bytes 53092352 | tf_op jit(solution)/vmap(jvp())/dot_general | solution.py:21
  206.3 40.0 %convolution_bitcast_fusion.1 = f32[1,4608,1152]{2,1,0:T(8,128)} fusion(f32[2048,4608]{1,0:T(8,128)} %fusion.68, f32[2048,4608]{1,0:T(8,128)} %fusion.64, bf16[1,2048,1152]{2,1,0:T(8,128)(2,1)} %param.5), kind=kOutput, calls=%fused_computation.37 | convolution fusion | flops 21799895040 | bytes 101449728 | tf_op jit(solution)/vmap(transpose(jvp()))/dot_general | solution.py:9
  253.3 33.6 %convolution_convert_fusion.1 = bf16[2048,4608]{1,0:T(8,128)(2,1)} fusion(bf16[2,4608,1152]{2,1,0:T(8,128)(2,1)} %param.4, bf16[1,2048,1152]{2,1,0:T(8,128)(2,1)} %param.5), kind=kOutput, calls=%fused_computation.42 | convolution fusion | flops 21752709120 | bytes 34209792 | tf_op jit(solution)/vmap(transpose(jvp()))/dot_general | solution.py:9
  286.9 39.1 %fusion.6 = bf16[2048,4608]{1,0:T(8,128)(2,1)} fusion(f32[2048,4608]{1,0:T(8,128)} %fusion.64, f32[2048,4608]{1,0:T(8,128)} %fusion.68, bf16[2048,4608]{1,0:T(8,128)(2,1)} %convolution_convert_fusion.1), kind=kLoop, calls=%fused_computation.11 | loop fusion | flops 113246208 | bytes 113246208
  326.0 29.5 %fusion.98 = bf16[2048,1152]{0,1:T(8,128)(2,1)} fusion(bf16[2048,4608]{1,0:T(8,128)(2,1)} %fusion.6, bf16[2,1152,4608]{2,1,0:T(8,128)(2,1)} %param), kind=kOutput, calls=%fused_computation.123 | convolution fusion | flops 21743271936 | bytes 34209792 | tf_op jit(solution)/vmap(transpose(jvp()))/dot_general | solution.py:20
  355.5 38.3 %fusion.88 = (f32[2048]{0:T(1024)S(1)}, bf16[1,1,2048,1152]{2,3,1,0:T(8,128)(2,1)}) fusion(bf16[1,1,2048,1152]{2,3,1,0:T(8,128)(2,1)} %get-tuple-element.10, bf16[2048,1152]{0,1:T(8,128)(2,1)} %fusion.98, bf16[2,1152,4608]{2,1,0:T(8,128)(2,1)} %param.3, bf16[2048,4608]{1,0:T(8,128)(2,1)} %convolution_convert_fusion.1, f32[2048,4608]{1,0:T(8,128)} %fusion.64), kind=kOutput, calls=%fused_computation.114 | convolution fusion | flops 21814048768 | bytes 81403904 | tf_op jit(solution)/vmap(transpose(jvp()))/dot_general | solution.py:21
  404.8 30.2 %convolution_bitcast_fusion = f32[1,4608,1152]{2,1,0:T(8,128)} fusion(bf16[2048,4608]{1,0:T(8,128)(2,1)} %fusion.35, bf16[2048,1152]{0,1:T(8,128)(2,1)S(1)} %fusion.131), kind=kOutput, calls=%fused_computation.36 | convolution fusion | flops 21743271936 | bytes 44826624 | tf_op jit(solution)/vmap(transpose(jvp()))/dot_general | solution.py:9
  435.1 28.7 %convolution_bitcast_fusion.2 = f32[1,1152,4608]{2,1,0:T(8,128)} fusion(bf16[2048,4608]{1,0:T(8,128)(2,1)} %fusion.6, bf16[1,1,2048,1152]{2,3,1,0:T(8,128)(2,1)} %get-tuple-element.10, f32[2048]{0:T(1024)S(1)} %bitcast.361), kind=kOutput, calls=%fused_computation.38 | convolution fusion | flops 21750349824 | bytes 44834816 | tf_op jit(solution)/vmap(transpose(jvp()))/dot_general | solution.py:20
  463.9 31.6 %convolution_convert_fusion = bf16[2048,4608]{1,0:T(8,128)(2,1)} fusion(bf16[2048,1152]{0,1:T(8,128)(2,1)} %copy-done.2, bf16[2,4608,1152]{2,1,0:T(8,128)(2,1)} %param.4), kind=kOutput, calls=%fused_computation.41 | convolution fusion | flops 21752709120 | bytes 34209792 | tf_op jit(solution)/vmap(transpose(jvp()))/dot_general | solution.py:9
  495.6 45.9 %fusion.26 = f32[1,1152,4608]{2,1,0:T(8,128)} fusion(f32[2048,4608]{1,0:T(8,128)} %fusion.77, f32[2048,4608]{1,0:T(8,128)} %fusion.75, bf16[2048,4608]{1,0:T(8,128)(2,1)} %convolution_convert_fusion, bf16[1,2048,1152]{1,2,0:T(8,128)(2,1)} %copy, f32[2048]{0:T(1024)S(1)} %copy-done.9), kind=kOutput, calls=%fused_computation.35 | convolution fusion | flops 21854158848 | bytes 120332288 | tf_op jit(solution)/vmap(transpose(jvp()))/dot_general | solution.py:20
  542.2 36.0 %fusion.29 = f32[1,1152,4608]{2,1,0:T(8,128)} fusion(bf16[2048,4608]{1,0:T(8,128)(2,1)} %convolution_convert_fusion.1, f32[2048,4608]{1,0:T(8,128)} %fusion.64, bf16[1,1,2048,1152]{2,3,1,0:T(8,128)(2,1)} %get-tuple-element.10, f32[2048]{0:T(1024)S(1)} %bitcast.362), kind=kOutput, calls=%fused_computation.39 | convolution fusion | flops 21806972928 | bytes 82583552 | tf_op jit(solution)/vmap(transpose(jvp()))/dot_general | solution.py:21
  578.2 43.1 %fusion.32 = f32[1,1152,4608]{2,1,0:T(8,128)} fusion(bf16[2048,4608]{1,0:T(8,128)(2,1)} %convolution_convert_fusion, f32[2048,4608]{1,0:T(8,128)} %fusion.77, bf16[1,2048,1152]{1,2,0:T(8,128)(2,1)} %copy, f32[2048]{0:T(1024)S(1)} %copy-done.9), kind=kOutput, calls=%fused_computation.40 | convolution fusion | flops 21806972928 | bytes 82583552 | tf_op jit(solution)/vmap(transpose(jvp()))/dot_general | solution.py:21
  650.0 84.3 %reduce-scatter.19.cloned.1.call-done = f32[1,288,4608]{2,1,0:T(8,128)} async-done(((f32[1,1152,4608]{2,1,0:T(8,128)}), f32[1,288,4608]{2,1,0:T(8,128)}) %reduce-scatter.19.cloned.1.call-update) | async-done | bytes 5308432
  737.2 146.8 %reduce-scatter.21.cloned.1.call-done = f32[1,288,4608]{2,1,0:T(8,128)} async-done(((f32[1,1152,4608]{2,1,0:T(8,128)}), f32[1,288,4608]{2,1,0:T(8,128)}) %reduce-scatter.21.cloned.1.call-update) | async-done | bytes 5308432
  911.8 121.1 %reduce-scatter.23.cloned.1.call-done = f32[1,288,4608]{2,1,0:T(8,128)} async-done(((f32[1,1152,4608]{2,1,0:T(8,128)}), f32[1,288,4608]{2,1,0:T(8,128)}) %reduce-scatter.23.cloned.1.call-update) | async-done | bytes 5308432
  1035.7 146.8 %reduce-scatter.25.cloned.1.call-done = f32[1,288,4608]{2,1,0:T(8,128)} async-done(((f32[1,1152,4608]{2,1,0:T(8,128)}), f32[1,288,4608]{2,1,0:T(8,128)}) %reduce-scatter.25.cloned.1.call-update) | async-done | bytes 5308432
  1209.9 102.8 %all-gather.14.cloned.1.call-done = bf16[1,2,4608,1152]{3,2,1,0:T(8,128)(2,1)} async-done(((bf16[1,2,1152,1152]{3,2,1,0:T(8,128)(2,1)}), bf16[1,2,4608,1152]{3,2,1,0:T(8,128)(2,1)}) %all-gather.14.cloned.1.call-update) | async-done | bytes 21233680 | tf_op jit(solution)/reshape | solution.py:52
  1312.7 130.8 %all-gather.10.cloned.1.call-done = bf16[1,2,1152,4608]{3,2,1,0:T(8,128)(2,1)} async-done(((bf16[1,2,288,4608]{3,2,1,0:T(8,128)(2,1)}), bf16[1,2,1152,4608]{3,2,1,0:T(8,128)(2,1)}) %all-gather.10.cloned.1.call-update) | async-done | bytes 21233680 | tf_op jit(solution)/reshape | solution.py:52
  1443.5 130.8 %all-gather.12.cloned.1.call-done = bf16[1,2,1152,4608]{3,2,1,0:T(8,128)(2,1)} async-done(((bf16[1,2,288,4608]{3,2,1,0:T(8,128)(2,1)}), bf16[1,2,1152,4608]{3,2,1,0:T(8,128)(2,1)}) %all-gather.12.cloned.1.call-update) | async-done | bytes 21233680 | tf_op jit(solution)/reshape | solution.py:52
  (81 shorter events, 160.8 us)
Async XLA Ops:
  7.2 616.1 %reduce-scatter.27.cloned.1.call-start = ((), (), s32[]{:S(2)}) async-start(), calls=%async_computation.13 | async-start | bytes 26542080
  10.5 38.8 %slice-start.6 = ((s8[4718592]{0:T(1024)(128)(4,1)}), s8[524288]{0:T(1024)(128)(4,1)S(1)}, s32[]{:S(2)}) async-start(s8[4718592]{0:T(1024)(128)(4,1)} %bitcast.353), calls=%async_computation.21 | async-start | bytes 1048576
  17.2 32.1 %copy-start.8 = (f32[2048]{0:T(1024)}, f32[2048]{0:T(1024)S(1)}, u32[]{:S(2)}) copy-start(f32[2048]{0:T(1024)S(1)} %add_rsqrt_fusion) | copy-start | bytes 24580
  17.2 32.1 %slice-start.7 = ((s8[4718592]{0:T(1024)(128)(4,1)}), s8[4194304]{0:T(1024)(128)(4,1)S(1)}, s32[]{:S(2)}) async-start(s8[4718592]{0:T(1024)(128)(4,1)} %bitcast.353), calls=%async_computation.22 | async-start | bytes 8388608
  142.0 33.0 %copy-start.5 = (f32[1,1,2048]{2,1,0:T(1,128)}, f32[1,1,2048]{2,1,0:T(1,128)S(1)}, u32[]{:S(2)}) copy-start(f32[1,1,2048]{2,1,0:T(1,128)S(1)} %rsqrt.31) | copy-start | bytes 24580
  142.6 32.4 %copy-start.1 = (bf16[1,1,2048,1152]{2,3,1,0:T(8,128)(2,1)S(1)}, bf16[1,1,2048,1152]{2,3,1,0:T(8,128)(2,1)}, u32[]{:S(2)}) copy-start(bf16[1,1,2048,1152]{2,3,1,0:T(8,128)(2,1)} %get-tuple-element.10) | copy-start | bytes 14155780
  246.3 379.8 %reduce-scatter.29.cloned.1.call-start = ((), (), s32[]{:S(2)}) async-start(), calls=%async_computation.14 | async-start | bytes 26542080
  355.5 38.3 %copy-start.4 = (f32[2048]{0:T(1024)S(1)}, f32[2048]{0:T(1024)}, u32[]{:S(2)}) copy-start(f32[2048]{0:T(1024)} %copy-done.3) | copy-start | bytes 24580
  355.5 38.3 %copy-start.6 = (f32[1,1,2048]{2,1,0:T(1,128)S(1)}, f32[1,1,2048]{2,1,0:T(1,128)}, u32[]{:S(2)}) copy-start(f32[1,1,2048]{2,1,0:T(1,128)} %copy-done.5) | copy-start | bytes 24580
  435.1 299.3 %reduce-scatter.19.cloned.1.call-start = ((), (), s32[]{:S(2)}) async-start(), calls=%async_computation.9 | async-start | bytes 26542080
  463.9 31.7 %copy-start.9 = (f32[2048]{0:T(1024)S(1)}, f32[2048]{0:T(1024)}, u32[]{:S(2)}) copy-start(f32[2048]{0:T(1024)} %copy-done.8) | copy-start | bytes 24580
  463.9 420.1 %reduce-scatter.21.cloned.1.call-start = ((), (), s32[]{:S(2)}) async-start(), calls=%async_computation.10 | async-start | bytes 26542080
  541.5 491.4 %reduce-scatter.23.cloned.1.call-start = ((), (), s32[]{:S(2)}) async-start(), calls=%async_computation.11 | async-start | bytes 26542080
  578.2 604.4 %reduce-scatter.25.cloned.1.call-start = ((), (), s32[]{:S(2)}) async-start(), calls=%async_computation.12 | async-start | bytes 26542080
  621.4 691.4 %all-gather.14.cloned.1.call-start = ((), (), s32[]{:S(2)}) async-start(), calls=%async_computation.8 | async-start | bytes 26542080 | tf_op jit(solution)/reshape | solution.py:52
  650.0 793.5 %all-gather.10.cloned.1.call-start = ((), (), s32[]{:S(2)}) async-start(), calls=%async_computation.6 | async-start | bytes 26542080 | tf_op jit(solution)/reshape | solution.py:52
  911.6 662.7 %all-gather.12.cloned.1.call-start = ((), (), s32[]{:S(2)}) async-start(), calls=%async_computation.7 | async-start | bytes 26542080 | tf_op jit(solution)/reshape | solution.py:52
  1574.3 21.0 %copy-start = (bf16[1,2,1152,4608]{3,2,1,0:T(8,128)(2,1)S(1)}, bf16[1,2,1152,4608]{3,2,1,0:T(8,128)(2,1)}, u32[]{:S(2)}) copy-start(bf16[1,2,1152,4608]{3,2,1,0:T(8,128)(2,1)} %all-gather.12.cloned.1.call-done) | copy-start | bytes 63700996
  1574.3 31.8 %slice-start = ((s8[21233664]{0:T(1024)(128)(4,1)}), s8[4194304]{0:T(1024)(128)(4,1)S(1)}, s32[]{:S(2)}) async-start(s8[21233664]{0:T(1024)(128)(4,1)} %bitcast.348), calls=%async_computation.15 | async-start | bytes 8388608
  1574.3 31.8 %slice-start.1 = ((s8[21233664]{0:T(1024)(128)(4,1)}), s8[4194304]{0:T(1024)(128)(4,1)S(1)}, s32[]{:S(2)}) async-start(s8[21233664]{0:T(1024)(128)(4,1)} %bitcast.348), calls=%async_computation.16 | async-start | bytes 8388608
  1574.3 31.8 %slice-start.2 = ((s8[21233664]{0:T(1024)(128)(4,1)}), s8[4194304]{0:T(1024)(128)(4,1)S(1)}, s32[]{:S(2)}) async-start(s8[21233664]{0:T(1024)(128)(4,1)} %bitcast.348), calls=%async_computation.17 | async-start | bytes 8388608
  1595.3 12.8 slice-start.3
  1595.3 14.0 slice-start.4
  1595.3 14.0 slice-start.5
  (4 other events, 4.1 us)
Sparse Core Ops, SparseCore 0:
  246.4 149.3 reduce-scatter.26
  435.2 149.4 reduce-scatter.28
  587.8 146.5 reduce-scatter.18
  737.4 146.5 reduce-scatter.20
  886.4 146.5 reduce-scatter.22
  1036.0 146.5 reduce-scatter.24
  1184.1 128.6 all-gather.13
  1314.8 128.6 all-gather.9
  1445.6 128.6 all-gather.11
where the time goes:
time: 1630 us; the launch traced here: 1620 us
  waiting for transfers between devices  864 us (53%)
  matrix products  514 us (32%)
  other arithmetic  170 us (10%)
  local copies, waits for them, and re-layouts  60.8 us (4%)
    unnamed x15, waiting for transfers between devices  499 us
    reshape x3, waiting for transfers between devices, step(): t.reshape(-1, *t.shape[2:])  364 us
    dot_general x5, matrix products, layer(): up = jnp.dot(a, w['w_up'], preferred_element_type=jnp.float32)  179 us
    dot_general x5, matrix products, layer(): gate = jnp.dot(a, w['w_gate'], preferred_element_type=jnp.float32)  169 us
    dot_general x5, matrix products, matmul(): jnp.dot(a, w, preferred_element_type=jnp.float32).astype(jnp.bfloat16)  166 us
    unnamed x5, other arithmetic  79.6 us
    reshape x3, other arithmetic, step(): t.reshape(-1, *t.shape[2:])  70.3 us
    unnamed x43, local copies, waits for them, and re-layouts  60.2 us
  transfers between devices with their start and end apart: 9, of which 7 were waited for; matrix products, arithmetic and copies ran while one was open for 28% of the time, Pallas kernels for 0%

commit v1 on v0

v1 whole, which is shorter than its diff:
```python
import jax
import jax.numpy as jnp
from jax import lax
from jax.experimental import pallas as pl
from jax.experimental.pallas import tpu as pltpu
from jax.sharding import PartitionSpec as P


f32, bf16 = jnp.float32, jnp.bfloat16
T, D, F = 2048, 1152, 4608
TT = 2 * T
HALF = F // 2
BM, BN = 1024, 768
NF, NH = F // BN, HALF // BN
RS, CS = 512, 256
QD, QF = D // 4, F // 4
ANY = pl.BlockSpec(memory_space=pl.ANY)
TOKEN = jax.ShapeDtypeStruct((8, 128), jnp.int32)
NT = (((1,), (1,)), ((), ()))
TN = (((0,), (0,)), ((), ()))

OVER_X = [(0, 2), (1, 3), (2, 0), (3, 1)]
OVER_CORE = [(0, 1), (1, 0), (2, 3), (3, 2)]


def over(array, pairs):
    return lax.ppermute(array, "dp", pairs)


def sigmoid(g):
    return 0.5 * jnp.tanh(0.5 * g) + 0.5


def dot(a, b):
    return jnp.dot(a, b, preferred_element_type=f32)


def call(body, place, after, ins, outs, grid, scratch=(), flops=0, moved=0):
    arrays = [a for a, _ in ins]
    specs = [s for _, s in ins]
    aliases = {}
    held = [(k, buffer) for k, (_, _, buffer) in enumerate(outs) if buffer is not None]
    for n, (k, buffer) in enumerate(held):
        aliases[1 + len(arrays) + n] = k
    arrays += [buffer for _, buffer in held]
    specs += [ANY] * len(held)
    if after is not None:
        arrays.append(after)
        specs.append(ANY)
    skip = len(arrays) - len(ins)

    def kernel(place_ref, *refs):
        refs, rest = refs[: len(ins)], refs[len(ins) + skip :]
        token = rest[len(outs)]
        token[...] = jnp.zeros_like(token)
        body(place_ref, *refs, *rest[: len(outs)], *rest[len(outs) + 1 :])

    result = pl.pallas_call(
        kernel,
        grid_spec=pltpu.PrefetchScalarGridSpec(
            num_scalar_prefetch=1,
            grid=grid,
            in_specs=specs,
            out_specs=[s for _, s, _ in outs] + [pl.BlockSpec((8, 128), lambda *_: (0, 0))],
            scratch_shapes=scratch,
        ),
        out_shape=[o for o, _, _ in outs] + [TOKEN],
        input_output_aliases=aliases,
        cost_estimate=pl.CostEstimate(flops=flops, bytes_accessed=moved, transcendentals=0),
        compiler_params=pltpu.CompilerParams(vmem_limit_bytes=63 << 20),
    )(place, *arrays)
    return result[:-1], result[-1]


def shaped(*shape, dtype=bf16):
    return jax.ShapeDtypeStruct(shape, dtype)


def normalise(h, a_s, aT):
    def rows_of(i, _):
        rows = pl.ds(pl.multiple_of(i * 256, 256), 256)
        wide = h[rows, :].astype(f32)
        scale = lax.rsqrt(jnp.mean(wide * wide, -1, keepdims=True) + 1e-6)
        a = (wide * scale).astype(bf16)
        a_s[rows, :] = a
        if aT is not None:
            aT[:, rows] = a.T
        return 0

    lax.fori_loop(0, h.shape[0] // 256, rows_of, 0)


def forward0(place, after, first, x, w_gate, w_up, w_down, held):
    rows = x.shape[0]

    def tile(j, place):
        return jnp.where(j < NH, place[0] * NH + j, (1 - place[0]) * NH + j - NH)

    def body(place, x, wg, wu, wd, g_o, u_o, hid_o, aT_o, h_o, a_s, acc, hs):
        j = pl.program_id(1)

        @pl.when(j == 0)
        def _():
            normalise(x, a_s, aT_o)

        for r in range(0, BM, RS):
            r = slice(r, r + RS)
            a = a_s[r, :]
            for c in range(0, BN, CS):
                c = slice(c, c + CS)
                g, u = dot(a, wg[:, c]), dot(a, wu[:, c])
                g_o[r, c] = g
                u_o[r, c] = u
                hs[r, c] = (g * sigmoid(g) * u).astype(bf16)
            acc[r, :] = jnp.where(j == 0, 0.0, acc[r, :]) + dot(hs[r, :], wd[...])

        @pl.when(j < NH)
        def _():
            hid_o[...] = hs[...]

        @pl.when(j == NF - 1)
        def _():
            def rows_of(i, _):
                rows = pl.ds(pl.multiple_of(i * 256, 256), 256)
                h_o[rows, :] = x[rows, :] + acc[rows, :].astype(bf16)
                return 0

            lax.fori_loop(0, BM // 256, rows_of, 0)

    wide = pl.BlockSpec((BM, BN), lambda i, j, p: (first + i, tile(j, p)))
    into = pl.BlockSpec((None, D, BN), lambda i, j, p: (0, 0, tile(j, p)))
    return call(
        body,
        place,
        after,
        [
            (x, pl.BlockSpec((BM, D), lambda i, j, p: (i, 0))),
            (w_gate, into),
            (w_up, into),
            (w_down, pl.BlockSpec((None, BN, D), lambda i, j, p: (0, tile(j, p), 0))),
        ],
        [
            (shaped(TT, F, dtype=f32), wide, held[0]),
            (shaped(TT, F, dtype=f32), wide, held[1]),
            (shaped(TT, HALF), pl.BlockSpec((BM, BN), lambda i, j, p: (first + i, jnp.minimum(j, NH - 1))), held[2]),
            (shaped(D, TT), pl.BlockSpec((D, BM), lambda i, j, p: (0, first + i)), held[3]),
            (shaped(TT, D), pl.BlockSpec((BM, D), lambda i, j, p: (first + i, 0)), held[4]),
        ],
        (rows // BM, NF),
        [pltpu.VMEM((BM, D), bf16), pltpu.VMEM((BM, D), f32), pltpu.VMEM((BM, BN), bf16)],
        flops=6 * rows * D * F,
        moved=rows * F * 9,
    )


def both1(place, after, first, own, h, dy, w_gate, w_up, w_down, held):
    rows = dy.shape[0]

    def tile(j, place):
        return (place[0] if own else 1 - place[0]) * NH + j

    def body(place, h, dy, wg, wu, wd, *refs):
        if own:
            dgu_o, hid_o, aT_o, a_s = refs
        else:
            (dgu_o, a_s), hid_o, aT_o = refs, None, None
        j = pl.program_id(1)

        @pl.when(j == 0)
        def _():
            normalise(h, a_s, aT_o)

        for r in range(0, BM, RS):
            r = slice(r, r + RS)
            a = a_s[r, :]
            for c in range(0, BN, CS):
                c = slice(c, c + CS)
                g, u = dot(a, wg[:, c]), dot(a, wu[:, c])
                back = lax.dot_general(dy[r, :], wd[c, :], NT, preferred_element_type=f32).astype(bf16).astype(f32)
                s = sigmoid(g)
                silu = g * s
                if own:
                    hid_o[r, c] = (silu * u).astype(bf16)
                dgu_o[0, r, c] = (back * u * (s + silu * (1 - s))).astype(bf16)
                dgu_o[1, r, c] = (back * silu).astype(bf16)

    into = pl.BlockSpec((None, D, BN), lambda i, j, p: (1, 0, tile(j, p)))
    outs = [(shaped(2, TT, F), pl.BlockSpec((2, BM, BN), lambda i, j, p: (0, first + i, tile(j, p))), held[0])]
    if own:
        outs += [
            (shaped(TT, HALF), pl.BlockSpec((BM, BN), lambda i, j, p: (first + i, j)), held[1]),
            (shaped(D, TT), pl.BlockSpec((D, BM), lambda i, j, p: (0, first + i)), held[2]),
        ]
    return call(
        body,
        place,
        after,
        [
            (h, pl.BlockSpec((BM, D), lambda i, j, p: (first + i, 0))),
            (dy, pl.BlockSpec((BM, D), lambda i, j, p: (i, 0))),
            (w_gate, into),
            (w_up, into),
            (w_down, pl.BlockSpec((None, BN, D), lambda i, j, p: (1, tile(j, p), 0))),
        ],
        outs,
        (rows // BM, NH),
        [pltpu.VMEM((BM, D), bf16)],
        flops=3 * rows * D * F,
        moved=rows * F * 3,
    )


def back1(place, after, first, dgu, dy, h, w_gate, w_up, held):
    rows = dy.shape[0]

    def body(place, dgu, wg, wu, h, dy, o, acc):
        j = pl.program_id(1)
        for r in range(0, BM, RS):
            r = slice(r, r + RS)
            for which, w in enumerate((wg, wu)):
                new = lax.dot_general(dgu[which, r, :], w[...], NT, preferred_element_type=f32)
                acc[which, r, :] = jnp.where(j == 0, 0.0, acc[which, r, :]) + new

        @pl.when(j == NF - 1)
        def _():
            def rows_of(i, _):
                rows = pl.ds(pl.multiple_of(i * 256, 256), 256)
                da = (acc[0, rows, :].astype(bf16) + acc[1, rows, :].astype(bf16)).astype(f32)
                wide = h[rows, :].astype(f32)
                scale = lax.rsqrt(jnp.mean(wide * wide, -1, keepdims=True) + 1e-6)
                along = jnp.mean(da * wide, -1, keepdims=True)
                dwide = (da * scale - wide * (along * scale * scale * scale)).astype(bf16)
                o[rows, :] = dy[rows, :] + dwide
                return 0

            lax.fori_loop(0, BM // 256, rows_of, 0)

    into = pl.BlockSpec((None, D, BN), lambda i, j, p: (1, 0, j))
    return call(
        body,
        place,
        after,
        [
            (dgu, pl.BlockSpec((2, BM, BN), lambda i, j, p: (0, first + i, j))),
            (w_gate, into),
            (w_up, into),
            (h, pl.BlockSpec((BM, D), lambda i, j, p: (first + i, 0))),
            (dy, pl.BlockSpec((BM, D), lambda i, j, p: (i, 0))),
        ],
        [(shaped(TT, D), pl.BlockSpec((BM, D), lambda i, j, p: (first + i, 0)), held)],
        (rows // BM, NF),
        [pltpu.VMEM((2, BM, D), f32)],
        flops=4 * rows * D * F,
        moved=rows * F * 4,
    )


def back0(place, after, own, dh, gate, up, w_down, held):
    def tile(j, place):
        return (place[0] if own else 1 - place[0]) * NH + j

    def body(place, dh, g_r, u_r, wd, dgu_o):
        for r in range(0, BM, RS):
            r = slice(r, r + RS)
            for c in range(0, BN, CS):
                c = slice(c, c + CS)
                back = lax.dot_general(dh[r, :], wd[c, :], NT, preferred_element_type=f32).astype(bf16).astype(f32)
                g, u = g_r[r, c], u_r[r, c]
                s = sigmoid(g)
                silu = g * s
                dgu_o[0, r, c] = (back * u * (s + silu * (1 - s))).astype(bf16)
                dgu_o[1, r, c] = (back * silu).astype(bf16)

    wide = pl.BlockSpec((BM, BN), lambda i, j, p: (i, tile(j, p)))
    return call(
        body,
        place,
        after,
        [
            (dh, pl.BlockSpec((BM, D), lambda i, j, p: (i, 0))),
            (gate, wide),
            (up, wide),
            (w_down, pl.BlockSpec((None, BN, D), lambda i, j, p: (0, tile(j, p), 0))),
        ],
        [(shaped(2, TT, F), pl.BlockSpec((2, BM, BN), lambda i, j, p: (0, i, tile(j, p))), held)],
        (TT // BM, NH),
        flops=TT * D * F,
        moved=TT * F * 6,
    )


def grad_down(place, after, hidden, back):
    rows = 384
    n = QF // rows
    parts = [b.shape[0] for b in back]

    def tile(i, place):
        return jnp.where(i < n, place[1] * n + i, (1 - place[1]) * n + i - n)

    def body(place, hidden, *refs):
        back, (own, out) = refs[:-2], refs[-2:]
        i = pl.program_id(0)
        total = None
        at = 0
        for b, size in zip(back, parts, strict=True):
            term = lax.dot_general(hidden[at : at + size, :], b[...], TN, preferred_element_type=f32)
            total = term if total is None else total + term
            at += size

        @pl.when(i < n)
        def _():
            own[...] = total

        @pl.when(i >= n)
        def _():
            out[...] = total.astype(bf16)

    return call(
        body,
        place,
        after,
        [(hidden, pl.BlockSpec((TT, rows), lambda i, p: (0, tile(i, p))))]
        + [(b, pl.BlockSpec((b.shape[0], D), lambda i, p: (0, 0), pipeline_mode=pl.Buffered(1))) for b in back],
        [
            (shaped(QF, D, dtype=f32), pl.BlockSpec((rows, D), lambda i, p: (jnp.minimum(i, n - 1), 0)), None),
            (shaped(QF, D), pl.BlockSpec((rows, D), lambda i, p: (jnp.maximum(i - n, 0), 0)), None),
        ],
        (2 * n,),
        flops=2 * TT * D * HALF,
        moved=TT * HALF * 2,
    )


def grad_into(place, after, own_half, aT, dgu):
    def tile(j, place):
        return (place[0] if own_half else 1 - place[0]) * NH + j

    def body(place, aT, dgu, own, out, total):
        total[...] = dot(aT[...], dgu[...])
        own[...] = total[pl.ds(pl.multiple_of(place[1] * QD, QD), QD), :]
        out[...] = total[pl.ds(pl.multiple_of((1 - place[1]) * QD, QD), QD), :].astype(bf16)

    block = pl.BlockSpec((None, QD, BN), lambda k, j, p: (k, 0, j))
    return call(
        body,
        place,
        after,
        [
            (aT, pl.BlockSpec((2 * QD, TT), lambda k, j, p: (p[0], 0), pipeline_mode=pl.Buffered(1))),
            (dgu, pl.BlockSpec((None, TT, BN), lambda k, j, p: (k, 0, tile(j, p)))),
        ],
        [(shaped(2, QD, HALF, dtype=f32), block, None), (shaped(2, QD, HALF), block, None)],
        (2, NH),
        [pltpu.VMEM((2 * QD, BN), f32)],
        flops=2 * TT * D * HALF,
        moved=TT * HALF * 4,
    )


def adamw(g, w, m, v):
    g = g.astype(bf16).astype(f32)
    m = 0.9 * m + 0.1 * g
    v = 0.95 * v + 0.05 * g * g
    return (w - 0.02 * (m * lax.rsqrt(v + 1e-8) + 0.1 * w)).astype(bf16), m, v


def step_down(place, after, layer, own, came, w, m, v, held):
    rows = 192

    def body(place, own, came, w, m, v, nw_o, m_o, v_o):
        nw_o[...], m_o[...], v_o[...] = adamw(own[...] + came[...].astype(f32), w[...].astype(f32), m[...], v[...])

    n = QF // rows
    block = pl.BlockSpec((rows, D), lambda i, p: (i, 0))
    kept = pl.BlockSpec((None, rows, D), lambda i, p: (layer, i, 0))
    return call(
        body,
        place,
        after,
        [
            (own, block),
            (came, block),
            (w, pl.BlockSpec((None, rows, D), lambda i, p: (layer, (2 * p[0] + p[1]) * n + i, 0))),
            (m, kept),
            (v, kept),
        ],
        [(shaped(QF, D), block, None), (shaped(2, QF, D, dtype=f32), kept, held[0]), (shaped(2, QF, D, dtype=f32), kept, held[1])],
        (n,),
        flops=QF * D * 10,
        moved=QF * D * 26,
    )


def step_into(place, after, layer, own_half, k, own, came, w, m, v, held):
    def body(place, own, came, w, m, v, nw_o, m_o, v_o):
        nw_o[...], m_o[...], v_o[...] = adamw(own[...] + came[...].astype(f32), w[...].astype(f32), m[...], v[...])

    def tile(j, place):
        return (place[0] if own_half else 1 - place[0]) * NH + j

    block = pl.BlockSpec((None, QD, BN), lambda j, p: (k, 0, j))
    kept = pl.BlockSpec((None, QD, BN), lambda j, p: (layer, 0, tile(j, p)))
    return call(
        body,
        place,
        after,
        [
            (own, block),
            (came, block),
            (w, pl.BlockSpec((None, QD, BN), lambda j, p: (layer, 2 * p[0] + p[1], tile(j, p)))),
            (m, kept),
            (v, kept),
        ],
        [
            (shaped(QD, HALF), pl.BlockSpec((QD, BN), lambda j, p: (0, j)), None),
            (shaped(2, QD, F, dtype=f32), kept, held[0]),
            (shaped(2, QD, F, dtype=f32), kept, held[1]),
        ],
        (NH,),
        flops=QD * HALF * 10,
        moved=QD * HALF * 26,
    )


def gathered(place, after, block, blocks, spec_in, spec_out, out, held):
    n = spec_in[0]

    def body(place, *refs):
        sources, o = refs[:4], refs[4]
        r = pl.program_id(0)
        for k, source in enumerate(sources):

            @pl.when(r == k)
            def _(source=source):
                o[...] = source[...]

    def source_spec(k):
        return pl.BlockSpec(block, lambda r, j, p: spec_in[1](jnp.where(r == k, j, jnp.where(r < k, 0, n - 1))))

    return call(
        body,
        place,
        after,
        [(b, source_spec(k)) for k, b in enumerate(blocks)],
        [(out, pl.BlockSpec((None,) + block, lambda r, j, p: spec_out(jnp.bitwise_xor(2 * p[0] + p[1], r), j, p)), held)],
        (4, n),
        moved=4 * blocks[0].size * 4,
        flops=blocks[0].size,
    )


def gather_down(place, after, layer, blocks, held):
    rows = 384
    n = QF // rows
    return gathered(
        place, after, (rows, D), blocks, (n, lambda j: (j, 0)), lambda d, j, p: (layer, d * n + j, 0), shaped(2, F, D), held
    )


def gather_into(place, after, layer, blocks, flip, held):
    def spec_out(d, j, p):
        half = jnp.bitwise_xor(d // 2, flip)
        return (layer, d, half * NH + j)

    return gathered(place, after, (QD, BN), blocks, (NH, lambda j: (0, j)), spec_out, shaped(2, D, F), held)


def spread(new):
    far = over(new, OVER_X)
    near = over(new, OVER_CORE)
    return [new, near, far, over(far, OVER_CORE)]


def whole_step(x, dy, w_gate, w_up, w_down, m_gate, m_up, m_down, v_gate, v_up, v_down):
    d = lax.axis_index("dp")
    place = jnp.stack([d // 2, d % 2]).astype(jnp.int32)
    x, dy = x[0], dy[0]
    x_far = over(x, OVER_X)
    dy_far = over(dy, OVER_X)
    per = T // BM

    ws0 = (w_gate, w_up, w_down)
    one, t = forward0(place, None, 0, x, *ws0, [None] * 5)
    (gate, up, hid0, aT0, h), t = forward0(place, t, per, x_far, *ws0, one)

    one, t = both1(place, t, 0, True, h, dy, *ws0, [None] * 3)
    (dgu, hid1, aT1), t = both1(place, t, per, True, h, dy_far, *ws0, one)

    down1, t = grad_down(place, t, hid1, (dy, dy_far))
    down1_came = over(down1[1], OVER_CORE)
    into1a, t = grad_into(place, t, True, aT1, dgu)
    into1a_came = over(into1a[1], OVER_CORE)

    (n_down1, *mv_down), t = step_down(place, t, 1, down1[0], down1_came, w_down, m_down, v_down, (None, None))
    s_down1 = spread(n_down1)

    (dgu,), t = both1(place, t, 0, False, h, dy, *ws0, [dgu])

    def steps_into(t, layer, own_half, grads, came, mv_gate, mv_up):
        (new_gate, *mv_gate), t = step_into(place, t, layer, own_half, 0, grads[0], came, w_gate, m_gate, v_gate, mv_gate)
        (new_up, *mv_up), t = step_into(place, t, layer, own_half, 1, grads[0], came, w_up, m_up, v_up, mv_up)
        return t, spread(new_gate), spread(new_up), mv_gate, mv_up

    t, s_gate1a, s_up1a, mv_gate, mv_up = steps_into(t, 1, True, into1a, into1a_came, (None, None), (None, None))
    (dgu,), t = both1(place, t, per, False, h, dy_far, *ws0, [dgu])

    into1b, t = grad_into(place, t, False, aT1, dgu)
    into1b_came = over(into1b[1], OVER_CORE)
    (dh,), t = back1(place, t, 0, dgu, dy, h, w_gate, w_up, None)
    t, s_gate1b, s_up1b, mv_gate, mv_up = steps_into(t, 1, False, into1b, into1b_came, mv_gate, mv_up)
    (dh,), t = back1(place, t, per, dgu, dy_far, h, w_gate, w_up, dh)

    down0, t = grad_down(place, t, hid0, (dh,))
    down0_came = over(down0[1], OVER_CORE)
    (dgu0,), t = back0(place, t, True, dh, gate, up, w_down, None)
    (n_down0, *mv_down), t = step_down(place, t, 0, down0[0], down0_came, w_down, m_down, v_down, mv_down)
    s_down0 = spread(n_down0)

    into0a, t = grad_into(place, t, True, aT0, dgu0)
    into0a_came = over(into0a[1], OVER_CORE)
    (dgu0,), t = back0(place, t, False, dh, gate, up, w_down, dgu0)
    t, s_gate0a, s_up0a, mv_gate, mv_up = steps_into(t, 0, True, into0a, into0a_came, mv_gate, mv_up)

    into0b, t = grad_into(place, t, False, aT0, dgu0)
    into0b_came = over(into0b[1], OVER_CORE)
    (o_down,), t = gather_down(place, t, 1, s_down1, None)
    (o_gate,), t = gather_into(place, t, 1, s_gate1a, 0, None)
    t, s_gate0b, s_up0b, mv_gate, mv_up = steps_into(t, 0, False, into0b, into0b_came, mv_gate, mv_up)
    (o_up,), t = gather_into(place, t, 1, s_up1a, 0, None)
    (o_gate,), t = gather_into(place, t, 1, s_gate1b, 1, o_gate)
    (o_up,), t = gather_into(place, t, 1, s_up1b, 1, o_up)
    (o_down,), t = gather_down(place, t, 0, s_down0, o_down)
    (o_gate,), t = gather_into(place, t, 0, s_gate0a, 0, o_gate)
    (o_up,), t = gather_into(place, t, 0, s_up0a, 0, o_up)
    (o_gate,), t = gather_into(place, t, 0, s_gate0b, 1, o_gate)
    (o_up,), t = gather_into(place, t, 0, s_up0b, 1, o_up)
    return o_gate, o_up, o_down, mv_gate[0], mv_up[0], mv_down[0], mv_gate[1], mv_up[1], mv_down[1]


def solution(mesh):
    sequences, whole = P(("rep", "dp"), None, None), P(None, None, None)
    block, group, own = P(None, "dp", None), P("rep", None, None), P("rep", "dp", None)
    return jax.shard_map(
        whole_step,
        mesh=mesh,
        in_specs=(sequences,) * 2 + (whole,) * 3 + (block,) * 6,
        out_specs=(group,) * 3 + (own,) * 6,
        check_vma=False,
    )
```

time: 1630 us -> 1230 us (0.75)
  Pallas kernels: 0 us -> 996 us
  waiting for transfers between devices: 864 us -> 203 us
  matrix products: 514 us -> 0 us
  other arithmetic: 170 us -> 0.61 us
  local copies, waits for them, and re-layouts: 60.8 us -> 0 us
  starting transfers between devices: 0.55 us -> 21.1 us
    pallas_call x0 -> x36, Pallas kernels: none -> 996 us  [call(): pl.pallas_call(kernel, grid_spec=pltpu.PrefetchScalarGridSpec(num_scalar_...]
    dot_general x15 -> x0, matrix products: 514 us -> none  [the longest x5 179 us: layer(): up = jnp.dot(a, w['w_up'], preferred_element_type=jnp.float32)]
    unnamed x15 -> x0, waiting for transfers between devices: 499 us -> none
    reshape x3 -> x0, waiting for transfers between devices: 364 us -> none  [step(): t.reshape(-1, *t.shape[2:])]
    ppermute x0 -> x38, waiting for transfers between devices: none -> 203 us  [over(): return lax.ppermute(array, 'dp', pairs)]
    unnamed x5 -> x0, other arithmetic: 79.6 us -> none
    reshape x3 -> x0, other arithmetic: 70.3 us -> none  [step(): t.reshape(-1, *t.shape[2:])]
    unnamed x43 -> x0, local copies, waits for them, and re-layouts: 60.2 us -> none
  transfers between devices with their start and end apart: 9 -> 38, of which waited for: 7 -> 9; matrix products, arithmetic and copies ran while one was open for 28% -> 0% of each run, Pallas kernels for 0% -> 53%
where the time goes in v1:
time: 1230 us; the launch traced here: 1220 us
  Pallas kernels  996 us (81%)
  waiting for transfers between devices  203 us (17%)
  starting transfers between devices  21.1 us (2%)
    pallas_call x36, Pallas kernels, call(): pl.pallas_call(kernel, grid_spec=pltpu.PrefetchScalarGridSpec(num_scalar_...  996 us
    ppermute x38, waiting for transfers between devices, over(): return lax.ppermute(array, 'dp', pairs)  203 us
  transfers between devices with their start and end apart: 38, of which 9 were waited for; matrix products, arithmetic and copies ran while one was open for 0% of the time, Pallas kernels for 53%

profile of v1, /device:TPU:0, one launch (start us, length us, event | category | flops | bytes accessed | tf_op | source)
XLA Modules:
  0.0 1222.0 jit_solution(6877826489187700790)
XLA Ops:
  4.6 89.8 %shard_map.178 = (f32[4096,4608]{1,0:T(8,128)}, f32[4096,4608]{1,0:T(8,128)}, bf16[4096,2304]{1,0:T(8,128)(2,1)}, bf16[1152,4096]{1,0:T(8,128)(2,1)}, bf16[4096,1152]{1,0:T(8,128)(2,1)}, /*index=5*/s32[8,128]{1,0:T(8,128)}) custom-call(s32[2]{0:T(128)} %pad_add_fusion.place_ref, bf16[2048,1152]{1,0:T(8,128)(2,1)} %bitcast.10, ...), custom_call_target="tpu_custom_call" | custom-call | flops 65229815808 | bytes 84934656 | tf_op jit(solution)/shard_map/pallas_call | solution.py:58
  106.9 89.9 %shard_map.179 = (f32[4096,4608]{1,0:T(8,128)}, f32[4096,4608]{1,0:T(8,128)}, bf16[4096,2304]{1,0:T(8,128)(2,1)}, bf16[1152,4096]{1,0:T(8,128)(2,1)}, bf16[4096,1152]{1,0:T(8,128)(2,1)}, /*index=5*/s32[8,128]{1,0:T(8,128)}) custom-call(s32[2]{0:T(128)} %pad_add_fusion.place_ref, ...), custom_call_target="tpu_custom_call", output_to_operand_aliasing={{0}: (5, {}), {1}: (6, {}), {2}: (7, {}), {3}: (8, {}), {4}... | custom-call | flops 65229815808 | bytes 84934656 | tf_op jit(solution)/shard_map/pallas_call | solution.py:58
  196.8 49.7 %shard_map.180 = (bf16[2,4096,4608]{2,1,0:T(8,128)(2,1)}, bf16[4096,2304]{1,0:T(8,128)(2,1)}, bf16[1152,4096]{1,0:T(8,128)(2,1)}, s32[8,128]{1,0:T(8,128)}) custom-call(s32[2]{0:T(128)} %pad_add_fusion.place_ref, bf16[4096,1152]{1,0:T(8,128)(2,1)} %get-tuple-element.125.refs_0_.refs_3_, bf16[2048,1152]{1,0:T(8,128)(2,1)} %bitcast.5, ...), custom_call_target="tpu_custom_call" | custom-call | flops 32614907904 | bytes 28311552 | tf_op jit(solution)/shard_map/pallas_call | solution.py:58
  246.5 49.3 %shard_map.181 = (bf16[2,4096,4608]{2,1,0:T(8,128)(2,1)}, bf16[4096,2304]{1,0:T(8,128)(2,1)}, bf16[1152,4096]{1,0:T(8,128)(2,1)}, s32[8,128]{1,0:T(8,128)}) custom-call(s32[2]{0:T(128)} %pad_add_fusion.place_ref, bf16[4096,1152]{1,0:T(8,128)(2,1)} %get-tuple-element.125.refs_0_.refs_3_, ...), custom_call_target="tpu_custom_call", output_to_operand_aliasing={{0}: (6, {}), {1}: (7, {}), {2}: (8, {})} | custom-call | flops 32614907904 | bytes 28311552 | tf_op jit(solution)/shard_map/pallas_call | solution.py:58
  295.8 33.3 %shard_map.182 = (f32[1152,1152]{1,0:T(8,128)}, bf16[1152,1152]{1,0:T(8,128)(2,1)}, s32[8,128]{1,0:T(8,128)}) custom-call(s32[2]{0:T(128)} %pad_add_fusion.place_ref, bf16[4096,2304]{1,0:T(8,128)(2,1)} %get-tuple-element.132.refs_0_, bf16[2048,1152]{1,0:T(8,128)(2,1)} %bitcast.6, bf16[2048,1152]{1,0:T(8,128)(2,1)} %collective-permute-done.1.refs_1_.refs_2_.refs_4_, ...), custom_call_target="tpu_custom_call" | custom-call | flops 21743271936 | bytes 18874368 | tf_op jit(solution)/shard_map/pallas_call | solution.py:58
  329.1 29.6 %shard_map.183 = (f32[2,288,2304]{2,1,0:T(8,128)}, bf16[2,288,2304]{2,1,0:T(8,128)(2,1)}, s32[8,128]{1,0:T(8,128)}) custom-call(s32[2]{0:T(128)} %pad_add_fusion.place_ref, bf16[1152,4096]{1,0:T(8,128)(2,1)} %get-tuple-element.136.refs_0_, bf16[2,4096,4608]{2,1,0:T(8,128)(2,1)} %get-tuple-element.131.refs_1_.refs_5_, s32[8,128]{1,0:T(8,128)} %get-tuple-element.137.refs_2_), custom_call_target="tpu_custom_call" | custom-call | flops 21743271936 | bytes 37748736 | tf_op jit(solution)/shard_map/pallas_call | solution.py:58
  359.2 13.7 %shard_map.184 = (bf16[1152,1152]{1,0:T(8,128)(2,1)}, f32[2,1152,1152]{2,1,0:T(8,128)}, f32[2,1152,1152]{2,1,0:T(8,128)}, s32[8,128]{1,0:T(8,128)}) custom-call(s32[2]{0:T(128)} %pad_add_fusion.place_ref, f32[1152,1152]{1,0:T(8,128)} %get-tuple-element.134.refs_0_, bf16[1152,1152]{1,0:T(8,128)(2,1)} %collective-permute-done.2.refs_1_, ...), custom_call_target="tpu_custom_call" | custom-call | flops 13271040 | bytes 34504704 | tf_op jit(solution)/shard_map/pallas_call | solution.py:58
  372.9 46.6 %shard_map.185 = (bf16[2,4096,4608]{2,1,0:T(8,128)(2,1)}, s32[8,128]{1,0:T(8,128)}) custom-call(s32[2]{0:T(128)} %pad_add_fusion.place_ref, bf16[4096,1152]{1,0:T(8,128)(2,1)} %get-tuple-element.125.refs_0_.refs_3_, bf16[2048,1152]{1,0:T(8,128)(2,1)} %bitcast.7, bf16[2,1152,4608]{2,1,0:T(8,128)(2,1)} %refs_2_.34, ...), custom_call_target="tpu_custom_call", output_to_operand_aliasing={{0}: (6, {})} | custom-call | flops 32614907904 | bytes 28311552 | tf_op jit(solution)/shard_map/pallas_call | solution.py:58
  437.1 46.8 %shard_map.188 = (bf16[2,4096,4608]{2,1,0:T(8,128)(2,1)}, s32[8,128]{1,0:T(8,128)}) custom-call(s32[2]{0:T(128)} %pad_add_fusion.place_ref, bf16[4096,1152]{1,0:T(8,128)(2,1)} %get-tuple-element.125.refs_0_.refs_3_, bf16[2048,1152]{1,0:T(8,128)(2,1)} %collective-permute-done.1.refs_1_.refs_2_.refs_4_, ...), custom_call_target="tpu_custom_call", output_to_operand_aliasing={{0}: (6, {})} | custom-call | flops 32614907904 | bytes 28311552 | tf_op jit(solution)/shard_map/pallas_call | solution.py:58
  483.9 29.6 %shard_map.189 = (f32[2,288,2304]{2,1,0:T(8,128)}, bf16[2,288,2304]{2,1,0:T(8,128)(2,1)}, s32[8,128]{1,0:T(8,128)}) custom-call(s32[2]{0:T(128)} %pad_add_fusion.place_ref, bf16[1152,4096]{1,0:T(8,128)(2,1)} %get-tuple-element.136.refs_0_, bf16[2,4096,4608]{2,1,0:T(8,128)(2,1)} %get-tuple-element.146.refs_1_.refs_0_, s32[8,128]{1,0:T(8,128)} %get-tuple-element.147.refs_2_), custom_call_target="tpu_custom_call" | custom-call | flops 21743271936 | bytes 37748736 | tf_op jit(solution)/shard_map/pallas_call | solution.py:58
  513.5 63.1 %shard_map.190 = (bf16[4096,1152]{1,0:T(8,128)(2,1)}, s32[8,128]{1,0:T(8,128)}) custom-call(s32[2]{0:T(128)} %pad_add_fusion.place_ref, bf16[2,4096,4608]{2,1,0:T(8,128)(2,1)} %get-tuple-element.146.refs_1_.refs_0_, bf16[2,1152,4608]{2,1,0:T(8,128)(2,1)} %refs_2_.34, bf16[2,1152,4608]{2,1,0:T(8,128)(2,1)} %refs_2_.35, ...), custom_call_target="tpu_custom_call" | custom-call | flops 43486543872 | bytes 37748736 | tf_op jit(solution)/shard_map/pallas_call | solution.py:58
  594.0 63.0 %shard_map.193 = (bf16[4096,1152]{1,0:T(8,128)(2,1)}, s32[8,128]{1,0:T(8,128)}) custom-call(s32[2]{0:T(128)} %pad_add_fusion.place_ref, bf16[2,4096,4608]{2,1,0:T(8,128)(2,1)} %get-tuple-element.146.refs_1_.refs_0_, bf16[2,1152,4608]{2,1,0:T(8,128)(2,1)} %refs_2_.34, bf16[2,1152,4608]{2,1,0:T(8,128)(2,1)} %refs_2_.35, ...), custom_call_target="tpu_custom_call", output_to_operand_aliasing={{0}: (6, {})} | custom-call | flops 43486543872 | bytes 37748736 | tf_op jit(solution)/shard_map/pallas_call | solution.py:58
  657.0 33.4 %shard_map.194 = (f32[1152,1152]{1,0:T(8,128)}, bf16[1152,1152]{1,0:T(8,128)(2,1)}, s32[8,128]{1,0:T(8,128)}) custom-call(s32[2]{0:T(128)} %pad_add_fusion.place_ref, bf16[4096,2304]{1,0:T(8,128)(2,1)} %get-tuple-element.162.refs_0_, bf16[4096,1152]{1,0:T(8,128)(2,1)} %get-tuple-element.159.refs_1_.refs_0_, s32[8,128]{1,0:T(8,128)} %get-tuple-element.163.refs_2_), custom_call_target="tpu_custom_call" | custom-call | flops 21743271936 | bytes 18874368 | tf_op jit(solution)/shard_map/pallas_call | solution.py:58
  690.9 55.3 %shard_map.195 = (bf16[2,4096,4608]{2,1,0:T(8,128)(2,1)}, s32[8,128]{1,0:T(8,128)}) custom-call(s32[2]{0:T(128)} %pad_add_fusion.place_ref, bf16[4096,1152]{1,0:T(8,128)(2,1)} %get-tuple-element.159.refs_1_.refs_0_, f32[4096,4608]{1,0:T(8,128)} %get-tuple-element.160.refs_1_, f32[4096,4608]{1,0:T(8,128)} %get-tuple-element.161.refs_2_, ...), custom_call_target="tpu_custom_call" | custom-call | flops 21743271936 | bytes 113246208 | tf_op jit(solution)/shard_map/pallas_call | solution.py:58
  746.2 13.7 %shard_map.196 = (bf16[1152,1152]{1,0:T(8,128)(2,1)}, f32[2,1152,1152]{2,1,0:T(8,128)}, f32[2,1152,1152]{2,1,0:T(8,128)}, s32[8,128]{1,0:T(8,128)}) custom-call(s32[2]{0:T(128)} %pad_add_fusion.place_ref, f32[1152,1152]{1,0:T(8,128)} %get-tuple-element.166.refs_0_, ...), custom_call_target="tpu_custom_call", output_to_operand_aliasing={{1}: (6, {}), {2}: (7, {})} | custom-call | flops 13271040 | bytes 34504704 | tf_op jit(solution)/shard_map/pallas_call | solution.py:58
  759.9 29.5 %shard_map.197 = (f32[2,288,2304]{2,1,0:T(8,128)}, bf16[2,288,2304]{2,1,0:T(8,128)(2,1)}, s32[8,128]{1,0:T(8,128)}) custom-call(s32[2]{0:T(128)} %pad_add_fusion.place_ref, bf16[1152,4096]{1,0:T(8,128)(2,1)} %get-tuple-element.124.refs_0_, bf16[2,4096,4608]{2,1,0:T(8,128)(2,1)} %get-tuple-element.165.refs_1_.refs_4_, s32[8,128]{1,0:T(8,128)} %get-tuple-element.171.refs_2_), custom_call_target="tpu_custom_call" | custom-call | flops 21743271936 | bytes 37748736 | tf_op jit(solution)/shard_map/pallas_call | solution.py:58
  792.0 29.8 %collective-permute-done.9.refs_2_ = bf16[288,2304]{1,0:T(8,128)(2,1)} collective-permute-done((bf16[288,2304]{1,0:T(8,128)(2,1)}, bf16[288,2304]{1,0:T(8,128)(2,1)}, u32[]{:S(2)}, u32[]{:S(2)}) %collective-permute-start.9) | collective-permute-done | bytes 1327136 | tf_op jit(solution)/shard_map/ppermute | solution.py:27
  823.8 26.5 %collective-permute-done.24.refs_2_ = bf16[288,2304]{1,0:T(8,128)(2,1)} collective-permute-done((bf16[288,2304]{1,0:T(8,128)(2,1)}, bf16[288,2304]{1,0:T(8,128)(2,1)}, u32[]{:S(2)}, u32[]{:S(2)}) %collective-permute-start.24) | collective-permute-done | bytes 1327136 | tf_op jit(solution)/shard_map/ppermute | solution.py:27
  852.8 55.3 %shard_map.198 = (bf16[2,4096,4608]{2,1,0:T(8,128)(2,1)}, s32[8,128]{1,0:T(8,128)}) custom-call(s32[2]{0:T(128)} %pad_add_fusion.place_ref, bf16[4096,1152]{1,0:T(8,128)(2,1)} %get-tuple-element.159.refs_1_.refs_0_, f32[4096,4608]{1,0:T(8,128)} %get-tuple-element.160.refs_1_, ...), custom_call_target="tpu_custom_call", output_to_operand_aliasing={{0}: (5, {})} | custom-call | flops 21743271936 | bytes 113246208 | tf_op jit(solution)/shard_map/pallas_call | solution.py:58
  935.6 29.5 %shard_map.201 = (f32[2,288,2304]{2,1,0:T(8,128)}, bf16[2,288,2304]{2,1,0:T(8,128)(2,1)}, s32[8,128]{1,0:T(8,128)}) custom-call(s32[2]{0:T(128)} %pad_add_fusion.place_ref, bf16[1152,4096]{1,0:T(8,128)(2,1)} %get-tuple-element.124.refs_0_, bf16[2,4096,4608]{2,1,0:T(8,128)(2,1)} %get-tuple-element.173.refs_1_, s32[8,128]{1,0:T(8,128)} %get-tuple-element.182.refs_2_), custom_call_target="tpu_custom_call" | custom-call | flops 21743271936 | bytes 37748736 | tf_op jit(solution)/shard_map/pallas_call | solution.py:58
  978.3 47.6 %collective-permute-done.27.refs_2_ = bf16[1152,1152]{1,0:T(8,128)(2,1)} collective-permute-done((bf16[1152,1152]{1,0:T(8,128)(2,1)}, bf16[1152,1152]{1,0:T(8,128)(2,1)}, u32[]{:S(2)}, u32[]{:S(2)}) %collective-permute-start.27) | collective-permute-done | bytes 2654240 | tf_op jit(solution)/shard_map/ppermute | solution.py:27
  1069.1 13.7 %collective-permute-done.33.refs_2_ = bf16[288,2304]{1,0:T(8,128)(2,1)} collective-permute-done((bf16[288,2304]{1,0:T(8,128)(2,1)}, bf16[288,2304]{1,0:T(8,128)(2,1)}, u32[]{:S(2)}, u32[]{:S(2)}) %collective-permute-start.33) | collective-permute-done | bytes 1327136 | tf_op jit(solution)/shard_map/ppermute | solution.py:27
  1085.3 26.0 %collective-permute-done.15.refs_2_ = bf16[288,2304]{1,0:T(8,128)(2,1)} collective-permute-done((bf16[288,2304]{1,0:T(8,128)(2,1)}, bf16[288,2304]{1,0:T(8,128)(2,1)}, u32[]{:S(2)}, u32[]{:S(2)}) %collective-permute-start.15) | collective-permute-done | bytes 1327136 | tf_op jit(solution)/shard_map/ppermute | solution.py:27
  1111.7 27.7 %collective-permute-done.36.refs_2_ = bf16[288,2304]{1,0:T(8,128)(2,1)} collective-permute-done((bf16[288,2304]{1,0:T(8,128)(2,1)}, bf16[288,2304]{1,0:T(8,128)(2,1)}, u32[]{:S(2)}, u32[]{:S(2)}) %collective-permute-start.36) | collective-permute-done | bytes 1327136 | tf_op jit(solution)/shard_map/ppermute | solution.py:27
  (89 shorter events, 228.7 us)
Async XLA Ops:
  0.6 106.3 %collective-permute-start = (bf16[2048,1152]{1,0:T(8,128)(2,1)}, bf16[2048,1152]{1,0:T(8,128)(2,1)}, u32[]{:S(2)}, u32[]{:S(2)}) collective-permute-start(bf16[2048,1152]{1,0:T(8,128)(2,1)} %bitcast.9), channel_id=1, source_target_pairs={{0,2},{1,3},{2,0},{3,1},{4,6},{5,7},{6,4},{7,5}} | collective-permute-start | bytes 14155784 | tf_op jit(solution)/shard_map/ppermute | solution.py:27
  4.0 242.6 %collective-permute-start.1 = (bf16[2048,1152]{1,0:T(8,128)(2,1)}, bf16[2048,1152]{1,0:T(8,128)(2,1)}, u32[]{:S(2)}, u32[]{:S(2)}) collective-permute-start(bf16[2048,1152]{1,0:T(8,128)(2,1)} %bitcast.4), channel_id=1, source_target_pairs={{0,2},{1,3},{2,0},{3,1},{4,6},{5,7},{6,4},{7,5}} | collective-permute-start | bytes 14155784 | tf_op jit(solution)/shard_map/ppermute | solution.py:27
  358.7 60.8 %collective-permute-start.3 = (bf16[2,288,2304]{2,1,0:T(8,128)(2,1)}, bf16[2,288,2304]{2,1,0:T(8,128)(2,1)}, u32[]{:S(2)}, u32[]{:S(2)}) collective-permute-start(bf16[2,288,2304]{2,1,0:T(8,128)(2,1)} %get-tuple-element.142), channel_id=1, source_target_pairs={{0,1},{1,0},{2,3},{3,2},{4,5},{5,4},{6,7},{7,6}} | collective-permute-start | bytes 7962632 | tf_op jit(solution)/shard_map/ppermute | solution.py:27
  513.5 63.1 %collective-permute-start.4 = (bf16[2,288,2304]{2,1,0:T(8,128)(2,1)}, bf16[2,288,2304]{2,1,0:T(8,128)(2,1)}, u32[]{:S(2)}, u32[]{:S(2)}) collective-permute-start(bf16[2,288,2304]{2,1,0:T(8,128)(2,1)} %get-tuple-element.151), channel_id=1, source_target_pairs={{0,1},{1,0},{2,3},{3,2},{4,5},{5,4},{6,7},{7,6}} | collective-permute-start | bytes 7962632 | tf_op jit(solution)/shard_map/ppermute | solution.py:27
  789.5 61.3 %collective-permute-start.6 = (bf16[2,288,2304]{2,1,0:T(8,128)(2,1)}, bf16[2,288,2304]{2,1,0:T(8,128)(2,1)}, u32[]{:S(2)}, u32[]{:S(2)}) collective-permute-start(bf16[2,288,2304]{2,1,0:T(8,128)(2,1)} %get-tuple-element.175), channel_id=1, source_target_pairs={{0,1},{1,0},{2,3},{3,2},{4,5},{5,4},{6,7},{7,6}} | collective-permute-start | bytes 7962632 | tf_op jit(solution)/shard_map/ppermute | solution.py:27
  791.7 58.6 %collective-permute-start.24 = (bf16[288,2304]{1,0:T(8,128)(2,1)}, bf16[288,2304]{1,0:T(8,128)(2,1)}, u32[]{:S(2)}, u32[]{:S(2)}) collective-permute-start(bf16[288,2304]{1,0:T(8,128)(2,1)} %get-tuple-element.196.refs_0_), channel_id=1, source_target_pairs={{0,2},{1,3},{2,0},{3,1},{4,6},{5,7},{6,4},{7,5}} | collective-permute-start | bytes 3981320 | tf_op jit(solution)/shard_map/ppermute | solution.py:27
  792.0 58.3 %collective-permute-start.23 = (bf16[288,2304]{1,0:T(8,128)(2,1)}, bf16[288,2304]{1,0:T(8,128)(2,1)}, u32[]{:S(2)}, u32[]{:S(2)}) collective-permute-start(bf16[288,2304]{1,0:T(8,128)(2,1)} %get-tuple-element.196.refs_0_), channel_id=1, source_target_pairs={{0,1},{1,0},{2,3},{3,2},{4,5},{5,4},{6,7},{7,6}} | collective-permute-start | bytes 3981320 | tf_op jit(solution)/shard_map/ppermute | solution.py:27
  821.8 104.0 %collective-permute-start.12 = (bf16[1152,1152]{1,0:T(8,128)(2,1)}, bf16[1152,1152]{1,0:T(8,128)(2,1)}, u32[]{:S(2)}, u32[]{:S(2)}) collective-permute-start(bf16[1152,1152]{1,0:T(8,128)(2,1)} %get-tuple-element.188.refs_0_), channel_id=1, source_target_pairs={{0,2},{1,3},{2,0},{3,1},{4,6},{5,7},{6,4},{7,5}} | collective-permute-start | bytes 7962632 | tf_op jit(solution)/shard_map/ppermute | solution.py:27
  823.8 141.3 %collective-permute-start.11 = (bf16[1152,1152]{1,0:T(8,128)(2,1)}, bf16[1152,1152]{1,0:T(8,128)(2,1)}, u32[]{:S(2)}, u32[]{:S(2)}) collective-permute-start(bf16[1152,1152]{1,0:T(8,128)(2,1)} %get-tuple-element.188.refs_0_), channel_id=1, source_target_pairs={{0,1},{1,0},{2,3},{3,2},{4,5},{5,4},{6,7},{7,6}} | collective-permute-start | bytes 7962632 | tf_op jit(solution)/shard_map/ppermute | solution.py:27
  850.3 75.4 %collective-permute-start.10 = (bf16[288,2304]{1,0:T(8,128)(2,1)}, bf16[288,2304]{1,0:T(8,128)(2,1)}, u32[]{:S(2)}, u32[]{:S(2)}) collective-permute-start(bf16[288,2304]{1,0:T(8,128)(2,1)} %collective-permute-done.9.refs_2_), channel_id=1, source_target_pairs={{0,1},{1,0},{2,3},{3,2},{4,5},{5,4},{6,7},{7,6}} | collective-permute-start | bytes 3981320 | tf_op jit(solution)/shard_map/ppermute | solution.py:27
  850.3 75.5 %collective-permute-start.25 = (bf16[288,2304]{1,0:T(8,128)(2,1)}, bf16[288,2304]{1,0:T(8,128)(2,1)}, u32[]{:S(2)}, u32[]{:S(2)}) collective-permute-start(bf16[288,2304]{1,0:T(8,128)(2,1)} %collective-permute-done.24.refs_2_), channel_id=1, source_target_pairs={{0,1},{1,0},{2,3},{3,2},{4,5},{5,4},{6,7},{7,6}} | collective-permute-start | bytes 3981320 | tf_op jit(solution)/shard_map/ppermute | solution.py:27
  850.8 84.8 %collective-permute-start.21 = (bf16[288,2304]{1,0:T(8,128)(2,1)}, bf16[288,2304]{1,0:T(8,128)(2,1)}, u32[]{:S(2)}, u32[]{:S(2)}) collective-permute-start(bf16[288,2304]{1,0:T(8,128)(2,1)} %get-tuple-element.194.refs_0_), channel_id=1, source_target_pairs={{0,2},{1,3},{2,0},{3,1},{4,6},{5,7},{6,4},{7,5}} | collective-permute-start | bytes 3981320 | tf_op jit(solution)/shard_map/ppermute | solution.py:27
  965.1 60.8 %collective-permute-start.27 = (bf16[1152,1152]{1,0:T(8,128)(2,1)}, bf16[1152,1152]{1,0:T(8,128)(2,1)}, u32[]{:S(2)}, u32[]{:S(2)}) collective-permute-start(bf16[1152,1152]{1,0:T(8,128)(2,1)} %get-tuple-element.203.refs_0_), channel_id=1, source_target_pairs={{0,2},{1,3},{2,0},{3,1},{4,6},{5,7},{6,4},{7,5}} | collective-permute-start | bytes 7962632 | tf_op jit(solution)/shard_map/ppermute | solution.py:27
  967.1 58.8 %collective-permute-start.13 = (bf16[1152,1152]{1,0:T(8,128)(2,1)}, bf16[1152,1152]{1,0:T(8,128)(2,1)}, u32[]{:S(2)}, u32[]{:S(2)}) collective-permute-start(bf16[1152,1152]{1,0:T(8,128)(2,1)} %collective-permute-done.12.refs_2_), channel_id=1, source_target_pairs={{0,1},{1,0},{2,3},{3,2},{4,5},{5,4},{6,7},{7,6}} | collective-permute-start | bytes 7962632 | tf_op jit(solution)/shard_map/ppermute | solution.py:27
  967.3 59.1 %collective-permute-start.7 = (bf16[2,288,2304]{2,1,0:T(8,128)(2,1)}, bf16[2,288,2304]{2,1,0:T(8,128)(2,1)}, u32[]{:S(2)}, u32[]{:S(2)}) collective-permute-start(bf16[2,288,2304]{2,1,0:T(8,128)(2,1)} %get-tuple-element.184), channel_id=1, source_target_pairs={{0,1},{1,0},{2,3},{3,2},{4,5},{5,4},{6,7},{7,6}} | collective-permute-start | bytes 7962632 | tf_op jit(solution)/shard_map/ppermute | solution.py:27
  967.8 91.9 %collective-permute-start.26 = (bf16[1152,1152]{1,0:T(8,128)(2,1)}, bf16[1152,1152]{1,0:T(8,128)(2,1)}, u32[]{:S(2)}, u32[]{:S(2)}) collective-permute-start(bf16[1152,1152]{1,0:T(8,128)(2,1)} %get-tuple-element.203.refs_0_), channel_id=1, source_target_pairs={{0,1},{1,0},{2,3},{3,2},{4,5},{5,4},{6,7},{7,6}} | collective-permute-start | bytes 7962632 | tf_op jit(solution)/shard_map/ppermute | solution.py:27
  978.1 81.7 %collective-permute-start.18 = (bf16[288,2304]{1,0:T(8,128)(2,1)}, bf16[288,2304]{1,0:T(8,128)(2,1)}, u32[]{:S(2)}, u32[]{:S(2)}) collective-permute-start(bf16[288,2304]{1,0:T(8,128)(2,1)} %get-tuple-element.193.refs_0_), channel_id=1, source_target_pairs={{0,2},{1,3},{2,0},{3,1},{4,6},{5,7},{6,4},{7,5}} | collective-permute-start | bytes 3981320 | tf_op jit(solution)/shard_map/ppermute | solution.py:27
  1025.9 58.9 %collective-permute-start.28 = (bf16[1152,1152]{1,0:T(8,128)(2,1)}, bf16[1152,1152]{1,0:T(8,128)(2,1)}, u32[]{:S(2)}, u32[]{:S(2)}) collective-permute-start(bf16[1152,1152]{1,0:T(8,128)(2,1)} %collective-permute-done.27.refs_2_), channel_id=1, source_target_pairs={{0,1},{1,0},{2,3},{3,2},{4,5},{5,4},{6,7},{7,6}} | collective-permute-start | bytes 7962632 | tf_op jit(solution)/shard_map/ppermute | solution.py:27
  1082.8 56.6 %collective-permute-start.36 = (bf16[288,2304]{1,0:T(8,128)(2,1)}, bf16[288,2304]{1,0:T(8,128)(2,1)}, u32[]{:S(2)}, u32[]{:S(2)}) collective-permute-start(bf16[288,2304]{1,0:T(8,128)(2,1)} %get-tuple-element.216.refs_0_), channel_id=1, source_target_pairs={{0,2},{1,3},{2,0},{3,1},{4,6},{5,7},{6,4},{7,5}} | collective-permute-start | bytes 3981320 | tf_op jit(solution)/shard_map/ppermute | solution.py:27
  1084.7 107.2 %collective-permute-start.34 = (bf16[288,2304]{1,0:T(8,128)(2,1)}, bf16[288,2304]{1,0:T(8,128)(2,1)}, u32[]{:S(2)}, u32[]{:S(2)}) collective-permute-start(bf16[288,2304]{1,0:T(8,128)(2,1)} %collective-permute-done.33.refs_2_), channel_id=1, source_target_pairs={{0,1},{1,0},{2,3},{3,2},{4,5},{5,4},{6,7},{7,6}} | collective-permute-start | bytes 3981320 | tf_op jit(solution)/shard_map/ppermute | solution.py:27
  1084.8 117.1 %collective-permute-start.14 = (bf16[288,2304]{1,0:T(8,128)(2,1)}, bf16[288,2304]{1,0:T(8,128)(2,1)}, u32[]{:S(2)}, u32[]{:S(2)}) collective-permute-start(bf16[288,2304]{1,0:T(8,128)(2,1)} %get-tuple-element.192.refs_0_), channel_id=1, source_target_pairs={{0,1},{1,0},{2,3},{3,2},{4,5},{5,4},{6,7},{7,6}} | collective-permute-start | bytes 3981320 | tf_op jit(solution)/shard_map/ppermute | solution.py:27
  1111.2 90.7 %collective-permute-start.16 = (bf16[288,2304]{1,0:T(8,128)(2,1)}, bf16[288,2304]{1,0:T(8,128)(2,1)}, u32[]{:S(2)}, u32[]{:S(2)}) collective-permute-start(bf16[288,2304]{1,0:T(8,128)(2,1)} %collective-permute-done.15.refs_2_), channel_id=1, source_target_pairs={{0,1},{1,0},{2,3},{3,2},{4,5},{5,4},{6,7},{7,6}} | collective-permute-start | bytes 3981320 | tf_op jit(solution)/shard_map/ppermute | solution.py:27
  1111.2 100.6 %collective-permute-start.35 = (bf16[288,2304]{1,0:T(8,128)(2,1)}, bf16[288,2304]{1,0:T(8,128)(2,1)}, u32[]{:S(2)}, u32[]{:S(2)}) collective-permute-start(bf16[288,2304]{1,0:T(8,128)(2,1)} %get-tuple-element.216.refs_0_), channel_id=1, source_target_pairs={{0,1},{1,0},{2,3},{3,2},{4,5},{5,4},{6,7},{7,6}} | collective-permute-start | bytes 3981320 | tf_op jit(solution)/shard_map/ppermute | solution.py:27
  1139.4 72.5 %collective-permute-start.37 = (bf16[288,2304]{1,0:T(8,128)(2,1)}, bf16[288,2304]{1,0:T(8,128)(2,1)}, u32[]{:S(2)}, u32[]{:S(2)}) collective-permute-start(bf16[288,2304]{1,0:T(8,128)(2,1)} %collective-permute-done.36.refs_2_), channel_id=1, source_target_pairs={{0,1},{1,0},{2,3},{3,2},{4,5},{5,4},{6,7},{7,6}} | collective-permute-start | bytes 3981320 | tf_op jit(solution)/shard_map/ppermute | solution.py:27
  (14 other events, 536.1 us)

commit v2 on v0

v2 whole, which is shorter than its diff:
```python
import functools

import jax
import jax.numpy as jnp
from jax import lax
from jax.experimental import pallas as pl
from jax.experimental.pallas import tpu as pltpu
from jax.sharding import PartitionSpec as P


f32, bf16 = jnp.float32, jnp.bfloat16
T, D, F = 2048, 1152, 4608
TT = 2 * T
HALF = F // 2
BM, BN = 1024, 768
NF, NH = F // BN, HALF // BN
RS, CS = 512, 256
NQ = 384
VMEM = 67043328
QD, QF = D // 4, F // 4
ANY = pl.BlockSpec(memory_space=pl.ANY)
TOKEN = jax.ShapeDtypeStruct((8, 128), jnp.int32)
NT = (((1,), (1,)), ((), ()))
TN = (((0,), (0,)), ((), ()))

OVER_X = [(d, d ^ 2) for d in range(4)]
OVER_CORE = [(d, d ^ 1) for d in range(4)]


def over(array, pairs):
    return lax.ppermute(array, "dp", pairs)


def sigmoid(g):
    return 0.5 * jnp.tanh(0.5 * g) + 0.5


def cuts(n, size):
    return [slice(at, at + size) for at in range(0, n, size)]


def added(first, total, new):
    return jnp.where(first, 0.0, total) + new


def gated(g, u, back):
    s = sigmoid(g)
    silu = g * s
    return (silu * u).astype(bf16), (back * u * (s + silu * (1 - s))).astype(bf16), (back * silu).astype(bf16)


def dot(a, b):
    return jnp.dot(a, b, preferred_element_type=f32)


def call(body, place, after, ins, outs, grid, scratch=(), jobs=()):
    bodies = [(body, len(ins), len(outs), len(scratch))] + [(job, len(i), len(o), len(s)) for i, o, job, s in jobs]
    ins = list(ins) + [one for i, _, _, _ in jobs for one in i]
    outs = list(outs) + [one for _, o, _, _ in jobs for one in o]
    scratch = list(scratch) + [one for _, _, _, s in jobs for one in s]
    arrays = [a for a, _ in ins]
    specs = [s for _, s in ins]
    aliases = {}
    held = [(k, buffer) for k, (_, _, buffer) in enumerate(outs) if buffer is not None]
    for n, (k, buffer) in enumerate(held):
        aliases[1 + len(arrays) + n] = k
    arrays += [buffer for _, buffer in held]
    specs += [ANY] * len(held)
    if after is not None:
        arrays.append(after)
        specs.append(ANY)
    skip = len(arrays) - len(ins)

    def kernel(place_ref, *refs):
        refs, rest = refs[: len(ins)], refs[len(ins) + skip :]
        results, token, own = rest[: len(outs)], rest[len(outs)], rest[len(outs) + 1 :]
        token[...] = jnp.zeros_like(token)
        parts = []
        at_in = at_out = at = 0
        for one, n_in, n_out, n in bodies:
            mine = (*refs[at_in : at_in + n_in], *results[at_out : at_out + n_out], *own[at : at + n])
            parts.append(functools.partial(one, place_ref, *mine))
            at_in, at_out, at = at_in + n_in, at_out + n_out, at + n
        for part, (one, *_) in zip(parts, bodies, strict=True):
            if getattr(one, "copies", False):
                part()
        last = [part() for part, (one, *_) in zip(parts, bodies, strict=True) if not getattr(one, "copies", False)]
        if last[0] is not None:
            last[0]()

    result = pl.pallas_call(
        kernel,
        grid_spec=pltpu.PrefetchScalarGridSpec(
            num_scalar_prefetch=1,
            grid=grid,
            in_specs=specs,
            out_specs=[s for _, s, _ in outs] + [pl.BlockSpec((8, 128), lambda *_: (0, 0))],
            scratch_shapes=scratch,
        ),
        out_shape=[o for o, _, _ in outs] + [TOKEN],
        input_output_aliases=aliases,
        cost_estimate=pl.CostEstimate(flops=T * D * F, bytes_accessed=T * D * F, transcendentals=0),
        compiler_params=pltpu.CompilerParams(vmem_limit_bytes=VMEM),
    )(place, *arrays)
    return result[:-1], result[-1]


def shaped(*shape, dtype=bf16):
    return jax.ShapeDtypeStruct(shape, dtype)


def normalise(h, a_s, aT):
    def rows_of(i, _):
        rows = pl.ds(pl.multiple_of(i * 256, 256), 256)
        wide = h[rows, :].astype(f32)
        scale = lax.rsqrt(jnp.mean(wide * wide, -1, keepdims=True) + 1e-6)
        a = (wide * scale).astype(bf16)
        a_s[rows, :] = a
        if aT is not None:
            aT[:, rows] = a.T
        return 0

    lax.fori_loop(0, h.shape[0] // 256, rows_of, 0)


def forward0(place, after, first, x, w_gate, w_up, w_down, held, whole):
    rows = x.shape[0]

    def tile(j, place):
        return jnp.where(j < NH, place[0] * NH + j, (1 - place[0]) * NH + j - NH)

    def body(place, x, wg, wu, *refs):
        if whole:
            wd, g_o, u_o, hid_o, aT_o, h_o, a1_o, aT1_o, a_s, hs, acc = refs
        else:
            g_o, u_o, hid_o, aT_o, a_s, hs = refs
        j = pl.program_id(1)

        @pl.when(j == 0)
        def _():
            normalise(x, a_s, aT_o)

        for r in cuts(BM, RS):
            a = a_s[r, :]
            for c in cuts(BN, CS):
                g, u = dot(a, wg[:, c]), dot(a, wu[:, c])
                g_o[r, c] = g
                u_o[r, c] = u
                hs[r, c] = (g * sigmoid(g) * u).astype(bf16)
            if whole:
                acc[r, :] = added(j == 0, acc[r, :], dot(hs[r, :], wd[...]))

        @pl.when(j < NH)
        def _():
            hid_o[...] = hs[...]

        if whole:

            @pl.when(j == NF - 1)
            def _():
                def rows_of(i, _):
                    rows = pl.ds(pl.multiple_of(i * 256, 256), 256)
                    h_o[rows, :] = x[rows, :] + acc[rows, :].astype(bf16)
                    return 0

                lax.fori_loop(0, BM // 256, rows_of, 0)
                normalise(h_o, a1_o, aT1_o)

    wide = pl.BlockSpec((BM, BN), lambda i, j, p: (first + i, tile(j, p)))
    into = pl.BlockSpec((None, D, BN), lambda i, j, p: (0, 0, tile(j, p)))
    plain = pl.BlockSpec((BM, D), lambda i, j, p: (i, 0))
    ins = [(x, plain), (w_gate, into), (w_up, into)]
    outs = [
        (shaped(TT, F, dtype=f32), wide, held[0]),
        (shaped(TT, F, dtype=f32), wide, held[1]),
        (shaped(TT, HALF), pl.BlockSpec((BM, BN), lambda i, j, p: (first + i, jnp.minimum(j, NH - 1))), held[2]),
        (shaped(D, TT), pl.BlockSpec((D, BM), lambda i, j, p: (0, first + i)), held[3]),
    ]
    scratch = [pltpu.VMEM((BM, D), bf16), pltpu.VMEM((BM, BN), bf16)]
    if whole:
        ins += [(w_down, pl.BlockSpec((None, BN, D), lambda i, j, p: (0, tile(j, p), 0)))]
        outs += [(shaped(T, D), plain, None), (shaped(T, D), plain, None)]
        outs += [(shaped(D, T), pl.BlockSpec((D, BM), lambda i, j, p: (0, i)), None)]
        scratch += [pltpu.VMEM((BM, D), f32)]
    return call(body, place, after, ins, outs, (rows // BM, NF), scratch)


def layer1(place, after, span, a1, aT, dy, w_gate, w_up, w_down, held):
    steps = T // BM
    first, stride, tiles = span
    t = first % NH
    rows = NQ if t == 1 else 2 * NQ

    def at(j):
        return first + stride * j

    def body(place, a1, aT, dy, wg, wu, wd, dgu_o, keep, out, down_keep, down_out, total, leaving, hid, down, down_leaving, sem):
        j, i = pl.program_id(0), pl.program_id(1)
        core = place[1]

        def mine(x, core):
            return pl.ds(pl.multiple_of((2 * x + core) * QD, QD), QD)

        def each(j, act):
            side = jnp.where(place[0] == at(j) // NH, 0, 1)
            columns = pl.ds(pl.multiple_of(j * BN, BN), BN)
            for x in range(2):
                act(pltpu.make_async_copy(total.at[:, mine(x, core), :], keep.at[:, x, :, columns], sem.at[x]))
            act(pltpu.make_async_copy(leaving, out.at[:, :, :, columns], sem.at[2]))
            for s in range(2):
                owner = (2 * t + s) // 3
                here, to = pl.ds(s * NQ, NQ), pl.ds(0 if t == 1 else s * NQ, NQ)

                @pl.when(core == owner)
                def _():
                    act(pltpu.make_async_copy(down.at[here, :], down_keep.at[side, to, :], sem.at[3 + s]))

                @pl.when(core != owner)
                def _():
                    act(pltpu.make_async_copy(down_leaving.at[here, :], down_out.at[side, to, :], sem.at[3 + s]))

        @pl.when((j > 0) & (i == 0))
        def _():
            each(j - 1, lambda copy: copy.wait())

        for r in cuts(BM, RS):
            a = a1[r, :]
            for c in cuts(BN, CS):
                g, u = dot(a, wg[:, c]), dot(a, wu[:, c])
                back = lax.dot_general(dy[r, :], wd[c, :], NT, preferred_element_type=f32).astype(bf16).astype(f32)
                hid[r, c], dgu_o[0, r, c], dgu_o[1, r, c] = gated(g, u, back)
        for k in range(2):
            total[k] = added(i == 0, total[k], dot(aT[...], dgu_o[k]))
        down[...] = added(i == 0, down[...], lax.dot_general(hid[...], dy[...], TN, preferred_element_type=f32))

        def last():
            @pl.when(i == steps - 1)
            def _():
                for x in range(2):
                    leaving[:, x] = total[:, mine(x, 1 - core), :].astype(bf16)
                down_leaving[...] = down[...].astype(bf16)
                each(j, lambda copy: copy.start())

            @pl.when((j == tiles - 1) & (i == steps - 1))
            def _():
                each(j, lambda copy: copy.wait())

        return last

    into = pl.BlockSpec((None, D, BN), lambda j, i, p: (1, 0, at(j)))
    plain = pl.BlockSpec((BM, D), lambda j, i, p: (i, 0))
    return call(
        body,
        place,
        after,
        [
            (a1, plain),
            (aT, pl.BlockSpec((D, BM), lambda j, i, p: (0, i))),
            (dy, plain),
            (w_gate, into),
            (w_up, into),
            (w_down, pl.BlockSpec((None, BN, D), lambda j, i, p: (1, at(j), 0))),
        ],
        [
            (shaped(2, T, F), pl.BlockSpec((2, BM, BN), lambda j, i, p: (0, i, at(j))), held[0]),
            (shaped(2, 2, QD, tiles * BN, dtype=f32), ANY, None),
            (shaped(2, 2, QD, tiles * BN), ANY, None),
            (shaped(2, rows, D, dtype=f32), ANY, held[1]),
            (shaped(2, rows, D), ANY, held[2]),
        ],
        (tiles, steps),
        [
            pltpu.VMEM((2, D, BN), f32),
            pltpu.VMEM((2, 2, QD, BN), bf16),
            pltpu.VMEM((BM, BN), bf16),
            pltpu.VMEM((BN, D), f32),
            pltpu.VMEM((BN, D), bf16),
            pltpu.SemaphoreType.DMA((5,)),
        ],
    )


def send_into_job(keep, came):
    def job(place, keep, came, out):
        out[...] = (keep[...] + came[...].astype(f32)).astype(bf16)

    columns = keep.shape[-1]
    half = pl.BlockSpec((None, None, QD, columns), lambda k, p: (k, 1 - p[0], 0, 0))
    return [(keep, half), (came, half)], [(shaped(2, QD, columns), pl.BlockSpec((None, QD, columns), lambda k, p: (k, 0, 0)), None)], job, ()


def send_down_job(keep, came):
    def job(place, keep, came, out):
        out[...] = (keep[...] + came[...].astype(f32)).astype(bf16)

    rows = keep.shape[1]
    theirs = pl.BlockSpec((None, rows // 2, D), lambda k, p: (1, k, 0))
    return [(keep, theirs), (came, theirs)], [(shaped(rows, D), pl.BlockSpec((rows // 2, D), lambda k, p: (k, 0)), None)], job, ()


def back1(place, after, dgu, dy, h, w_gate, w_up, jobs=()):
    WN = 2 * BN

    def body(place, dgu, wg, wu, h, dy, o, acc):
        j = pl.program_id(1)
        for r in cuts(BM, RS):
            for which, w in enumerate((wg, wu)):
                new = lax.dot_general(dgu[which, r, :], w[...], NT, preferred_element_type=f32)
                acc[which, r, :] = added(j == 0, acc[which, r, :], new)

        def last():
            @pl.when(j == F // WN - 1)
            def _():
                def rows_of(r, _):
                    r = pl.ds(pl.multiple_of(r * 256, 256), 256)
                    da = (acc[0, r, :].astype(bf16) + acc[1, r, :].astype(bf16)).astype(f32)
                    wide = h[r, :].astype(f32)
                    scale = lax.rsqrt(jnp.mean(wide * wide, -1, keepdims=True) + 1e-6)
                    along = jnp.mean(da * wide, -1, keepdims=True)
                    dwide = (da * scale - wide * (along * scale * scale * scale)).astype(bf16)
                    o[r, :] = dy[r, :] + dwide
                    return 0

                lax.fori_loop(0, BM // 256, rows_of, 0)

        return last

    into = pl.BlockSpec((None, D, WN), lambda i, j, p: (1, 0, j))
    plain = pl.BlockSpec((BM, D), lambda i, j, p: (i, 0))
    return call(
        body,
        place,
        after,
        [(dgu, pl.BlockSpec((2, BM, WN), lambda i, j, p: (0, i, j))), (w_gate, into), (w_up, into), (h, plain), (dy, plain)],
        [(shaped(T // BM, BM, D), pl.BlockSpec((None, BM, D), lambda i, j, p: (i, 0, 0)), None)],
        (T // BM, F // WN),
        [pltpu.VMEM((2, BM, D), f32)],
        jobs,
    )


def back0(place, after, span, dhs, gate, up, aT, w_down, jobs=()):
    first, _, tiles = span
    steps = TT // BM
    arrays = []
    for array, _ in dhs:
        if not any(array is one for one in arrays):
            arrays.append(array)

    def body(place, *refs):
        refs, (g_r, u_r, aT, wd, into_own, into_out, dgu, total, dh, sem) = refs[: len(arrays)], refs[len(arrays) :]
        j, i = pl.program_id(0), pl.program_id(1)

        def copy(k):
            array, index = dhs[k]
            source = refs[next(n for n, one in enumerate(arrays) if one is array)]
            return pltpu.make_async_copy(source.at[index], dh.at[k], sem.at[k])

        @pl.when((j == 0) & (i == 0))
        def _():
            for k in range(steps):
                copy(k).start()

        for k in range(steps):
            pl.when((j == 0) & (i == k))(lambda k=k: copy(k).wait())

        for r in cuts(BM, RS):
            for c in cuts(BN, CS):
                back = lax.dot_general(dh[i, r, :], wd[c, :], NT, preferred_element_type=f32).astype(bf16).astype(f32)
                _, dgu[0, r, c], dgu[1, r, c] = gated(g_r[r, c], u_r[r, c], back)
        for k in range(2):
            total[k] = added(i == 0, total[k], dot(aT[...], dgu[k]))

        def last():
            @pl.when(i == steps - 1)
            def _():
                into_own[...] = total[:, pl.ds(pl.multiple_of(place[1] * QD, QD), QD), :]
                into_out[...] = total[:, pl.ds(pl.multiple_of((1 - place[1]) * QD, QD), QD), :].astype(bf16)

        return last

    wide = pl.BlockSpec((BM, BN), lambda j, i, p: (i, first + j))
    block = pl.BlockSpec((2, QD, BN), lambda j, i, p: (0, 0, j))
    return call(
        body,
        place,
        after,
        [(array, ANY) for array in arrays]
        + [
            (gate, wide),
            (up, wide),
            (aT, pl.BlockSpec((2 * QD, BM), lambda j, i, p: (p[0], i))),
            (w_down, pl.BlockSpec((None, BN, D), lambda j, i, p: (0, first + j, 0))),
        ],
        [(shaped(2, QD, tiles * BN, dtype=f32), block, None), (shaped(2, QD, tiles * BN), block, None)],
        (tiles, steps),
        [
            pltpu.VMEM((2, BM, BN), bf16),
            pltpu.VMEM((2, 2 * QD, BN), f32),
            pltpu.VMEM((steps, BM, D), bf16),
            pltpu.SemaphoreType.DMA((steps,)),
        ],
        jobs,
    )


def grad_down(place, after, hidden, dhs):
    rows = 384
    n = QF // rows

    def tile(i, place):
        return jnp.where(i < n, place[1] * n + i, (1 - place[1]) * n + i - n)

    def body(place, hidden, *refs):
        dhs, (own, out) = refs[:-2], refs[-2:]
        i = pl.program_id(0)
        total = None
        for k, dh in enumerate(dhs):
            term = lax.dot_general(hidden[k * BM : (k + 1) * BM, :], dh[...], TN, preferred_element_type=f32)
            total = term if total is None else total + term

        @pl.when(i < n)
        def _():
            own[...] = total

        @pl.when(i >= n)
        def _():
            out[...] = total.astype(bf16)

    once = pl.Buffered(1)
    return call(
        body,
        place,
        after,
        [(hidden, pl.BlockSpec((TT, rows), lambda i, p: (0, tile(i, p))))]
        + [(b, pl.BlockSpec((None, BM, D), lambda i, p, k=k: (k, 0, 0), pipeline_mode=once)) for b, k in dhs],
        [
            (shaped(QF, D, dtype=f32), pl.BlockSpec((rows, D), lambda i, p: (jnp.minimum(i, n - 1), 0)), None),
            (shaped(QF, D), pl.BlockSpec((rows, D), lambda i, p: (jnp.maximum(i - n, 0), 0)), None),
        ],
        (2 * n,),
    )


def adamw(g, w, m, v):
    g = g.astype(bf16).astype(f32)
    m = 0.9 * m + 0.1 * g
    v = 0.95 * v + 0.05 * g * g
    return (w - 0.02 * (m * lax.rsqrt(v + 1e-8) + 0.1 * w)).astype(bf16), m, v


def nothing(place):
    pass


def down_job(layer, chunks, own, came, far, w, m, v, held):
    on0, on1, n = chunks

    def job(place, *refs):
        terms, (w, m, v, new_o, m_o, v_o) = refs[:-6], refs[-6:]
        g = sum(term[...].astype(f32) for term in terms)
        new_o[...], m_o[...], v_o[...] = adamw(g, w[...].astype(f32), m[...], v[...])

    def at(s, p):
        return s + jnp.where(p[1] == 0, on0, on1)

    block = pl.BlockSpec((NQ, D), lambda s, p: (s, 0))
    ours = pl.BlockSpec((None, NQ, D), lambda s, p: (0, s, 0)) if far else block
    kept = pl.BlockSpec((None, NQ, D), lambda s, p: (layer, at(s, p), 0))
    whole = pl.BlockSpec((None, NQ, D), lambda s, p: (layer, (2 * p[0] + p[1]) * 3 + at(s, p), 0))
    ins = [(own, ours), (came, ours)] + [(one, block) for one in far] + [(w, whole), (m, kept), (v, kept)]
    outs = [(shaped(n * NQ, D), block, None)]
    outs += [(shaped(2, QF, D, dtype=f32), kept, one) for one in held]
    return ins, outs, job, ()


def into_job(layer, span, parts, ws, ms, vs, held):
    first, stride, tiles = span
    columns = 384
    per = BN // columns
    terms = len(parts)

    def at(s):
        return (first + stride * (s // per)) * per + s % per

    def job(place, *refs):
        parts, refs = refs[:terms], refs[terms:]
        ws, ms, vs = refs[:2], refs[2:4], refs[4:6]
        new, m_o, v_o = refs[6], refs[7:9], refs[9:11]
        for k in range(2):
            g = sum(part[k].astype(f32) for part in parts)
            new[k], m_o[k][...], v_o[k][...] = adamw(g, ws[k][...].astype(f32), ms[k][...], vs[k][...])

    block = pl.BlockSpec((2, QD, columns), lambda s, p: (0, 0, s))
    of_both = pl.BlockSpec((2, None, QD, columns), lambda s, p: (0, p[0], 0, s))
    whole = pl.BlockSpec((None, QD, columns), lambda s, p: (layer, 2 * p[0] + p[1], at(s)))
    kept = pl.BlockSpec((None, QD, columns), lambda s, p: (layer, 0, at(s)))
    ins = [(part, of_both if part.ndim == 4 else block) for part in parts]
    ins += [(w, whole) for w in ws] + [(m, kept) for m in ms] + [(v, kept) for v in vs]
    outs = [(shaped(2, QD, tiles * BN), block, None)] + [(shaped(2, QD, F, dtype=f32), kept, one) for one in held]
    return ins, outs, job, ()


def alone(place, after, grid, jobs):
    return call(nothing, place, after, [], [], grid, jobs=jobs)


def down_pieces(layer, chunks, blocks):
    on0, on1, n = chunks
    rows = n * NQ // 2
    for r, block in enumerate(blocks):
        for h in range(2):

            def there(place, r=r, h=h):
                d = jnp.bitwise_xor(2 * place[0] + place[1], r)
                at = d * QF + jnp.where(lax.rem(d, 2) == 0, on0, on1) * NQ + h * rows
                return layer, pl.ds(pl.multiple_of(at, 192), rows), slice(None)

            yield block, (slice(h * rows, (h + 1) * rows), slice(None)), "down", there


def into_pieces(layer, span, blocks):
    first, stride, tiles = span
    if stride == 1:
        places = [(0, first, tiles)]
    else:
        places = [(j, first + stride * j, 1) for j in range(tiles)]
    for r, block in enumerate(blocks):
        for k, name in enumerate(("gate", "up")):
            for here, to, n in places:

                def there(place, r=r, to=to, n=n):
                    d = jnp.bitwise_xor(2 * place[0] + place[1], r)
                    return layer, pl.ds(pl.multiple_of(d * QD, QD), QD), slice(to * BN, (to + n) * BN)

                yield block, (k, slice(None), slice(here * BN, (here + n) * BN)), name, there


def copy_job(grid, q, pieces, held):
    pieces = list(pieces)
    sources, names = [], []
    for block, _, name, _ in pieces:
        if not any(block is one for one in sources):
            sources.append(block)
        if name not in names:
            names.append(name)
    block, part, _, _ = pieces[0]
    shape = jax.eval_shape(lambda b: b[part], block).shape
    groups = [pieces[at : at + q] for at in range(0, len(pieces), q)]
    steps = grid[0] * (grid[1] if len(grid) > 1 else 1)
    assert steps >= len(groups) + 2

    def body(place, *refs):
        outs, (buffer, reads, writes) = dict(zip(names, refs[len(sources) : -3], strict=True)), refs[-3:]
        step = pl.program_id(0) if len(grid) == 1 else pl.program_id(0) * grid[1] + pl.program_id(1)

        def copies(g):
            for n, (block, part, name, there) in enumerate(groups[g]):
                source = refs[next(k for k, one in enumerate(sources) if one is block)]
                slot = (g % 2) * q + n
                yield (
                    functools.partial(pltpu.make_async_copy, source.at[part], buffer.at[slot], reads.at[slot]),
                    functools.partial(pltpu.make_async_copy, buffer.at[slot], outs[name].at[there(place)], writes.at[slot]),
                )

        for s in range(len(groups) + 2):

            @pl.when(step == s)
            def _(s=s):
                if s >= 2:
                    for _, write in copies(s - 2):
                        write().wait()
                if s < len(groups):
                    for read, _ in copies(s):
                        read().start()
                if 1 <= s <= len(groups):
                    for read, write in copies(s - 1):
                        read().wait()
                        write().start()

    body.copies = True
    whole = {"gate": shaped(2, D, F), "up": shaped(2, D, F), "down": shaped(2, F, D)}
    outs = [(whole[name], ANY, held[name]) for name in names]
    scratch = (pltpu.VMEM((2 * q,) + shape, bf16), pltpu.SemaphoreType.DMA((2 * q,)), pltpu.SemaphoreType.DMA((2 * q,)))
    return [(one, ANY) for one in sources], outs, body, scratch


def spread(new):
    far = over(new, OVER_X)
    near = over(new, OVER_CORE)
    return [new, near, far, over(far, OVER_CORE)]


def whole_step(x, dy, w_gate, w_up, w_down, m_gate, m_up, m_down, v_gate, v_up, v_down):
    d = lax.axis_index("dp")
    place = jnp.stack([d // 2, d % 2]).astype(jnp.int32)
    x, dy = x[0], dy[0]
    x_far = over(x, OVER_X)

    weights = (w_gate, w_up, w_down)
    (gate, up, hid0, aT0, h, a1, aT1), t = forward0(place, None, 0, x, *weights, [None] * 4, True)

    mv = {"into": (None,) * 4, "down": (None,) * 2}
    ALL, ONE, TWO = (0, 0, 3), (2, 0, 1), (0, 1, 2)

    def into(layer, span, *parts):
        return into_job(layer, span, parts, (w_gate, w_up), (m_gate, m_up), (v_gate, v_up), mv["into"])

    def down(layer, chunks, own, came, *far):
        return down_job(layer, chunks, own, came, far, w_down, m_down, v_down, mv["down"])

    def took(results, kind):
        new, *mv[kind] = results
        return spread(new)

    dgu = None
    terms, new1 = {}, {}

    SPANS = {"p": (1, 1, 1), "q": (4, 1, 1), "r": (0, 3, 1), "s": (3, 3, 1), "t": (2, 3, 2)}

    def gradients(t, name, held_down):
        nonlocal dgu
        (dgu, keep, out, *downs), t = layer1(place, t, SPANS[name], a1, aT1, dy, *weights, [dgu, *held_down])
        terms[name] = [keep, over(out, OVER_CORE)]
        return t, downs

    def send(t, name, downs=None):
        jobs = [send_into_job(*terms[name])]
        if downs is not None:
            downs[1] = over(downs[1], OVER_CORE)
            jobs.append(send_down_job(*downs))
        results, t = call(nothing, place, t, [], [], (2,), jobs=jobs)
        terms[name].append(over(results[0], OVER_X))
        if downs is not None:
            downs.append(over(results[1], OVER_X))
        return t

    def adam(t, name):
        span = SPANS[name]
        results, t = alone(place, t, (2 * span[2],), [into(1, span, *terms[name])])
        new1[name] = took(results, "into")
        return t

    def adam_down(t, chunks, downs):
        results, t = alone(place, t, (chunks[2],), [down(1, chunks, *downs)])
        return took(results, "down"), t

    t, downs1 = gradients(t, "p", (None, None))
    t = send(t, "p")
    t, downs1 = gradients(t, "q", downs1)
    t = adam(t, "p")
    t = send(t, "q", downs1)
    t, downs2 = gradients(t, "r", (None, None))
    t = adam(t, "q")
    t = send(t, "r")
    t, downs2 = gradients(t, "s", downs2)
    down1, t = adam_down(t, ONE, downs1)
    t = send(t, "s")
    t = adam(t, "r")
    t, downs2 = gradients(t, "t", downs2)
    t = send(t, "t", downs2)
    (dh,), t = back1(place, t, dgu, dy, h, w_gate, w_up)
    dh_far = over(dh, OVER_X)
    t = adam(t, "s")
    t = adam(t, "t")
    down2, t = adam_down(t, TWO, downs2)
    (gate, up, hid0, aT0), t = forward0(place, t, T // BM, x_far, *weights, [gate, up, hid0, aT0], False)
    dhs = [(dh, 0), (dh, 1), (dh_far, 0), (dh_far, 1)]

    weights_out = {"gate": None, "up": None, "down": None}

    def copying(grid, q, pieces):
        return copy_job(grid, q, pieces, weights_out)

    def copied(results, names):
        weights_out.update(zip(names, results, strict=True))

    (own_d, out_d), t = grad_down(place, t, hid0, dhs)
    came_d = over(out_d, OVER_CORE)
    results, t = alone(place, t, (3,), [down(0, ALL, own_d, came_d)])
    down0 = took(results, "down")

    def first_pieces(*names):
        return [piece for name in names for piece in into_pieces(1, SPANS[name], new1[name])]

    new0 = {}
    spans = {"a": (0, 1, 3), "c": (3, 1, 2), "d": (5, 1, 1)}
    beside = {
        "a": lambda: [copying((3, 4), 4, first_pieces("p", "q", "r", "s")), copying((3, 4), 1, down_pieces(1, ONE, down1))],
        "c": lambda: [
            copying((2, 4), 4, first_pieces("t")),
            copying((2, 4), 2, [*down_pieces(1, TWO, down2)]),
        ],
        "d": lambda: [copying((1, 4), 4, down_pieces(0, ALL, down0))],
    }
    for name, span in spans.items():
        (own, out, *results), t = back0(place, t, span, dhs, gate, up, aT0, w_down, beside[name]())
        copied(results, ("gate", "up", "down")[-len(results) :])
        came = over(out, OVER_CORE)
        results, t = alone(place, t, (2 * span[2],), [into(0, span, own, came)])
        new0[name] = took(results, "into")

    for name, q in (("a", 4), ("c", 8), ("d", 8)):
        grid = (8 // q + 2,)
        results, t = call(nothing, place, t, [], [], grid, jobs=[copying(grid, q, into_pieces(0, spans[name], new0[name]))])
        copied(results, ("gate", "up"))
    held, o_down = (weights_out["gate"], weights_out["up"]), weights_out["down"]
    (m_gate, m_up, v_gate, v_up), (m_down, v_down) = mv["into"], mv["down"]
    return *held, o_down, m_gate, m_up, m_down, v_gate, v_up, v_down


def solution(mesh):
    sequences, whole = P(("rep", "dp"), None, None), P(None, None, None)
    block, group, own = P(None, "dp", None), P("rep", None, None), P("rep", "dp", None)
    return jax.shard_map(
        whole_step,
        mesh=mesh,
        in_specs=(sequences,) * 2 + (whole,) * 3 + (block,) * 6,
        out_specs=(group,) * 3 + (own,) * 6,
        check_vma=False,
    )
```

time: 1630 us -> 1230 us (0.75)
  Pallas kernels: 0 us -> 736 us
  matrix products: 514 us -> 0 us
  waiting for transfers between devices: 864 us -> 465 us
  other arithmetic: 170 us -> 0.59 us
  local copies, waits for them, and re-layouts: 60.8 us -> 1.35 us
  starting transfers between devices: 0.55 us -> 25.7 us
    pallas_call x0 -> x31, Pallas kernels: none -> 736 us  [call(): pl.pallas_call(kernel, grid_spec=pltpu.PrefetchScalarGridSpec(num_scalar_...]
    dot_general x15 -> x0, matrix products: 514 us -> none  [the longest x5 179 us: layer(): up = jnp.dot(a, w['w_up'], preferred_element_type=jnp.float32)]
    unnamed x15 -> x0, waiting for transfers between devices: 499 us -> none
    ppermute x0 -> x53, waiting for transfers between devices: none -> 465 us  [over(): return lax.ppermute(array, 'dp', pairs)]
    reshape x3 -> x0, waiting for transfers between devices: 364 us -> none  [step(): t.reshape(-1, *t.shape[2:])]
    unnamed x5 -> x0, other arithmetic: 79.6 us -> none
    reshape x3 -> x0, other arithmetic: 70.3 us -> none  [step(): t.reshape(-1, *t.shape[2:])]
    unnamed x43 -> x8, local copies, waits for them, and re-layouts: 60.2 us -> 1.35 us
  transfers between devices with their start and end apart: 9 -> 53, of which waited for: 7 -> 19; matrix products, arithmetic and copies ran while one was open for 28% -> 0% of each run, Pallas kernels for 0% -> 37%
where the time goes in v2:
time: 1230 us
  Pallas kernels  736 us (60%)
  waiting for transfers between devices  465 us (38%)
  starting transfers between devices  25.7 us (2%)
    pallas_call x31, Pallas kernels, call(): pl.pallas_call(kernel, grid_spec=pltpu.PrefetchScalarGridSpec(num_scalar_...  736 us
    ppermute x53, waiting for transfers between devices, over(): return lax.ppermute(array, 'dp', pairs)  465 us
    ppermute x53, starting transfers between devices, over(): return lax.ppermute(array, 'dp', pairs)  25.7 us
  transfers between devices with their start and end apart: 53, of which 19 were waited for; matrix products, arithmetic and copies ran while one was open for 0% of the time, Pallas kernels for 37%

profile of v2, /device:TPU:0, one launch (start us, length us, event | category | flops | bytes accessed | tf_op | source)
XLA Modules:
  0.0 1230.2 jit_solution(2024611225524550248)
XLA Ops:
  1.2 94.3 %shard_map.178 = (f32[4096,4608]{1,0:T(8,128)}, f32[4096,4608]{1,0:T(8,128)}, bf16[4096,2304]{1,0:T(8,128)(2,1)}, bf16[1152,4096]{1,0:T(8,128)(2,1)}, bf16[2048,...) custom-call(s32[2]{0:T(128)} %pad_add_fusion.place_ref, ...), custom_call_target="tpu_custom_call" | custom-call | flops 10871635968 | bytes 10871635968 | tf_op jit(solution)/shard_map/pallas_call | solution.py:91
  95.5 34.4 %shard_map.179 = (bf16[2,2048,4608]{2,1,0:T(8,128)(2,1)}, f32[2,2,288,768]{3,2,1,0:T(8,128)}, bf16[2,2,288,768]{3,2,1,0:T(8,128)(2,1)}, f32[2,384,1152]{2,1,0:T(...) custom-call(s32[2]{0:T(128)} %pad_add_fusion.place_ref, bf16[2048,1152]{1,0:T(8,128)(2,1)} %get-tuple-element.153.refs_0_, ...), custom_call_target="tpu_custom_call" | custom-call | flops 10871635968 | bytes 10871635968 | tf_op jit(solution)/shard_map/pallas_call | solution.py:91
  140.5 34.5 %shard_map.181 = (bf16[2,2048,4608]{2,1,0:T(8,128)(2,1)}, f32[2,2,288,768]{3,2,1,0:T(8,128)}, bf16[2,2,288,768]{3,2,1,0:T(8,128)(2,1)}, f32[2,384,1152]{2,1,0:T(...) custom-call(s32[2]{0:T(128)} %pad_add_fusion.place_ref, ...), custom_call_target="tpu_custom_call", output_to_operand_aliasing={{0}: (7, {}), {3}: (8, {}), {4}: (9, {})} | custom-call | flops 10871635968 | bytes 10871635968 | tf_op jit(solution)/shard_map/pallas_call | solution.py:91
  185.8 34.7 %shard_map.184 = (bf16[2,2048,4608]{2,1,0:T(8,128)(2,1)}, f32[2,2,288,768]{3,2,1,0:T(8,128)}, bf16[2,2,288,768]{3,2,1,0:T(8,128)(2,1)}, f32[2,768,1152]{2,1,0:T(...) custom-call(s32[2]{0:T(128)} %pad_add_fusion.place_ref, ...), custom_call_target="tpu_custom_call", output_to_operand_aliasing={{0}: (7, {})} | custom-call | flops 10871635968 | bytes 10871635968 | tf_op jit(solution)/shard_map/pallas_call | solution.py:91
  231.6 34.6 %shard_map.187 = (bf16[2,2048,4608]{2,1,0:T(8,128)(2,1)}, f32[2,2,288,768]{3,2,1,0:T(8,128)}, bf16[2,2,288,768]{3,2,1,0:T(8,128)(2,1)}, f32[2,768,1152]{2,1,0:T(...) custom-call(s32[2]{0:T(128)} %pad_add_fusion.place_ref, ...), custom_call_target="tpu_custom_call", output_to_operand_aliasing={{0}: (7, {}), {3}: (8, {}), {4}: (9, {})} | custom-call | flops 10871635968 | bytes 10871635968 | tf_op jit(solution)/shard_map/pallas_call | solution.py:91
  294.4 63.1 %shard_map.191 = (bf16[2,2048,4608]{2,1,0:T(8,128)(2,1)}, f32[2,2,288,1536]{3,2,1,0:T(8,128)}, bf16[2,2,288,1536]{3,2,1,0:T(8,128)(2,1)}, f32[2,768,1152]{2,1,0:...) custom-call(s32[2]{0:T(128)} %pad_add_fusion.place_ref, ...), custom_call_target="tpu_custom_call", output_to_operand_aliasing={{0}: (7, {}), {3}: (8, {}), {4}: (9, {})} | custom-call | flops 10871635968 | bytes 10871635968 | tf_op jit(solution)/shard_map/pallas_call | solution.py:91
  377.1 62.9 %shard_map.193 = (bf16[2,1024,1152]{2,1,0:T(8,128)(2,1)}, s32[8,128]{1,0:T(8,128)}) custom-call(s32[2]{0:T(128)} %pad_add_fusion.place_ref, bf16[2,2048,4608]{2,1,0:T(8,128)(2,1)} %get-tuple-element.200.refs_0_, bf16[2,1152,4608]{2,1,0:T(8,128)(2,1)} %refs_2_.13, bf16[2,1152,4608]{2,1,0:T(8,128)(2,1)} %refs_3_.33, ...), custom_call_target="tpu_custom_call" | custom-call | flops 10871635968 | bytes 10871635968 | tf_op jit(solution)/shard_map/pallas_call | solution.py:91
  442.0 40.5 %collective-permute-done.15.refs_2_ = bf16[2,288,768]{2,1,0:T(8,128)(2,1)} collective-permute-done((bf16[2,288,768]{2,1,0:T(8,128)(2,1)}, bf16[2,288,768]{2,1,0:T(8,128)(2,1)}, u32[]{:S(2)}, u32[]{:S(2)}) %collective-permute-start.15) | collective-permute-done | bytes 884768 | tf_op jit(solution)/shard_map/ppermute | solution.py:31
  488.8 31.5 %collective-permute-done.14.refs_2_ = bf16[2,288,1536]{2,1,0:T(8,128)(2,1)} collective-permute-done((bf16[2,288,1536]{2,1,0:T(8,128)(2,1)}, bf16[2,288,1536]{2,1,0:T(8,128)(2,1)}, u32[]{:S(2)}, u32[]{:S(2)}) %collective-permute-start.14) | collective-permute-done | bytes 1769504 | tf_op jit(solution)/shard_map/ppermute | solution.py:31
  530.3 147.6 %collective-permute-done.13.refs_2_ = bf16[768,1152]{1,0:T(8,128)(2,1)} collective-permute-done((bf16[768,1152]{1,0:T(8,128)(2,1)}, bf16[768,1152]{1,0:T(8,128)(2,1)}, u32[]{:S(2)}, u32[]{:S(2)}) %collective-permute-start.13) | collective-permute-done | bytes 1769504 | tf_op jit(solution)/shard_map/ppermute | solution.py:31
  687.8 64.4 %shard_map.197 = (f32[4096,4608]{1,0:T(8,128)}, f32[4096,4608]{1,0:T(8,128)}, bf16[4096,2304]{1,0:T(8,128)(2,1)}, bf16[1152,4096]{1,0:T(8,128)(2,1)}, s32[8,128]{1,0:T(8,128)}) custom-call(s32[2]{0:T(128)} %pad_add_fusion.place_ref, ...), custom_call_target="tpu_custom_call", output_to_operand_aliasing={{0}: (4, {}), {1}: (5, {}), {2}: (6, {}), {3}: (7, {})} | custom-call | flops 10871635968 | bytes 10871635968 | tf_op jit(solution)/shard_map/pallas_call | solution.py:91
  752.2 33.2 %shard_map.198 = (f32[1152,1152]{1,0:T(8,128)}, bf16[1152,1152]{1,0:T(8,128)(2,1)}, s32[8,128]{1,0:T(8,128)}) custom-call(s32[2]{0:T(128)} %pad_add_fusion.place_ref, bf16[4096,2304]{1,0:T(8,128)(2,1)} %get-tuple-element.233.refs_0_, bf16[2,1024,1152]{2,1,0:T(8,128)(2,1)} %get-tuple-element.208.refs_1_.refs_2_.refs_0_, ...), custom_call_target="tpu_custom_call" | custom-call | flops 10871635968 | bytes 10871635968 | tf_op jit(solution)/shard_map/pallas_call | solution.py:91
  792.1 16.5 %collective-permute-done.30.refs_12_ = bf16[2,288,768]{2,1,0:T(8,128)(2,1)S(1)} collective-permute-done((bf16[2,288,768]{2,1,0:T(8,128)(2,1)}, bf16[2,288,768]{2,1,0:T(8,128)(2,1)S(1)}, u32[]{:S(2)}, u32[]{:S(2)}) %collective-permute-start.30) | collective-permute-done | bytes 884768 | tf_op jit(solution)/shard_map/ppermute | solution.py:31
  810.2 17.6 %collective-permute-done.39.refs_24_ = bf16[384,1152]{1,0:T(8,128)(2,1)} collective-permute-done((bf16[384,1152]{1,0:T(8,128)(2,1)}, bf16[384,1152]{1,0:T(8,128)(2,1)}, u32[]{:S(2)}, u32[]{:S(2)}) %collective-permute-start.39) | collective-permute-done | bytes 884768 | tf_op jit(solution)/shard_map/ppermute | solution.py:31
  829.2 17.5 %collective-permute-done.33.refs_16_ = bf16[2,288,768]{2,1,0:T(8,128)(2,1)} collective-permute-done((bf16[2,288,768]{2,1,0:T(8,128)(2,1)}, bf16[2,288,768]{2,1,0:T(8,128)(2,1)}, u32[]{:S(2)}, u32[]{:S(2)}) %collective-permute-start.33) | collective-permute-done | bytes 884768 | tf_op jit(solution)/shard_map/ppermute | solution.py:31
  846.7 18.0 %collective-permute-done.36.refs_20_ = bf16[2,288,768]{2,1,0:T(8,128)(2,1)} collective-permute-done((bf16[2,288,768]{2,1,0:T(8,128)(2,1)}, bf16[2,288,768]{2,1,0:T(8,128)(2,1)}, u32[]{:S(2)}, u32[]{:S(2)}) %collective-permute-start.36) | collective-permute-done | bytes 884768 | tf_op jit(solution)/shard_map/ppermute | solution.py:31
  879.5 66.2 %shard_map.200 = (f32[2,288,2304]{2,1,0:T(8,128)}, bf16[2,288,2304]{2,1,0:T(8,128)(2,1)}, bf16[2,1152,4608]{2,1,0:T(8,128)(2,1)}, bf16[2,1152,4608]{2,1,0:T(8,12...) custom-call(s32[2]{0:T(128)} %pad_add_fusion.place_ref, ...), custom_call_target="tpu_custom_call" | custom-call | flops 10871635968 | bytes 10871635968 | tf_op jit(solution)/shard_map/pallas_call | solution.py:91
  948.2 39.3 %collective-permute-done.24.refs_12_ = bf16[768,1152]{1,0:T(8,128)(2,1)} collective-permute-done((bf16[768,1152]{1,0:T(8,128)(2,1)}, bf16[768,1152]{1,0:T(8,128)(2,1)}, u32[]{:S(2)}, u32[]{:S(2)}) %collective-permute-start.24) | collective-permute-done | bytes 1769504 | tf_op jit(solution)/shard_map/ppermute | solution.py:31
  987.5 37.4 %collective-permute-done.21.refs_8_ = bf16[2,288,1536]{2,1,0:T(8,128)(2,1)} collective-permute-done((bf16[2,288,1536]{2,1,0:T(8,128)(2,1)}, bf16[2,288,1536]{2,1,0:T(8,128)(2,1)}, u32[]{:S(2)}, u32[]{:S(2)}) %collective-permute-start.21) | collective-permute-done | bytes 1769504 | tf_op jit(solution)/shard_map/ppermute | solution.py:31
  1038.9 48.4 %shard_map.202 = (f32[2,288,1536]{2,1,0:T(8,128)}, bf16[2,288,1536]{2,1,0:T(8,128)(2,1)}, bf16[2,1152,4608]{2,1,0:T(8,128)(2,1)}, bf16[2,1152,4608]{2,1,0:T(8,12...) custom-call(s32[2]{0:T(128)} %pad_add_fusion.place_ref, ...), custom_call_target="tpu_custom_call", output_to_operand_aliasing={{2}: (15, {}), {3}: (16, {}), {4}: (17, {})} | custom-call | flops 10871635968 | bytes 10871635968 | tf_op jit(solution)/shard_map/pallas_call | solution.py:91
  1100.8 30.5 %shard_map.204 = (f32[2,288,768]{2,1,0:T(8,128)}, bf16[2,288,768]{2,1,0:T(8,128)(2,1)}, bf16[2,4608,1152]{2,1,0:T(8,128)(2,1)}, s32[8,128]{1,0:T(8,128)}) custom-call(s32[2]{0:T(128)} %pad_add_fusion.place_ref, bf16[2,1024,1152]{2,1,0:T(8,128)(2,1)} %get-tuple-element.208.refs_1_.refs_2_.refs_0_, ...), custom_call_target="tpu_custom_call", output_to_operand_aliasing={{2}: (11, {})} | custom-call | flops 10871635968 | bytes 10871635968 | tf_op jit(solution)/shard_map/pallas_call | solution.py:91
  1131.8 16.3 %collective-permute-done.51.refs_2_ = bf16[2,288,2304]{2,1,0:T(8,128)(2,1)} collective-permute-done((bf16[2,288,2304]{2,1,0:T(8,128)(2,1)}, bf16[2,288,2304]{2,1,0:T(8,128)(2,1)}, u32[]{:S(2)}, u32[]{:S(2)}) %collective-permute-start.51) | collective-permute-done | bytes 2654240 | tf_op jit(solution)/shard_map/ppermute | solution.py:31
  1155.6 34.3 %collective-permute-done.48.refs_2_ = bf16[2,288,1536]{2,1,0:T(8,128)(2,1)} collective-permute-done((bf16[2,288,1536]{2,1,0:T(8,128)(2,1)}, bf16[2,288,1536]{2,1,0:T(8,128)(2,1)}, u32[]{:S(2)}, u32[]{:S(2)}) %collective-permute-start.48) | collective-permute-done | bytes 1769504 | tf_op jit(solution)/shard_map/ppermute | solution.py:31
  1190.4 18.0 %collective-permute-done.45.refs_2_ = bf16[2,288,768]{2,1,0:T(8,128)(2,1)} collective-permute-done((bf16[2,288,768]{2,1,0:T(8,128)(2,1)}, bf16[2,288,768]{2,1,0:T(8,128)(2,1)}, u32[]{:S(2)}, u32[]{:S(2)}) %collective-permute-start.45) | collective-permute-done | bytes 884768 | tf_op jit(solution)/shard_map/ppermute | solution.py:31
  (122 shorter events, 193.1 us)
Async XLA Ops:
  220.5 45.8 %collective-permute-start.8 = (bf16[384,1152]{1,0:T(8,128)(2,1)}, bf16[384,1152]{1,0:T(8,128)(2,1)}, u32[]{:S(2)}, u32[]{:S(2)}) collective-permute-start(bf16[384,1152]{1,0:T(8,128)(2,1)} %get-tuple-element.195), channel_id=1, source_target_pairs={{0,2},{1,3},{2,0},{3,1},{4,6},{5,7},{6,4},{7,5}} | collective-permute-start | bytes 2654216 | tf_op jit(solution)/shard_map/ppermute | solution.py:31
  358.5 329.4 %collective-permute-start.12 = (bf16[2048,1152]{1,0:T(8,128)(2,1)}, bf16[2048,1152]{1,0:T(8,128)(2,1)}, u32[]{:S(2)}, u32[]{:S(2)}) collective-permute-start(bf16[2048,1152]{1,0:T(8,128)(2,1)} %bitcast.11), channel_id=1, source_target_pairs={{0,2},{1,3},{2,0},{3,1},{4,6},{5,7},{6,4},{7,5}} | collective-permute-start | bytes 14155784 | tf_op jit(solution)/shard_map/ppermute | solution.py:31
  359.0 123.4 %collective-permute-start.15 = (bf16[2,288,768]{2,1,0:T(8,128)(2,1)}, bf16[2,288,768]{2,1,0:T(8,128)(2,1)}, u32[]{:S(2)}, u32[]{:S(2)}) collective-permute-start(bf16[2,288,768]{2,1,0:T(8,128)(2,1)} %get-tuple-element.217), channel_id=1, source_target_pairs={{0,2},{1,3},{2,0},{3,1},{4,6},{5,7},{6,4},{7,5}} | collective-permute-start | bytes 2654216 | tf_op jit(solution)/shard_map/ppermute | solution.py:31
  376.5 143.8 %collective-permute-start.14 = (bf16[2,288,1536]{2,1,0:T(8,128)(2,1)}, bf16[2,288,1536]{2,1,0:T(8,128)(2,1)}, u32[]{:S(2)}, u32[]{:S(2)}) collective-permute-start(bf16[2,288,1536]{2,1,0:T(8,128)(2,1)} %get-tuple-element.216), channel_id=1, source_target_pairs={{0,2},{1,3},{2,0},{3,1},{4,6},{5,7},{6,4},{7,5}} | collective-permute-start | bytes 5308424 | tf_op jit(solution)/shard_map/ppermute | solution.py:31
  439.9 312.3 %collective-permute-start.11 = (bf16[2,1024,1152]{2,1,0:T(8,128)(2,1)}, bf16[2,1024,1152]{2,1,0:T(8,128)(2,1)}, u32[]{:S(2)}, u32[]{:S(2)}) collective-permute-start(bf16[2,1024,1152]{2,1,0:T(8,128)(2,1)} %get-tuple-element.208.refs_1_.refs_2_.refs_0_), channel_id=1, source_target_pairs={{0,2},{1,3},{2,0},{3,1},{4,6},{5,7},{6,4},{7,5}} | collective-permute-start | bytes 14155784 | tf_op jit(solution)/shard_map/ppermute | solution.py:31
  441.4 344.0 %collective-permute-start.27 = (bf16[2,288,768]{2,1,0:T(8,128)(2,1)}, bf16[2,288,768]{2,1,0:T(8,128)(2,1)}, u32[]{:S(2)}, u32[]{:S(2)}) collective-permute-start(bf16[2,288,768]{2,1,0:T(8,128)(2,1)} %get-tuple-element.243.refs_6_), channel_id=1, source_target_pairs={{0,2},{1,3},{2,0},{3,1},{4,6},{5,7},{6,4},{7,5}} | collective-permute-start | bytes 2654216 | tf_op jit(solution)/shard_map/ppermute | solution.py:31
  482.4 195.4 %collective-permute-start.13 = (bf16[768,1152]{1,0:T(8,128)(2,1)}, bf16[768,1152]{1,0:T(8,128)(2,1)}, u32[]{:S(2)}, u32[]{:S(2)}) collective-permute-start(bf16[768,1152]{1,0:T(8,128)(2,1)} %get-tuple-element.213), channel_id=1, source_target_pairs={{0,2},{1,3},{2,0},{3,1},{4,6},{5,7},{6,4},{7,5}} | collective-permute-start | bytes 5308424 | tf_op jit(solution)/shard_map/ppermute | solution.py:31
  520.3 266.1 %collective-permute-start.26 = (bf16[2,288,768]{2,1,0:T(8,128)(2,1)}, bf16[2,288,768]{2,1,0:T(8,128)(2,1)}, u32[]{:S(2)}, u32[]{:S(2)}) collective-permute-start(bf16[2,288,768]{2,1,0:T(8,128)(2,1)} %get-tuple-element.243.refs_6_), channel_id=1, source_target_pairs={{0,1},{1,0},{2,3},{3,2},{4,5},{5,4},{6,7},{7,6}} | collective-permute-start | bytes 2654216 | tf_op jit(solution)/shard_map/ppermute | solution.py:31
  785.4 79.3 %collective-permute-start.16 = (bf16[1152,1152]{1,0:T(8,128)(2,1)}, bf16[1152,1152]{1,0:T(8,128)(2,1)}, u32[]{:S(2)}, u32[]{:S(2)}) collective-permute-start(bf16[1152,1152]{1,0:T(8,128)(2,1)} %get-tuple-element.236), channel_id=1, source_target_pairs={{0,1},{1,0},{2,3},{3,2},{4,5},{5,4},{6,7},{7,6}} | collective-permute-start | bytes 7962632 | tf_op jit(solution)/shard_map/ppermute | solution.py:31
  828.3 51.2 %collective-permute-start.40 = (bf16[384,1152]{1,0:T(8,128)(2,1)}, bf16[384,1152]{1,0:T(8,128)(2,1)}, u32[]{:S(2)}, u32[]{:S(2)}) collective-permute-start(bf16[384,1152]{1,0:T(8,128)(2,1)} %collective-permute-done.39.refs_24_), channel_id=1, source_target_pairs={{0,1},{1,0},{2,3},{3,2},{4,5},{5,4},{6,7},{7,6}} | collective-permute-start | bytes 2654216 | tf_op jit(solution)/shard_map/ppermute | solution.py:31
  828.3 51.1 %collective-permute-start.32 = (bf16[2,288,768]{2,1,0:T(8,128)(2,1)}, bf16[2,288,768]{2,1,0:T(8,128)(2,1)}, u32[]{:S(2)}, u32[]{:S(2)}) collective-permute-start(bf16[2,288,768]{2,1,0:T(8,128)(2,1)} %get-tuple-element.245.refs_14_), channel_id=1, source_target_pairs={{0,1},{1,0},{2,3},{3,2},{4,5},{5,4},{6,7},{7,6}} | collective-permute-start | bytes 2654216 | tf_op jit(solution)/shard_map/ppermute | solution.py:31
  945.6 79.3 %collective-permute-start.41 = (bf16[2,288,2304]{2,1,0:T(8,128)(2,1)}, bf16[2,288,2304]{2,1,0:T(8,128)(2,1)}, u32[]{:S(2)}, u32[]{:S(2)}) collective-permute-start(bf16[2,288,2304]{2,1,0:T(8,128)(2,1)} %get-tuple-element.253), channel_id=1, source_target_pairs={{0,1},{1,0},{2,3},{3,2},{4,5},{5,4},{6,7},{7,6}} | collective-permute-start | bytes 7962632 | tf_op jit(solution)/shard_map/ppermute | solution.py:31
  945.7 41.8 %collective-permute-start.24 = (bf16[768,1152]{1,0:T(8,128)(2,1)}, bf16[768,1152]{1,0:T(8,128)(2,1)}, u32[]{:S(2)}, u32[]{:S(2)}) collective-permute-start(bf16[768,1152]{1,0:T(8,128)(2,1)} %get-tuple-element.242.refs_10_), channel_id=1, source_target_pairs={{0,2},{1,3},{2,0},{3,1},{4,6},{5,7},{6,4},{7,5}} | collective-permute-start | bytes 5308424 | tf_op jit(solution)/shard_map/ppermute | solution.py:31
  946.2 78.7 %collective-permute-start.21 = (bf16[2,288,1536]{2,1,0:T(8,128)(2,1)}, bf16[2,288,1536]{2,1,0:T(8,128)(2,1)}, u32[]{:S(2)}, u32[]{:S(2)}) collective-permute-start(bf16[2,288,1536]{2,1,0:T(8,128)(2,1)} %get-tuple-element.241.refs_6_), channel_id=1, source_target_pairs={{0,2},{1,3},{2,0},{3,1},{4,6},{5,7},{6,4},{7,5}} | collective-permute-start | bytes 5308424 | tf_op jit(solution)/shard_map/ppermute | solution.py:31
  947.7 91.1 %collective-permute-start.23 = (bf16[768,1152]{1,0:T(8,128)(2,1)}, bf16[768,1152]{1,0:T(8,128)(2,1)}, u32[]{:S(2)}, u32[]{:S(2)}) collective-permute-start(bf16[768,1152]{1,0:T(8,128)(2,1)} %get-tuple-element.242.refs_10_), channel_id=1, source_target_pairs={{0,1},{1,0},{2,3},{3,2},{4,5},{5,4},{6,7},{7,6}} | collective-permute-start | bytes 5308424 | tf_op jit(solution)/shard_map/ppermute | solution.py:31
  947.7 91.1 %collective-permute-start.20 = (bf16[2,288,1536]{2,1,0:T(8,128)(2,1)}, bf16[2,288,1536]{2,1,0:T(8,128)(2,1)}, u32[]{:S(2)}, u32[]{:S(2)}) collective-permute-start(bf16[2,288,1536]{2,1,0:T(8,128)(2,1)} %get-tuple-element.241.refs_6_), channel_id=1, source_target_pairs={{0,1},{1,0},{2,3},{3,2},{4,5},{5,4},{6,7},{7,6}} | collective-permute-start | bytes 5308424 | tf_op jit(solution)/shard_map/ppermute | solution.py:31
  987.5 51.3 %collective-permute-start.25 = (bf16[768,1152]{1,0:T(8,128)(2,1)}, bf16[768,1152]{1,0:T(8,128)(2,1)}, u32[]{:S(2)}, u32[]{:S(2)}) collective-permute-start(bf16[768,1152]{1,0:T(8,128)(2,1)} %collective-permute-done.24.refs_12_), channel_id=1, source_target_pairs={{0,1},{1,0},{2,3},{3,2},{4,5},{5,4},{6,7},{7,6}} | collective-permute-start | bytes 5308424 | tf_op jit(solution)/shard_map/ppermute | solution.py:31
  1024.9 62.9 %collective-permute-start.18 = (bf16[1152,1152]{1,0:T(8,128)(2,1)}, bf16[1152,1152]{1,0:T(8,128)(2,1)}, u32[]{:S(2)}, u32[]{:S(2)}) collective-permute-start(bf16[1152,1152]{1,0:T(8,128)(2,1)} %get-tuple-element.240.refs_6_), channel_id=1, source_target_pairs={{0,2},{1,3},{2,0},{3,1},{4,6},{5,7},{6,4},{7,5}} | collective-permute-start | bytes 7962632 | tf_op jit(solution)/shard_map/ppermute | solution.py:31
  1088.0 60.1 %collective-permute-start.51 = (bf16[2,288,2304]{2,1,0:T(8,128)(2,1)}, bf16[2,288,2304]{2,1,0:T(8,128)(2,1)}, u32[]{:S(2)}, u32[]{:S(2)}) collective-permute-start(bf16[2,288,2304]{2,1,0:T(8,128)(2,1)} %get-tuple-element.278.refs_0_), channel_id=1, source_target_pairs={{0,2},{1,3},{2,0},{3,1},{4,6},{5,7},{6,4},{7,5}} | collective-permute-start | bytes 7962632 | tf_op jit(solution)/shard_map/ppermute | solution.py:31
  1131.5 58.4 %collective-permute-start.50 = (bf16[2,288,2304]{2,1,0:T(8,128)(2,1)}, bf16[2,288,2304]{2,1,0:T(8,128)(2,1)}, u32[]{:S(2)}, u32[]{:S(2)}) collective-permute-start(bf16[2,288,2304]{2,1,0:T(8,128)(2,1)} %get-tuple-element.278.refs_0_), channel_id=1, source_target_pairs={{0,1},{1,0},{2,3},{3,2},{4,5},{5,4},{6,7},{7,6}} | collective-permute-start | bytes 7962632 | tf_op jit(solution)/shard_map/ppermute | solution.py:31
  1148.1 60.3 %collective-permute-start.52 = (bf16[2,288,2304]{2,1,0:T(8,128)(2,1)}, bf16[2,288,2304]{2,1,0:T(8,128)(2,1)}, u32[]{:S(2)}, u32[]{:S(2)}) collective-permute-start(bf16[2,288,2304]{2,1,0:T(8,128)(2,1)} %collective-permute-done.51.refs_2_), channel_id=1, source_target_pairs={{0,1},{1,0},{2,3},{3,2},{4,5},{5,4},{6,7},{7,6}} | collective-permute-start | bytes 7962632 | tf_op jit(solution)/shard_map/ppermute | solution.py:31
  1148.1 41.8 %collective-permute-start.48 = (bf16[2,288,1536]{2,1,0:T(8,128)(2,1)}, bf16[2,288,1536]{2,1,0:T(8,128)(2,1)}, u32[]{:S(2)}, u32[]{:S(2)}) collective-permute-start(bf16[2,288,1536]{2,1,0:T(8,128)(2,1)} %get-tuple-element.277.refs_0_), channel_id=1, source_target_pairs={{0,2},{1,3},{2,0},{3,1},{4,6},{5,7},{6,4},{7,5}} | collective-permute-start | bytes 5308424 | tf_op jit(solution)/shard_map/ppermute | solution.py:31
  1155.1 53.3 %collective-permute-start.45 = (bf16[2,288,768]{2,1,0:T(8,128)(2,1)}, bf16[2,288,768]{2,1,0:T(8,128)(2,1)}, u32[]{:S(2)}, u32[]{:S(2)}) collective-permute-start(bf16[2,288,768]{2,1,0:T(8,128)(2,1)} %get-tuple-element.276.refs_0_), channel_id=1, source_target_pairs={{0,2},{1,3},{2,0},{3,1},{4,6},{5,7},{6,4},{7,5}} | collective-permute-start | bytes 2654216 | tf_op jit(solution)/shard_map/ppermute | solution.py:31
  1155.6 62.3 %collective-permute-start.47 = (bf16[2,288,1536]{2,1,0:T(8,128)(2,1)}, bf16[2,288,1536]{2,1,0:T(8,128)(2,1)}, u32[]{:S(2)}, u32[]{:S(2)}) collective-permute-start(bf16[2,288,1536]{2,1,0:T(8,128)(2,1)} %get-tuple-element.277.refs_0_), channel_id=1, source_target_pairs={{0,1},{1,0},{2,3},{3,2},{4,5},{5,4},{6,7},{7,6}} | collective-permute-start | bytes 5308424 | tf_op jit(solution)/shard_map/ppermute | solution.py:31
  (33 other events, 614.8 us)

commit v3 on v2

--- a/solution.py
+++ b/solution.py
@@ -131,7 +131,7 @@
 
     def body(place, x, wg, wu, *refs):
         if whole:
-            wd, g_o, u_o, hid_o, aT_o, h_o, a1_o, aT1_o, a_s, hs, acc = refs
+            wd, g_o, u_o, hid_o, aT_o, h_o, a1_o, a_s, hs, acc = refs
         else:
             g_o, u_o, hid_o, aT_o, a_s, hs = refs
         j = pl.program_id(1)
@@ -164,7 +164,7 @@
                     return 0
 
                 lax.fori_loop(0, BM // 256, rows_of, 0)
-                normalise(h_o, a1_o, aT1_o)
+                normalise(h_o, a1_o, None)
 
     wide = pl.BlockSpec((BM, BN), lambda i, j, p: (first + i, tile(j, p)))
     into = pl.BlockSpec((None, D, BN), lambda i, j, p: (0, 0, tile(j, p)))
@@ -180,12 +180,11 @@
     if whole:
         ins += [(w_down, pl.BlockSpec((None, BN, D), lambda i, j, p: (0, tile(j, p), 0)))]
         outs += [(shaped(T, D), plain, None), (shaped(T, D), plain, None)]
-        outs += [(shaped(D, T), pl.BlockSpec((D, BM), lambda i, j, p: (0, i)), None)]
         scratch += [pltpu.VMEM((BM, D), f32)]
     return call(body, place, after, ins, outs, (rows // BM, NF), scratch)
 
 
-def layer1(place, after, span, a1, aT, dy, w_gate, w_up, w_down, held):
+def layer1(place, after, span, a1, dy, w_gate, w_up, w_down, held):
     steps = T // BM
     first, stride, tiles = span
     t = first % NH
@@ -194,7 +193,7 @@
     def at(j):
         return first + stride * j
 
-    def body(place, a1, aT, dy, wg, wu, wd, dgu_o, keep, out, down_keep, down_out, total, leaving, hid, down, down_leaving, sem):
+    def body(place, a1, dy, wg, wu, wd, dgu_o, keep, out, down_keep, down_out, total, leaving, hid, down, down_leaving, sem):
         j, i = pl.program_id(0), pl.program_id(1)
         core = place[1]
 
@@ -230,7 +229,7 @@
                 back = lax.dot_general(dy[r, :], wd[c, :], NT, preferred_element_type=f32).astype(bf16).astype(f32)
                 hid[r, c], dgu_o[0, r, c], dgu_o[1, r, c] = gated(g, u, back)
         for k in range(2):
-            total[k] = added(i == 0, total[k], dot(aT[...], dgu_o[k]))
+            total[k] = added(i == 0, total[k], lax.dot_general(a1[...], dgu_o[k], TN, preferred_element_type=f32))
         down[...] = added(i == 0, down[...], lax.dot_general(hid[...], dy[...], TN, preferred_element_type=f32))
 
         def last():
@@ -255,7 +254,6 @@
         after,
         [
             (a1, plain),
-            (aT, pl.BlockSpec((D, BM), lambda j, i, p: (0, i))),
             (dy, plain),
             (w_gate, into),
             (w_up, into),
@@ -298,11 +296,11 @@
     return [(keep, theirs), (came, theirs)], [(shaped(rows, D), pl.BlockSpec((rows // 2, D), lambda k, p: (k, 0)), None)], job, ()
 
 
-def back1(place, after, dgu, dy, h, w_gate, w_up, jobs=()):
+def back1(place, after, tile, dgu, dy, h, w_gate, w_up):
     WN = 2 * BN
 
     def body(place, dgu, wg, wu, h, dy, o, acc):
-        j = pl.program_id(1)
+        j = pl.program_id(0)
         for r in cuts(BM, RS):
             for which, w in enumerate((wg, wu)):
                 new = lax.dot_general(dgu[which, r, :], w[...], NT, preferred_element_type=f32)
@@ -325,36 +323,29 @@
 
         return last
 
-    into = pl.BlockSpec((None, D, WN), lambda i, j, p: (1, 0, j))
-    plain = pl.BlockSpec((BM, D), lambda i, j, p: (i, 0))
+    into = pl.BlockSpec((None, D, WN), lambda j, p: (1, 0, j))
+    plain = pl.BlockSpec((BM, D), lambda j, p: (tile, 0))
     return call(
         body,
         place,
         after,
-        [(dgu, pl.BlockSpec((2, BM, WN), lambda i, j, p: (0, i, j))), (w_gate, into), (w_up, into), (h, plain), (dy, plain)],
-        [(shaped(T // BM, BM, D), pl.BlockSpec((None, BM, D), lambda i, j, p: (i, 0, 0)), None)],
-        (T // BM, F // WN),
+        [(dgu, pl.BlockSpec((2, BM, WN), lambda j, p: (0, tile, j))), (w_gate, into), (w_up, into), (h, plain), (dy, plain)],
+        [(shaped(BM, D), pl.BlockSpec((BM, D), lambda j, p: (0, 0)), None)],
+        (F // WN,),
         [pltpu.VMEM((2, BM, D), f32)],
-        jobs,
     )
 
 
 def back0(place, after, span, dhs, gate, up, aT, w_down, jobs=()):
     first, _, tiles = span
     steps = TT // BM
-    arrays = []
-    for array, _ in dhs:
-        if not any(array is one for one in arrays):
-            arrays.append(array)
 
     def body(place, *refs):
-        refs, (g_r, u_r, aT, wd, into_own, into_out, dgu, total, dh, sem) = refs[: len(arrays)], refs[len(arrays) :]
+        refs, (g_r, u_r, aT, wd, into_own, into_out, dgu, total, dh, sem) = refs[:steps], refs[steps:]
         j, i = pl.program_id(0), pl.program_id(1)
 
         def copy(k):
-            array, index = dhs[k]
-            source = refs[next(n for n, one in enumerate(arrays) if one is array)]
-            return pltpu.make_async_copy(source.at[index], dh.at[k], sem.at[k])
+            return pltpu.make_async_copy(refs[k], dh.at[k], sem.at[k])
 
         @pl.when((j == 0) & (i == 0))
         def _():
@@ -385,7 +376,7 @@
         body,
         place,
         after,
-        [(array, ANY) for array in arrays]
+        [(one, ANY) for one in dhs]
         + [
             (gate, wide),
             (up, wide),
@@ -433,7 +424,7 @@
         place,
         after,
         [(hidden, pl.BlockSpec((TT, rows), lambda i, p: (0, tile(i, p))))]
-        + [(b, pl.BlockSpec((None, BM, D), lambda i, p, k=k: (k, 0, 0), pipeline_mode=once)) for b, k in dhs],
+        + [(one, pl.BlockSpec((BM, D), lambda i, p: (0, 0), pipeline_mode=once)) for one in dhs],
         [
             (shaped(QF, D, dtype=f32), pl.BlockSpec((rows, D), lambda i, p: (jnp.minimum(i, n - 1), 0)), None),
             (shaped(QF, D), pl.BlockSpec((rows, D), lambda i, p: (jnp.maximum(i - n, 0), 0)), None),
@@ -598,7 +589,7 @@
     x_far = over(x, OVER_X)
 
     weights = (w_gate, w_up, w_down)
-    (gate, up, hid0, aT0, h, a1, aT1), t = forward0(place, None, 0, x, *weights, [None] * 4, True)
+    (gate, up, hid0, aT0, h, a1), t = forward0(place, None, 0, x, *weights, [None] * 4, True)
 
     mv = {"into": (None,) * 4, "down": (None,) * 2}
     ALL, ONE, TWO = (0, 0, 3), (2, 0, 1), (0, 1, 2)
@@ -616,11 +607,11 @@
     dgu = None
     terms, new1 = {}, {}
 
-    SPANS = {"p": (1, 1, 1), "q": (4, 1, 1), "r": (0, 3, 1), "s": (3, 3, 1), "t": (2, 3, 2)}
+    SPANS = {"p": (1, 1, 1), "q": (4, 1, 1), "r": (0, 3, 1), "s": (3, 3, 1), "u": (2, 3, 1), "v": (5, 3, 1)}
 
     def gradients(t, name, held_down):
         nonlocal dgu
-        (dgu, keep, out, *downs), t = layer1(place, t, SPANS[name], a1, aT1, dy, *weights, [dgu, *held_down])
+        (dgu, keep, out, *downs), t = layer1(place, t, SPANS[name], a1, dy, *weights, [dgu, *held_down])
         terms[name] = [keep, over(out, OVER_CORE)]
         return t, downs
 
@@ -657,15 +648,20 @@
     down1, t = adam_down(t, ONE, downs1)
     t = send(t, "s")
     t = adam(t, "r")
-    t, downs2 = gradients(t, "t", downs2)
-    t = send(t, "t", downs2)
-    (dh,), t = back1(place, t, dgu, dy, h, w_gate, w_up)
-    dh_far = over(dh, OVER_X)
+    t, downs2 = gradients(t, "u", downs2)
     t = adam(t, "s")
-    t = adam(t, "t")
-    down2, t = adam_down(t, TWO, downs2)
+    t = send(t, "u")
+    t, downs2 = gradients(t, "v", downs2)
+    t = adam(t, "u")
+    t = send(t, "v", downs2)
+    dhs, dhs_far = [], []
+    for tile in range(T // BM):
+        (dh,), t = back1(place, t, tile, dgu, dy, h, w_gate, w_up)
+        dhs.append(dh)
+        dhs_far.append(over(dh, OVER_X))
+    dhs += dhs_far
+    t = adam(t, "v")
     (gate, up, hid0, aT0), t = forward0(place, t, T // BM, x_far, *weights, [gate, up, hid0, aT0], False)
-    dhs = [(dh, 0), (dh, 1), (dh_far, 0), (dh_far, 1)]
 
     weights_out = {"gate": None, "up": None, "down": None}
 
@@ -677,6 +673,7 @@
 
     (own_d, out_d), t = grad_down(place, t, hid0, dhs)
     came_d = over(out_d, OVER_CORE)
+    down2, t = adam_down(t, TWO, downs2)
     results, t = alone(place, t, (3,), [down(0, ALL, own_d, came_d)])
     down0 = took(results, "down")
 
@@ -686,24 +683,22 @@
     new0 = {}
     spans = {"a": (0, 1, 3), "c": (3, 1, 2), "d": (5, 1, 1)}
     beside = {
-        "a": lambda: [copying((3, 4), 4, first_pieces("p", "q", "r", "s")), copying((3, 4), 1, down_pieces(1, ONE, down1))],
-        "c": lambda: [
-            copying((2, 4), 4, first_pieces("t")),
-            copying((2, 4), 2, [*down_pieces(1, TWO, down2)]),
-        ],
+        "a": lambda: [copying((3, 4), 3, first_pieces("p", "q", "r")), copying((3, 4), 1, down_pieces(1, ONE, down1))],
+        "c": lambda: [copying((2, 4), 4, first_pieces("s", "u", "v")), copying((2, 4), 2, down_pieces(1, TWO, down2))],
         "d": lambda: [copying((1, 4), 4, down_pieces(0, ALL, down0))],
     }
     for name, span in spans.items():
         (own, out, *results), t = back0(place, t, span, dhs, gate, up, aT0, w_down, beside[name]())
-        copied(results, ("gate", "up", "down")[-len(results) :])
+        copied(results, ("gate", "up", "down")[: len(results)] if name != "d" else ("down",))
         came = over(out, OVER_CORE)
         results, t = alone(place, t, (2 * span[2],), [into(0, span, own, came)])
         new0[name] = took(results, "into")
 
     for name, q in (("a", 4), ("c", 8), ("d", 8)):
         grid = (8 // q + 2,)
-        results, t = call(nothing, place, t, [], [], grid, jobs=[copying(grid, q, into_pieces(0, spans[name], new0[name]))])
-        copied(results, ("gate", "up"))
+        jobs = [copying(grid, q, into_pieces(0, spans[name], new0[name]))]
+        results, t = call(nothing, place, t, [], [], grid, jobs=jobs)
+        copied(results, ("gate", "up", "down")[: len(results)])
     held, o_down = (weights_out["gate"], weights_out["up"]), weights_out["down"]
     (m_gate, m_up, v_gate, v_up), (m_down, v_down) = mv["into"], mv["down"]
     return *held, o_down, m_gate, m_up, m_down, v_gate, v_up, v_down

time: 1230 us -> 1100 us (0.89)
  waiting for transfers between devices: 465 us -> 314 us
    ppermute x53 -> x59, waiting for transfers between devices: 465 us -> 314 us  [over(): return lax.ppermute(array, 'dp', pairs)]
    pallas_call x31 -> x35, Pallas kernels: 736 us -> 746 us  [call(): pl.pallas_call(kernel, grid_spec=pltpu.PrefetchScalarGridSpec(num_scalar_...]
    ppermute x53 -> x59, starting transfers between devices: 25.7 us -> 29.9 us  [over(): return lax.ppermute(array, 'dp', pairs)]
  transfers between devices with their start and end apart: 53 -> 59, of which waited for: 19 -> 20; matrix products, arithmetic and copies ran while one was open for 0% -> 0% of each run, Pallas kernels for 37% -> 52%
where the time goes in v3:
time: 1100 us; the launch traced here: 1090 us
  Pallas kernels  746 us (68%)
  waiting for transfers between devices  314 us (29%)
  starting transfers between devices  29.9 us (3%)
    pallas_call x35, Pallas kernels, call(): pl.pallas_call(kernel, grid_spec=pltpu.PrefetchScalarGridSpec(num_scalar_...  746 us
    ppermute x59, waiting for transfers between devices, over(): return lax.ppermute(array, 'dp', pairs)  314 us
    ppermute x59, starting transfers between devices, over(): return lax.ppermute(array, 'dp', pairs)  29.9 us
  transfers between devices with their start and end apart: 59, of which 20 were waited for; matrix products, arithmetic and copies ran while one was open for 0% of the time, Pallas kernels for 52%

profile of v3, /device:TPU:0, one launch (start us, length us, event | category | flops | bytes accessed | tf_op | source)
XLA Modules:
  0.0 1093.4 jit_solution(15425550119999016898)
XLA Ops:
  1.3 92.2 %shard_map.178 = (f32[4096,4608]{1,0:T(8,128)}, f32[4096,4608]{1,0:T(8,128)}, bf16[4096,2304]{1,0:T(8,128)(2,1)}, bf16[1152,4096]{1,0:T(8,128)(2,1)}, bf16[2048,...) custom-call(s32[2]{0:T(128)} %pad_add_fusion.place_ref, bf16[2048,1152]{1,0:T(8,128)(2,1)} %bitcast.12, ...), custom_call_target="tpu_custom_call" | custom-call | flops 10871635968 | bytes 10871635968 | tf_op jit(solution)/shard_map/pallas_call | solution.py:91
  93.5 33.6 %shard_map.179 = (bf16[2,2048,4608]{2,1,0:T(8,128)(2,1)}, f32[2,2,288,768]{3,2,1,0:T(8,128)}, bf16[2,2,288,768]{3,2,1,0:T(8,128)(2,1)}, f32[2,384,1152]{2,1,0:T(...) custom-call(s32[2]{0:T(128)} %pad_add_fusion.place_ref, bf16[2048,1152]{1,0:T(8,128)(2,1)} %get-tuple-element.168.refs_0_, ...), custom_call_target="tpu_custom_call" | custom-call | flops 10871635968 | bytes 10871635968 | tf_op jit(solution)/shard_map/pallas_call | solution.py:91
  137.7 33.8 %shard_map.181 = (bf16[2,2048,4608]{2,1,0:T(8,128)(2,1)}, f32[2,2,288,768]{3,2,1,0:T(8,128)}, bf16[2,2,288,768]{3,2,1,0:T(8,128)(2,1)}, f32[2,384,1152]{2,1,0:T(...) custom-call(s32[2]{0:T(128)} %pad_add_fusion.place_ref, ...), custom_call_target="tpu_custom_call", output_to_operand_aliasing={{0}: (6, {}), {3}: (7, {}), {4}: (8, {})} | custom-call | flops 10871635968 | bytes 10871635968 | tf_op jit(solution)/shard_map/pallas_call | solution.py:91
  182.5 34.0 %shard_map.184 = (bf16[2,2048,4608]{2,1,0:T(8,128)(2,1)}, f32[2,2,288,768]{3,2,1,0:T(8,128)}, bf16[2,2,288,768]{3,2,1,0:T(8,128)(2,1)}, f32[2,768,1152]{2,1,0:T(...) custom-call(s32[2]{0:T(128)} %pad_add_fusion.place_ref, ...), custom_call_target="tpu_custom_call", output_to_operand_aliasing={{0}: (6, {})} | custom-call | flops 10871635968 | bytes 10871635968 | tf_op jit(solution)/shard_map/pallas_call | solution.py:91
  227.5 33.8 %shard_map.187 = (bf16[2,2048,4608]{2,1,0:T(8,128)(2,1)}, f32[2,2,288,768]{3,2,1,0:T(8,128)}, bf16[2,2,288,768]{3,2,1,0:T(8,128)(2,1)}, f32[2,768,1152]{2,1,0:T(...) custom-call(s32[2]{0:T(128)} %pad_add_fusion.place_ref, ...), custom_call_target="tpu_custom_call", output_to_operand_aliasing={{0}: (6, {}), {3}: (7, {}), {4}: (8, {})} | custom-call | flops 10871635968 | bytes 10871635968 | tf_op jit(solution)/shard_map/pallas_call | solution.py:91
  290.0 33.6 %shard_map.191 = (bf16[2,2048,4608]{2,1,0:T(8,128)(2,1)}, f32[2,2,288,768]{3,2,1,0:T(8,128)}, bf16[2,2,288,768]{3,2,1,0:T(8,128)(2,1)}, f32[2,768,1152]{2,1,0:T(...) custom-call(s32[2]{0:T(128)} %pad_add_fusion.place_ref, ...), custom_call_target="tpu_custom_call", output_to_operand_aliasing={{0}: (6, {}), {3}: (7, {}), {4}: (8, {})} | custom-call | flops 10871635968 | bytes 10871635968 | tf_op jit(solution)/shard_map/pallas_call | solution.py:91
  332.7 33.3 %shard_map.194 = (bf16[2,2048,4608]{2,1,0:T(8,128)(2,1)}, f32[2,2,288,768]{3,2,1,0:T(8,128)}, bf16[2,2,288,768]{3,2,1,0:T(8,128)(2,1)}, f32[2,768,1152]{2,1,0:T(...) custom-call(s32[2]{0:T(128)} %pad_add_fusion.place_ref, ...), custom_call_target="tpu_custom_call", output_to_operand_aliasing={{0}: (6, {}), {3}: (7, {}), {4}: (8, {})} | custom-call | flops 10871635968 | bytes 10871635968 | tf_op jit(solution)/shard_map/pallas_call | solution.py:91
  369.1 20.8 %collective-permute-done.13.refs_2_ = bf16[2,288,768]{2,1,0:T(8,128)(2,1)} collective-permute-done((bf16[2,288,768]{2,1,0:T(8,128)(2,1)}, bf16[2,288,768]{2,1,0:T(8,128)(2,1)}, u32[]{:S(2)}, u32[]{:S(2)}) %collective-permute-start.13) | collective-permute-done | bytes 884768 | tf_op jit(solution)/shard_map/ppermute | solution.py:31
  401.1 35.6 %shard_map.197 = (bf16[1024,1152]{1,0:T(8,128)(2,1)}, s32[8,128]{1,0:T(8,128)}) custom-call(s32[2]{0:T(128)} %pad_add_fusion.place_ref, bf16[2,2048,4608]{2,1,0:T(8,128)(2,1)} %get-tuple-element.227.refs_0_, bf16[2,1152,4608]{2,1,0:T(8,128)(2,1)} %refs_2_.27, bf16[2,1152,4608]{2,1,0:T(8,128)(2,1)} %refs_3_.37, ...), custom_call_target="tpu_custom_call" | custom-call | flops 10871635968 | bytes 10871635968 | tf_op jit(solution)/shard_map/pallas_call | solution.py:91
  436.7 36.0 %shard_map.198 = (bf16[1024,1152]{1,0:T(8,128)(2,1)}, s32[8,128]{1,0:T(8,128)}) custom-call(s32[2]{0:T(128)} %pad_add_fusion.place_ref, bf16[2,2048,4608]{2,1,0:T(8,128)(2,1)} %get-tuple-element.227.refs_0_, bf16[2,1152,4608]{2,1,0:T(8,128)(2,1)} %refs_2_.27, bf16[2,1152,4608]{2,1,0:T(8,128)(2,1)} %refs_3_.37, ...), custom_call_target="tpu_custom_call" | custom-call | flops 10871635968 | bytes 10871635968 | tf_op jit(solution)/shard_map/pallas_call | solution.py:91
  476.7 33.3 %collective-permute-done.17.refs_2_ = bf16[2,288,768]{2,1,0:T(8,128)(2,1)} collective-permute-done((bf16[2,288,768]{2,1,0:T(8,128)(2,1)}, bf16[2,288,768]{2,1,0:T(8,128)(2,1)}, u32[]{:S(2)}, u32[]{:S(2)}) %collective-permute-start.17) | collective-permute-done | bytes 884768 | tf_op jit(solution)/shard_map/ppermute | solution.py:31
  515.8 64.2 %shard_map.200 = (f32[4096,4608]{1,0:T(8,128)}, f32[4096,4608]{1,0:T(8,128)}, bf16[4096,2304]{1,0:T(8,128)(2,1)}, bf16[1152,4096]{1,0:T(8,128)(2,1)}, s32[8,128]{1,0:T(8,128)}) custom-call(s32[2]{0:T(128)} %pad_add_fusion.place_ref, ...), custom_call_target="tpu_custom_call", output_to_operand_aliasing={{0}: (4, {}), {1}: (5, {}), {2}: (6, {}), {3}: (7, {})} | custom-call | flops 10871635968 | bytes 10871635968 | tf_op jit(solution)/shard_map/pallas_call | solution.py:91
  580.0 31.1 %collective-permute-done.14.refs_3_.refs_2_ = bf16[1024,1152]{1,0:T(8,128)(2,1)} collective-permute-done((bf16[1024,1152]{1,0:T(8,128)(2,1)}, bf16[1024,1152]{1,0:T(8,128)(2,1)}, u32[]{:S(2)}, u32[]{:S(2)}) %collective-permute-start.14) | collective-permute-done | bytes 2359328 | tf_op jit(solution)/shard_map/ppermute | solution.py:31
  611.1 33.4 %shard_map.201 = (f32[1152,1152]{1,0:T(8,128)}, bf16[1152,1152]{1,0:T(8,128)(2,1)}, s32[8,128]{1,0:T(8,128)}) custom-call(s32[2]{0:T(128)} %pad_add_fusion.place_ref, bf16[4096,2304]{1,0:T(8,128)(2,1)} %get-tuple-element.258.refs_0_, bf16[1024,1152]{1,0:T(8,128)(2,1)} %get-tuple-element.241.refs_1_.refs_0_, ...), custom_call_target="tpu_custom_call" | custom-call | flops 10871635968 | bytes 10871635968 | tf_op jit(solution)/shard_map/pallas_call | solution.py:91
  687.4 18.4 %collective-permute-done.45.refs_22_ = bf16[384,1152]{1,0:T(8,128)(2,1)} collective-permute-done((bf16[384,1152]{1,0:T(8,128)(2,1)}, bf16[384,1152]{1,0:T(8,128)(2,1)}, u32[]{:S(2)}, u32[]{:S(2)}) %collective-permute-start.45) | collective-permute-done | bytes 884768 | tf_op jit(solution)/shard_map/ppermute | solution.py:31
  705.9 18.0 %collective-permute-done.42.refs_18_ = bf16[2,288,768]{2,1,0:T(8,128)(2,1)} collective-permute-done((bf16[2,288,768]{2,1,0:T(8,128)(2,1)}, bf16[2,288,768]{2,1,0:T(8,128)(2,1)}, u32[]{:S(2)}, u32[]{:S(2)}) %collective-permute-start.42) | collective-permute-done | bytes 884768 | tf_op jit(solution)/shard_map/ppermute | solution.py:31
  739.0 64.9 %shard_map.204 = (f32[2,288,2304]{2,1,0:T(8,128)}, bf16[2,288,2304]{2,1,0:T(8,128)(2,1)}, bf16[2,1152,4608]{2,1,0:T(8,128)(2,1)}, bf16[2,1152,4608]{2,1,0:T(8,12...) custom-call(s32[2]{0:T(128)} %pad_add_fusion.place_ref, ...), custom_call_target="tpu_custom_call" | custom-call | flops 10871635968 | bytes 10871635968 | tf_op jit(solution)/shard_map/pallas_call | solution.py:91
  810.6 53.5 %collective-permute-done.27.refs_14_ = bf16[2,288,768]{2,1,0:T(8,128)(2,1)S(1)} collective-permute-done((bf16[2,288,768]{2,1,0:T(8,128)(2,1)}, bf16[2,288,768]{2,1,0:T(8,128)(2,1)S(1)}, u32[]{:S(2)}, u32[]{:S(2)}) %collective-permute-start.27) | collective-permute-done | bytes 884768 | tf_op jit(solution)/shard_map/ppermute | solution.py:31
  869.3 18.7 %collective-permute-done.30.refs_18_ = bf16[2,288,768]{2,1,0:T(8,128)(2,1)} collective-permute-done((bf16[2,288,768]{2,1,0:T(8,128)(2,1)}, bf16[2,288,768]{2,1,0:T(8,128)(2,1)}, u32[]{:S(2)}, u32[]{:S(2)}) %collective-permute-start.30) | collective-permute-done | bytes 884768 | tf_op jit(solution)/shard_map/ppermute | solution.py:31
  901.9 48.7 %shard_map.206 = (f32[2,288,1536]{2,1,0:T(8,128)}, bf16[2,288,1536]{2,1,0:T(8,128)(2,1)}, bf16[2,1152,4608]{2,1,0:T(8,128)(2,1)}, bf16[2,1152,4608]{2,1,0:T(8,12...) custom-call(s32[2]{0:T(128)} %pad_add_fusion.place_ref, ...), custom_call_target="tpu_custom_call", output_to_operand_aliasing={{2}: (25, {}), {3}: (26, {}), {4}: (27, {})} | custom-call | flops 10871635968 | bytes 10871635968 | tf_op jit(solution)/shard_map/pallas_call | solution.py:91
  964.3 30.5 %shard_map.208 = (f32[2,288,768]{2,1,0:T(8,128)}, bf16[2,288,768]{2,1,0:T(8,128)(2,1)}, bf16[2,4608,1152]{2,1,0:T(8,128)(2,1)}, s32[8,128]{1,0:T(8,128)}) custom-call(s32[2]{0:T(128)} %pad_add_fusion.place_ref, bf16[1024,1152]{1,0:T(8,128)(2,1)} %get-tuple-element.241.refs_1_.refs_0_, ...), custom_call_target="tpu_custom_call", output_to_operand_aliasing={{2}: (13, {})} | custom-call | flops 10871635968 | bytes 10871635968 | tf_op jit(solution)/shard_map/pallas_call | solution.py:91
  995.3 16.3 %collective-permute-done.57.refs_2_ = bf16[2,288,2304]{2,1,0:T(8,128)(2,1)} collective-permute-done((bf16[2,288,2304]{2,1,0:T(8,128)(2,1)}, bf16[2,288,2304]{2,1,0:T(8,128)(2,1)}, u32[]{:S(2)}, u32[]{:S(2)}) %collective-permute-start.57) | collective-permute-done | bytes 2654240 | tf_op jit(solution)/shard_map/ppermute | solution.py:31
  1019.1 34.2 %collective-permute-done.54.refs_2_ = bf16[2,288,1536]{2,1,0:T(8,128)(2,1)} collective-permute-done((bf16[2,288,1536]{2,1,0:T(8,128)(2,1)}, bf16[2,288,1536]{2,1,0:T(8,128)(2,1)}, u32[]{:S(2)}, u32[]{:S(2)}) %collective-permute-start.54) | collective-permute-done | bytes 1769504 | tf_op jit(solution)/shard_map/ppermute | solution.py:31
  1053.8 18.0 %collective-permute-done.51.refs_2_ = bf16[2,288,768]{2,1,0:T(8,128)(2,1)} collective-permute-done((bf16[2,288,768]{2,1,0:T(8,128)(2,1)}, bf16[2,288,768]{2,1,0:T(8,128)(2,1)}, u32[]{:S(2)}, u32[]{:S(2)}) %collective-permute-start.51) | collective-permute-done | bytes 884768 | tf_op jit(solution)/shard_map/ppermute | solution.py:31
  (138 shorter events, 222.3 us)
Async XLA Ops:
  271.8 51.8 %collective-permute-start.10 = (bf16[2,288,768]{2,1,0:T(8,128)(2,1)}, bf16[2,288,768]{2,1,0:T(8,128)(2,1)}, u32[]{:S(2)}, u32[]{:S(2)}) collective-permute-start(bf16[2,288,768]{2,1,0:T(8,128)(2,1)} %get-tuple-element.219), channel_id=1, source_target_pairs={{0,2},{1,3},{2,0},{3,1},{4,6},{5,7},{6,4},{7,5}} | collective-permute-start | bytes 2654216 | tf_op jit(solution)/shard_map/ppermute | solution.py:31
  367.1 148.7 %collective-permute-start.16 = (bf16[2048,1152]{1,0:T(8,128)(2,1)}, bf16[2048,1152]{1,0:T(8,128)(2,1)}, u32[]{:S(2)}, u32[]{:S(2)}) collective-permute-start(bf16[2048,1152]{1,0:T(8,128)(2,1)} %bitcast.13), channel_id=1, source_target_pairs={{0,2},{1,3},{2,0},{3,1},{4,6},{5,7},{6,4},{7,5}} | collective-permute-start | bytes 14155784 | tf_op jit(solution)/shard_map/ppermute | solution.py:31
  401.1 108.9 %collective-permute-start.17 = (bf16[2,288,768]{2,1,0:T(8,128)(2,1)}, bf16[2,288,768]{2,1,0:T(8,128)(2,1)}, u32[]{:S(2)}, u32[]{:S(2)}) collective-permute-start(bf16[2,288,768]{2,1,0:T(8,128)(2,1)} %get-tuple-element.248), channel_id=1, source_target_pairs={{0,2},{1,3},{2,0},{3,1},{4,6},{5,7},{6,4},{7,5}} | collective-permute-start | bytes 2654216 | tf_op jit(solution)/shard_map/ppermute | solution.py:31
  472.6 107.4 %collective-permute-start.15 = (bf16[1024,1152]{1,0:T(8,128)(2,1)}, bf16[1024,1152]{1,0:T(8,128)(2,1)}, u32[]{:S(2)}, u32[]{:S(2)}) collective-permute-start(bf16[1024,1152]{1,0:T(8,128)(2,1)} %get-tuple-element.243.refs_2_.refs_1_), channel_id=1, source_target_pairs={{0,2},{1,3},{2,0},{3,1},{4,6},{5,7},{6,4},{7,5}} | collective-permute-start | bytes 7077896 | tf_op jit(solution)/shard_map/ppermute | solution.py:31
  474.6 136.4 %collective-permute-start.14 = (bf16[1024,1152]{1,0:T(8,128)(2,1)}, bf16[1024,1152]{1,0:T(8,128)(2,1)}, u32[]{:S(2)}, u32[]{:S(2)}) collective-permute-start(bf16[1024,1152]{1,0:T(8,128)(2,1)} %get-tuple-element.241.refs_1_.refs_0_), channel_id=1, source_target_pairs={{0,2},{1,3},{2,0},{3,1},{4,6},{5,7},{6,4},{7,5}} | collective-permute-start | bytes 7077896 | tf_op jit(solution)/shard_map/ppermute | solution.py:31
  474.7 170.3 %collective-permute-start.36 = (bf16[2,288,768]{2,1,0:T(8,128)(2,1)}, bf16[2,288,768]{2,1,0:T(8,128)(2,1)}, u32[]{:S(2)}, u32[]{:S(2)}) collective-permute-start(bf16[2,288,768]{2,1,0:T(8,128)(2,1)} %get-tuple-element.274.refs_8_), channel_id=1, source_target_pairs={{0,2},{1,3},{2,0},{3,1},{4,6},{5,7},{6,4},{7,5}} | collective-permute-start | bytes 2654216 | tf_op jit(solution)/shard_map/ppermute | solution.py:31
  510.0 158.0 %collective-permute-start.19 = (bf16[768,1152]{1,0:T(8,128)(2,1)}, bf16[768,1152]{1,0:T(8,128)(2,1)}, u32[]{:S(2)}, u32[]{:S(2)}) collective-permute-start(bf16[768,1152]{1,0:T(8,128)(2,1)} %get-tuple-element.262), channel_id=1, source_target_pairs={{0,2},{1,3},{2,0},{3,1},{4,6},{5,7},{6,4},{7,5}} | collective-permute-start | bytes 5308424 | tf_op jit(solution)/shard_map/ppermute | solution.py:31
  644.5 79.4 %collective-permute-start.18 = (bf16[1152,1152]{1,0:T(8,128)(2,1)}, bf16[1152,1152]{1,0:T(8,128)(2,1)}, u32[]{:S(2)}, u32[]{:S(2)}) collective-permute-start(bf16[1152,1152]{1,0:T(8,128)(2,1)} %get-tuple-element.261), channel_id=1, source_target_pairs={{0,1},{1,0},{2,3},{3,2},{4,5},{5,4},{6,7},{7,6}} | collective-permute-start | bytes 7962632 | tf_op jit(solution)/shard_map/ppermute | solution.py:31
  652.3 53.6 %collective-permute-start.45 = (bf16[384,1152]{1,0:T(8,128)(2,1)}, bf16[384,1152]{1,0:T(8,128)(2,1)}, u32[]{:S(2)}, u32[]{:S(2)}) collective-permute-start(bf16[384,1152]{1,0:T(8,128)(2,1)} %get-tuple-element.277.refs_20_), channel_id=1, source_target_pairs={{0,2},{1,3},{2,0},{3,1},{4,6},{5,7},{6,4},{7,5}} | collective-permute-start | bytes 2654216 | tf_op jit(solution)/shard_map/ppermute | solution.py:31
  668.0 55.9 %collective-permute-start.42 = (bf16[2,288,768]{2,1,0:T(8,128)(2,1)}, bf16[2,288,768]{2,1,0:T(8,128)(2,1)}, u32[]{:S(2)}, u32[]{:S(2)}) collective-permute-start(bf16[2,288,768]{2,1,0:T(8,128)(2,1)} %get-tuple-element.276.refs_16_), channel_id=1, source_target_pairs={{0,2},{1,3},{2,0},{3,1},{4,6},{5,7},{6,4},{7,5}} | collective-permute-start | bytes 2654216 | tf_op jit(solution)/shard_map/ppermute | solution.py:31
  686.9 51.8 %collective-permute-start.44 = (bf16[384,1152]{1,0:T(8,128)(2,1)}, bf16[384,1152]{1,0:T(8,128)(2,1)}, u32[]{:S(2)}, u32[]{:S(2)}) collective-permute-start(bf16[384,1152]{1,0:T(8,128)(2,1)} %get-tuple-element.277.refs_20_), channel_id=1, source_target_pairs={{0,1},{1,0},{2,3},{3,2},{4,5},{5,4},{6,7},{7,6}} | collective-permute-start | bytes 2654216 | tf_op jit(solution)/shard_map/ppermute | solution.py:31
  686.9 52.1 %collective-permute-start.40 = (bf16[2,288,768]{2,1,0:T(8,128)(2,1)}, bf16[2,288,768]{2,1,0:T(8,128)(2,1)}, u32[]{:S(2)}, u32[]{:S(2)}) collective-permute-start(bf16[2,288,768]{2,1,0:T(8,128)(2,1)} %collective-permute-done.39.refs_14_), channel_id=1, source_target_pairs={{0,1},{1,0},{2,3},{3,2},{4,5},{5,4},{6,7},{7,6}} | collective-permute-start | bytes 2654216 | tf_op jit(solution)/shard_map/ppermute | solution.py:31
  738.7 67.8 %collective-permute-start.24 = (bf16[2,288,768]{2,1,0:T(8,128)(2,1)}, bf16[2,288,768]{2,1,0:T(8,128)(2,1)}, u32[]{:S(2)}, u32[]{:S(2)}) collective-permute-start(bf16[2,288,768]{2,1,0:T(8,128)(2,1)} %get-tuple-element.270.refs_8_), channel_id=1, source_target_pairs={{0,2},{1,3},{2,0},{3,1},{4,6},{5,7},{6,4},{7,5}} | collective-permute-start | bytes 2654216 | tf_op jit(solution)/shard_map/ppermute | solution.py:31
  803.9 84.1 %collective-permute-start.47 = (bf16[2,288,2304]{2,1,0:T(8,128)(2,1)}, bf16[2,288,2304]{2,1,0:T(8,128)(2,1)}, u32[]{:S(2)}, u32[]{:S(2)}) collective-permute-start(bf16[2,288,2304]{2,1,0:T(8,128)(2,1)} %get-tuple-element.283), channel_id=1, source_target_pairs={{0,1},{1,0},{2,3},{3,2},{4,5},{5,4},{6,7},{7,6}} | collective-permute-start | bytes 7962632 | tf_op jit(solution)/shard_map/ppermute | solution.py:31
  804.4 62.7 %collective-permute-start.33 = (bf16[768,1152]{1,0:T(8,128)(2,1)}, bf16[768,1152]{1,0:T(8,128)(2,1)}, u32[]{:S(2)}, u32[]{:S(2)}) collective-permute-start(bf16[768,1152]{1,0:T(8,128)(2,1)} %get-tuple-element.273.refs_20_), channel_id=1, source_target_pairs={{0,2},{1,3},{2,0},{3,1},{4,6},{5,7},{6,4},{7,5}} | collective-permute-start | bytes 5308424 | tf_op jit(solution)/shard_map/ppermute | solution.py:31
  806.2 58.0 %collective-permute-start.27 = (bf16[2,288,768]{2,1,0:T(8,128)(2,1)}, bf16[2,288,768]{2,1,0:T(8,128)(2,1)S(1)}, u32[]{:S(2)}, u32[]{:S(2)}) collective-permute-start(bf16[2,288,768]{2,1,0:T(8,128)(2,1)} %get-tuple-element.271.refs_12_), channel_id=1, source_target_pairs={{0,2},{1,3},{2,0},{3,1},{4,6},{5,7},{6,4},{7,5}} | collective-permute-start | bytes 2654216 | tf_op jit(solution)/shard_map/ppermute | solution.py:31
  806.5 58.7 %collective-permute-start.25 = (bf16[2,288,768]{2,1,0:T(8,128)(2,1)}, bf16[2,288,768]{2,1,0:T(8,128)(2,1)S(1)}, u32[]{:S(2)}, u32[]{:S(2)}) collective-permute-start(bf16[2,288,768]{2,1,0:T(8,128)(2,1)} %collective-permute-done.24.refs_10_), channel_id=1, source_target_pairs={{0,1},{1,0},{2,3},{3,2},{4,5},{5,4},{6,7},{7,6}} | collective-permute-start | bytes 2654216 | tf_op jit(solution)/shard_map/ppermute | solution.py:31
  810.5 56.4 %collective-permute-start.26 = (bf16[2,288,768]{2,1,0:T(8,128)(2,1)}, bf16[2,288,768]{2,1,0:T(8,128)(2,1)S(1)}, u32[]{:S(2)}, u32[]{:S(2)}) collective-permute-start(bf16[2,288,768]{2,1,0:T(8,128)(2,1)} %get-tuple-element.271.refs_12_), channel_id=1, source_target_pairs={{0,1},{1,0},{2,3},{3,2},{4,5},{5,4},{6,7},{7,6}} | collective-permute-start | bytes 2654216 | tf_op jit(solution)/shard_map/ppermute | solution.py:31
  867.9 83.3 %collective-permute-start.21 = (bf16[1152,1152]{1,0:T(8,128)(2,1)}, bf16[1152,1152]{1,0:T(8,128)(2,1)}, u32[]{:S(2)}, u32[]{:S(2)}) collective-permute-start(bf16[1152,1152]{1,0:T(8,128)(2,1)} %get-tuple-element.269.refs_8_), channel_id=1, source_target_pairs={{0,2},{1,3},{2,0},{3,1},{4,6},{5,7},{6,4},{7,5}} | collective-permute-start | bytes 7962632 | tf_op jit(solution)/shard_map/ppermute | solution.py:31
  951.3 60.3 %collective-permute-start.57 = (bf16[2,288,2304]{2,1,0:T(8,128)(2,1)}, bf16[2,288,2304]{2,1,0:T(8,128)(2,1)}, u32[]{:S(2)}, u32[]{:S(2)}) collective-permute-start(bf16[2,288,2304]{2,1,0:T(8,128)(2,1)} %get-tuple-element.308.refs_0_), channel_id=1, source_target_pairs={{0,2},{1,3},{2,0},{3,1},{4,6},{5,7},{6,4},{7,5}} | collective-permute-start | bytes 7962632 | tf_op jit(solution)/shard_map/ppermute | solution.py:31
  994.9 58.4 %collective-permute-start.56 = (bf16[2,288,2304]{2,1,0:T(8,128)(2,1)}, bf16[2,288,2304]{2,1,0:T(8,128)(2,1)}, u32[]{:S(2)}, u32[]{:S(2)}) collective-permute-start(bf16[2,288,2304]{2,1,0:T(8,128)(2,1)} %get-tuple-element.308.refs_0_), channel_id=1, source_target_pairs={{0,1},{1,0},{2,3},{3,2},{4,5},{5,4},{6,7},{7,6}} | collective-permute-start | bytes 7962632 | tf_op jit(solution)/shard_map/ppermute | solution.py:31
  1011.5 60.3 %collective-permute-start.58 = (bf16[2,288,2304]{2,1,0:T(8,128)(2,1)}, bf16[2,288,2304]{2,1,0:T(8,128)(2,1)}, u32[]{:S(2)}, u32[]{:S(2)}) collective-permute-start(bf16[2,288,2304]{2,1,0:T(8,128)(2,1)} %collective-permute-done.57.refs_2_), channel_id=1, source_target_pairs={{0,1},{1,0},{2,3},{3,2},{4,5},{5,4},{6,7},{7,6}} | collective-permute-start | bytes 7962632 | tf_op jit(solution)/shard_map/ppermute | solution.py:31
  1018.8 53.0 %collective-permute-start.51 = (bf16[2,288,768]{2,1,0:T(8,128)(2,1)}, bf16[2,288,768]{2,1,0:T(8,128)(2,1)}, u32[]{:S(2)}, u32[]{:S(2)}) collective-permute-start(bf16[2,288,768]{2,1,0:T(8,128)(2,1)} %get-tuple-element.306.refs_0_), channel_id=1, source_target_pairs={{0,2},{1,3},{2,0},{3,1},{4,6},{5,7},{6,4},{7,5}} | collective-permute-start | bytes 2654216 | tf_op jit(solution)/shard_map/ppermute | solution.py:31
  1019.1 62.3 %collective-permute-start.53 = (bf16[2,288,1536]{2,1,0:T(8,128)(2,1)}, bf16[2,288,1536]{2,1,0:T(8,128)(2,1)}, u32[]{:S(2)}, u32[]{:S(2)}) collective-permute-start(bf16[2,288,1536]{2,1,0:T(8,128)(2,1)} %get-tuple-element.307.refs_0_), channel_id=1, source_target_pairs={{0,1},{1,0},{2,3},{3,2},{4,5},{5,4},{6,7},{7,6}} | collective-permute-start | bytes 5308424 | tf_op jit(solution)/shard_map/ppermute | solution.py:31
  (39 other events, 722.8 us)

commit v4 on v3

--- a/solution.py
+++ b/solution.py
@@ -109,15 +109,12 @@
     return jax.ShapeDtypeStruct(shape, dtype)
 
 
-def normalise(h, a_s, aT):
+def normalise(h, a):
     def rows_of(i, _):
         rows = pl.ds(pl.multiple_of(i * 256, 256), 256)
         wide = h[rows, :].astype(f32)
         scale = lax.rsqrt(jnp.mean(wide * wide, -1, keepdims=True) + 1e-6)
-        a = (wide * scale).astype(bf16)
-        a_s[rows, :] = a
-        if aT is not None:
-            aT[:, rows] = a.T
+        a[rows, :] = (wide * scale).astype(bf16)
         return 0
 
     lax.fori_loop(0, h.shape[0] // 256, rows_of, 0)
@@ -138,8 +135,10 @@
 
         @pl.when(j == 0)
         def _():
-            normalise(x, a_s, aT_o)
-
+            normalise(x, a_s)
+
+        part = pl.ds(pl.multiple_of(jnp.minimum(j * 256, BM - 256), 256), 256)
+        aT_o[:, part] = a_s[part, :].T
         for r in cuts(BM, RS):
             a = a_s[r, :]
             for c in cuts(BN, CS):
@@ -164,7 +163,7 @@
                     return 0
 
                 lax.fori_loop(0, BM // 256, rows_of, 0)
-                normalise(h_o, a1_o, None)
+                normalise(h_o, a1_o)
 
     wide = pl.BlockSpec((BM, BN), lambda i, j, p: (first + i, tile(j, p)))
     into = pl.BlockSpec((None, D, BN), lambda i, j, p: (0, 0, tile(j, p)))
@@ -681,20 +680,20 @@
         return [piece for name in names for piece in into_pieces(1, SPANS[name], new1[name])]
 
     new0 = {}
-    spans = {"a": (0, 1, 3), "c": (3, 1, 2), "d": (5, 1, 1)}
+    spans = {"a": (0, 1, 3), "c": (3, 1, 2), "e": (5, 1, 1)}
     beside = {
         "a": lambda: [copying((3, 4), 3, first_pieces("p", "q", "r")), copying((3, 4), 1, down_pieces(1, ONE, down1))],
         "c": lambda: [copying((2, 4), 4, first_pieces("s", "u", "v")), copying((2, 4), 2, down_pieces(1, TWO, down2))],
-        "d": lambda: [copying((1, 4), 4, down_pieces(0, ALL, down0))],
+        "e": lambda: [copying((1, 4), 4, down_pieces(0, ALL, down0))],
     }
     for name, span in spans.items():
         (own, out, *results), t = back0(place, t, span, dhs, gate, up, aT0, w_down, beside[name]())
-        copied(results, ("gate", "up", "down")[: len(results)] if name != "d" else ("down",))
+        copied(results, ("gate", "up", "down")[: len(results)] if name != "e" else ("down",))
         came = over(out, OVER_CORE)
         results, t = alone(place, t, (2 * span[2],), [into(0, span, own, came)])
         new0[name] = took(results, "into")
 
-    for name, q in (("a", 4), ("c", 8), ("d", 8)):
+    for name, q in (("a", 4), ("c", 8), ("e", 8)):
         grid = (8 // q + 2,)
         jobs = [copying(grid, q, into_pieces(0, spans[name], new0[name]))]
         results, t = call(nothing, place, t, [], [], grid, jobs=jobs)

time: 1100 us -> 1100 us (level)
  no operation moved by 1% of the time
where the time goes in v4:
time: 1100 us; the launch traced here: 1090 us
  Pallas kernels  743 us (68%)
  waiting for transfers between devices  316 us (29%)
  starting transfers between devices  29.9 us (3%)
    pallas_call x35, Pallas kernels, call(): pl.pallas_call(kernel, grid_spec=pltpu.PrefetchScalarGridSpec(num_scalar_...  743 us
    ppermute x59, waiting for transfers between devices, over(): return lax.ppermute(array, 'dp', pairs)  316 us
    ppermute x59, starting transfers between devices, over(): return lax.ppermute(array, 'dp', pairs)  29.9 us
  transfers between devices with their start and end apart: 59, of which 20 were waited for; matrix products, arithmetic and copies ran while one was open for 0% of the time, Pallas kernels for 52%

profile of v4, /device:TPU:0, one launch (start us, length us, event | category | flops | bytes accessed | tf_op | source)
XLA Modules:
  0.0 1092.2 jit_solution(4486477337256433940)
XLA Ops:
  1.3 91.1 %shard_map.178 = (f32[4096,4608]{1,0:T(8,128)}, f32[4096,4608]{1,0:T(8,128)}, bf16[4096,2304]{1,0:T(8,128)(2,1)}, bf16[1152,4096]{1,0:T(8,128)(2,1)}, bf16[2048,...) custom-call(s32[2]{0:T(128)} %pad_add_fusion.place_ref, bf16[2048,1152]{1,0:T(8,128)(2,1)} %bitcast.12, ...), custom_call_target="tpu_custom_call" | custom-call | flops 10871635968 | bytes 10871635968 | tf_op jit(solution)/shard_map/pallas_call | solution.py:91
  92.4 33.6 %shard_map.179 = (bf16[2,2048,4608]{2,1,0:T(8,128)(2,1)}, f32[2,2,288,768]{3,2,1,0:T(8,128)}, bf16[2,2,288,768]{3,2,1,0:T(8,128)(2,1)}, f32[2,384,1152]{2,1,0:T(...) custom-call(s32[2]{0:T(128)} %pad_add_fusion.place_ref, bf16[2048,1152]{1,0:T(8,128)(2,1)} %get-tuple-element.168.refs_0_, ...), custom_call_target="tpu_custom_call" | custom-call | flops 10871635968 | bytes 10871635968 | tf_op jit(solution)/shard_map/pallas_call | solution.py:91
  136.5 33.8 %shard_map.181 = (bf16[2,2048,4608]{2,1,0:T(8,128)(2,1)}, f32[2,2,288,768]{3,2,1,0:T(8,128)}, bf16[2,2,288,768]{3,2,1,0:T(8,128)(2,1)}, f32[2,384,1152]{2,1,0:T(...) custom-call(s32[2]{0:T(128)} %pad_add_fusion.place_ref, ...), custom_call_target="tpu_custom_call", output_to_operand_aliasing={{0}: (6, {}), {3}: (7, {}), {4}: (8, {})} | custom-call | flops 10871635968 | bytes 10871635968 | tf_op jit(solution)/shard_map/pallas_call | solution.py:91
  181.3 34.0 %shard_map.184 = (bf16[2,2048,4608]{2,1,0:T(8,128)(2,1)}, f32[2,2,288,768]{3,2,1,0:T(8,128)}, bf16[2,2,288,768]{3,2,1,0:T(8,128)(2,1)}, f32[2,768,1152]{2,1,0:T(...) custom-call(s32[2]{0:T(128)} %pad_add_fusion.place_ref, ...), custom_call_target="tpu_custom_call", output_to_operand_aliasing={{0}: (6, {})} | custom-call | flops 10871635968 | bytes 10871635968 | tf_op jit(solution)/shard_map/pallas_call | solution.py:91
  226.4 33.8 %shard_map.187 = (bf16[2,2048,4608]{2,1,0:T(8,128)(2,1)}, f32[2,2,288,768]{3,2,1,0:T(8,128)}, bf16[2,2,288,768]{3,2,1,0:T(8,128)(2,1)}, f32[2,768,1152]{2,1,0:T(...) custom-call(s32[2]{0:T(128)} %pad_add_fusion.place_ref, ...), custom_call_target="tpu_custom_call", output_to_operand_aliasing={{0}: (6, {}), {3}: (7, {}), {4}: (8, {})} | custom-call | flops 10871635968 | bytes 10871635968 | tf_op jit(solution)/shard_map/pallas_call | solution.py:91
  288.9 33.6 %shard_map.191 = (bf16[2,2048,4608]{2,1,0:T(8,128)(2,1)}, f32[2,2,288,768]{3,2,1,0:T(8,128)}, bf16[2,2,288,768]{3,2,1,0:T(8,128)(2,1)}, f32[2,768,1152]{2,1,0:T(...) custom-call(s32[2]{0:T(128)} %pad_add_fusion.place_ref, ...), custom_call_target="tpu_custom_call", output_to_operand_aliasing={{0}: (6, {}), {3}: (7, {}), {4}: (8, {})} | custom-call | flops 10871635968 | bytes 10871635968 | tf_op jit(solution)/shard_map/pallas_call | solution.py:91
  331.5 33.3 %shard_map.194 = (bf16[2,2048,4608]{2,1,0:T(8,128)(2,1)}, f32[2,2,288,768]{3,2,1,0:T(8,128)}, bf16[2,2,288,768]{3,2,1,0:T(8,128)(2,1)}, f32[2,768,1152]{2,1,0:T(...) custom-call(s32[2]{0:T(128)} %pad_add_fusion.place_ref, ...), custom_call_target="tpu_custom_call", output_to_operand_aliasing={{0}: (6, {}), {3}: (7, {}), {4}: (8, {})} | custom-call | flops 10871635968 | bytes 10871635968 | tf_op jit(solution)/shard_map/pallas_call | solution.py:91
  367.9 20.8 %collective-permute-done.13.refs_2_ = bf16[2,288,768]{2,1,0:T(8,128)(2,1)} collective-permute-done((bf16[2,288,768]{2,1,0:T(8,128)(2,1)}, bf16[2,288,768]{2,1,0:T(8,128)(2,1)}, u32[]{:S(2)}, u32[]{:S(2)}) %collective-permute-start.13) | collective-permute-done | bytes 884768 | tf_op jit(solution)/shard_map/ppermute | solution.py:31
  399.9 35.6 %shard_map.197 = (bf16[1024,1152]{1,0:T(8,128)(2,1)}, s32[8,128]{1,0:T(8,128)}) custom-call(s32[2]{0:T(128)} %pad_add_fusion.place_ref, bf16[2,2048,4608]{2,1,0:T(8,128)(2,1)} %get-tuple-element.227.refs_0_, bf16[2,1152,4608]{2,1,0:T(8,128)(2,1)} %refs_2_.27, bf16[2,1152,4608]{2,1,0:T(8,128)(2,1)} %refs_3_.37, ...), custom_call_target="tpu_custom_call" | custom-call | flops 10871635968 | bytes 10871635968 | tf_op jit(solution)/shard_map/pallas_call | solution.py:91
  435.5 36.0 %shard_map.198 = (bf16[1024,1152]{1,0:T(8,128)(2,1)}, s32[8,128]{1,0:T(8,128)}) custom-call(s32[2]{0:T(128)} %pad_add_fusion.place_ref, bf16[2,2048,4608]{2,1,0:T(8,128)(2,1)} %get-tuple-element.227.refs_0_, bf16[2,1152,4608]{2,1,0:T(8,128)(2,1)} %refs_2_.27, bf16[2,1152,4608]{2,1,0:T(8,128)(2,1)} %refs_3_.37, ...), custom_call_target="tpu_custom_call" | custom-call | flops 10871635968 | bytes 10871635968 | tf_op jit(solution)/shard_map/pallas_call | solution.py:91
  475.5 33.3 %collective-permute-done.17.refs_2_ = bf16[2,288,768]{2,1,0:T(8,128)(2,1)} collective-permute-done((bf16[2,288,768]{2,1,0:T(8,128)(2,1)}, bf16[2,288,768]{2,1,0:T(8,128)(2,1)}, u32[]{:S(2)}, u32[]{:S(2)}) %collective-permute-start.17) | collective-permute-done | bytes 884768 | tf_op jit(solution)/shard_map/ppermute | solution.py:31
  514.6 63.0 %shard_map.200 = (f32[4096,4608]{1,0:T(8,128)}, f32[4096,4608]{1,0:T(8,128)}, bf16[4096,2304]{1,0:T(8,128)(2,1)}, bf16[1152,4096]{1,0:T(8,128)(2,1)}, s32[8,128]{1,0:T(8,128)}) custom-call(s32[2]{0:T(128)} %pad_add_fusion.place_ref, ...), custom_call_target="tpu_custom_call", output_to_operand_aliasing={{0}: (4, {}), {1}: (5, {}), {2}: (6, {}), {3}: (7, {})} | custom-call | flops 10871635968 | bytes 10871635968 | tf_op jit(solution)/shard_map/pallas_call | solution.py:91
  577.6 32.3 %collective-permute-done.14.refs_3_.refs_2_ = bf16[1024,1152]{1,0:T(8,128)(2,1)} collective-permute-done((bf16[1024,1152]{1,0:T(8,128)(2,1)}, bf16[1024,1152]{1,0:T(8,128)(2,1)}, u32[]{:S(2)}, u32[]{:S(2)}) %collective-permute-start.14) | collective-permute-done | bytes 2359328 | tf_op jit(solution)/shard_map/ppermute | solution.py:31
  609.9 33.4 %shard_map.201 = (f32[1152,1152]{1,0:T(8,128)}, bf16[1152,1152]{1,0:T(8,128)(2,1)}, s32[8,128]{1,0:T(8,128)}) custom-call(s32[2]{0:T(128)} %pad_add_fusion.place_ref, bf16[4096,2304]{1,0:T(8,128)(2,1)} %get-tuple-element.258.refs_0_, bf16[1024,1152]{1,0:T(8,128)(2,1)} %get-tuple-element.241.refs_1_.refs_0_, ...), custom_call_target="tpu_custom_call" | custom-call | flops 10871635968 | bytes 10871635968 | tf_op jit(solution)/shard_map/pallas_call | solution.py:91
  686.3 18.4 %collective-permute-done.45.refs_22_ = bf16[384,1152]{1,0:T(8,128)(2,1)} collective-permute-done((bf16[384,1152]{1,0:T(8,128)(2,1)}, bf16[384,1152]{1,0:T(8,128)(2,1)}, u32[]{:S(2)}, u32[]{:S(2)}) %collective-permute-start.45) | collective-permute-done | bytes 884768 | tf_op jit(solution)/shard_map/ppermute | solution.py:31
  704.7 18.0 %collective-permute-done.42.refs_18_ = bf16[2,288,768]{2,1,0:T(8,128)(2,1)} collective-permute-done((bf16[2,288,768]{2,1,0:T(8,128)(2,1)}, bf16[2,288,768]{2,1,0:T(8,128)(2,1)}, u32[]{:S(2)}, u32[]{:S(2)}) %collective-permute-start.42) | collective-permute-done | bytes 884768 | tf_op jit(solution)/shard_map/ppermute | solution.py:31
  737.9 64.9 %shard_map.204 = (f32[2,288,2304]{2,1,0:T(8,128)}, bf16[2,288,2304]{2,1,0:T(8,128)(2,1)}, bf16[2,1152,4608]{2,1,0:T(8,128)(2,1)}, bf16[2,1152,4608]{2,1,0:T(8,12...) custom-call(s32[2]{0:T(128)} %pad_add_fusion.place_ref, ...), custom_call_target="tpu_custom_call" | custom-call | flops 10871635968 | bytes 10871635968 | tf_op jit(solution)/shard_map/pallas_call | solution.py:91
  809.5 53.5 %collective-permute-done.27.refs_14_ = bf16[2,288,768]{2,1,0:T(8,128)(2,1)S(1)} collective-permute-done((bf16[2,288,768]{2,1,0:T(8,128)(2,1)}, bf16[2,288,768]{2,1,0:T(8,128)(2,1)S(1)}, u32[]{:S(2)}, u32[]{:S(2)}) %collective-permute-start.27) | collective-permute-done | bytes 884768 | tf_op jit(solution)/shard_map/ppermute | solution.py:31
  868.2 18.7 %collective-permute-done.30.refs_18_ = bf16[2,288,768]{2,1,0:T(8,128)(2,1)} collective-permute-done((bf16[2,288,768]{2,1,0:T(8,128)(2,1)}, bf16[2,288,768]{2,1,0:T(8,128)(2,1)}, u32[]{:S(2)}, u32[]{:S(2)}) %collective-permute-start.30) | collective-permute-done | bytes 884768 | tf_op jit(solution)/shard_map/ppermute | solution.py:31
  900.8 48.7 %shard_map.206 = (f32[2,288,1536]{2,1,0:T(8,128)}, bf16[2,288,1536]{2,1,0:T(8,128)(2,1)}, bf16[2,1152,4608]{2,1,0:T(8,128)(2,1)}, bf16[2,1152,4608]{2,1,0:T(8,12...) custom-call(s32[2]{0:T(128)} %pad_add_fusion.place_ref, ...), custom_call_target="tpu_custom_call", output_to_operand_aliasing={{2}: (25, {}), {3}: (26, {}), {4}: (27, {})} | custom-call | flops 10871635968 | bytes 10871635968 | tf_op jit(solution)/shard_map/pallas_call | solution.py:91
  963.1 30.5 %shard_map.208 = (f32[2,288,768]{2,1,0:T(8,128)}, bf16[2,288,768]{2,1,0:T(8,128)(2,1)}, bf16[2,4608,1152]{2,1,0:T(8,128)(2,1)}, s32[8,128]{1,0:T(8,128)}) custom-call(s32[2]{0:T(128)} %pad_add_fusion.place_ref, bf16[1024,1152]{1,0:T(8,128)(2,1)} %get-tuple-element.241.refs_1_.refs_0_, ...), custom_call_target="tpu_custom_call", output_to_operand_aliasing={{2}: (13, {})} | custom-call | flops 10871635968 | bytes 10871635968 | tf_op jit(solution)/shard_map/pallas_call | solution.py:91
  994.1 16.3 %collective-permute-done.57.refs_2_ = bf16[2,288,2304]{2,1,0:T(8,128)(2,1)} collective-permute-done((bf16[2,288,2304]{2,1,0:T(8,128)(2,1)}, bf16[2,288,2304]{2,1,0:T(8,128)(2,1)}, u32[]{:S(2)}, u32[]{:S(2)}) %collective-permute-start.57) | collective-permute-done | bytes 2654240 | tf_op jit(solution)/shard_map/ppermute | solution.py:31
  1017.9 34.2 %collective-permute-done.54.refs_2_ = bf16[2,288,1536]{2,1,0:T(8,128)(2,1)} collective-permute-done((bf16[2,288,1536]{2,1,0:T(8,128)(2,1)}, bf16[2,288,1536]{2,1,0:T(8,128)(2,1)}, u32[]{:S(2)}, u32[]{:S(2)}) %collective-permute-start.54) | collective-permute-done | bytes 1769504 | tf_op jit(solution)/shard_map/ppermute | solution.py:31
  1052.7 18.0 %collective-permute-done.51.refs_2_ = bf16[2,288,768]{2,1,0:T(8,128)(2,1)} collective-permute-done((bf16[2,288,768]{2,1,0:T(8,128)(2,1)}, bf16[2,288,768]{2,1,0:T(8,128)(2,1)}, u32[]{:S(2)}, u32[]{:S(2)}) %collective-permute-start.51) | collective-permute-done | bytes 884768 | tf_op jit(solution)/shard_map/ppermute | solution.py:31
  (138 shorter events, 222.3 us)
Async XLA Ops:
  270.7 51.8 %collective-permute-start.10 = (bf16[2,288,768]{2,1,0:T(8,128)(2,1)}, bf16[2,288,768]{2,1,0:T(8,128)(2,1)}, u32[]{:S(2)}, u32[]{:S(2)}) collective-permute-start(bf16[2,288,768]{2,1,0:T(8,128)(2,1)} %get-tuple-element.219), channel_id=1, source_target_pairs={{0,2},{1,3},{2,0},{3,1},{4,6},{5,7},{6,4},{7,5}} | collective-permute-start | bytes 2654216 | tf_op jit(solution)/shard_map/ppermute | solution.py:31
  365.9 148.7 %collective-permute-start.16 = (bf16[2048,1152]{1,0:T(8,128)(2,1)}, bf16[2048,1152]{1,0:T(8,128)(2,1)}, u32[]{:S(2)}, u32[]{:S(2)}) collective-permute-start(bf16[2048,1152]{1,0:T(8,128)(2,1)} %bitcast.13), channel_id=1, source_target_pairs={{0,2},{1,3},{2,0},{3,1},{4,6},{5,7},{6,4},{7,5}} | collective-permute-start | bytes 14155784 | tf_op jit(solution)/shard_map/ppermute | solution.py:31
  399.9 108.9 %collective-permute-start.17 = (bf16[2,288,768]{2,1,0:T(8,128)(2,1)}, bf16[2,288,768]{2,1,0:T(8,128)(2,1)}, u32[]{:S(2)}, u32[]{:S(2)}) collective-permute-start(bf16[2,288,768]{2,1,0:T(8,128)(2,1)} %get-tuple-element.248), channel_id=1, source_target_pairs={{0,2},{1,3},{2,0},{3,1},{4,6},{5,7},{6,4},{7,5}} | collective-permute-start | bytes 2654216 | tf_op jit(solution)/shard_map/ppermute | solution.py:31
  471.4 106.2 %collective-permute-start.15 = (bf16[1024,1152]{1,0:T(8,128)(2,1)}, bf16[1024,1152]{1,0:T(8,128)(2,1)}, u32[]{:S(2)}, u32[]{:S(2)}) collective-permute-start(bf16[1024,1152]{1,0:T(8,128)(2,1)} %get-tuple-element.243.refs_2_.refs_1_), channel_id=1, source_target_pairs={{0,2},{1,3},{2,0},{3,1},{4,6},{5,7},{6,4},{7,5}} | collective-permute-start | bytes 7077896 | tf_op jit(solution)/shard_map/ppermute | solution.py:31
  473.5 136.4 %collective-permute-start.14 = (bf16[1024,1152]{1,0:T(8,128)(2,1)}, bf16[1024,1152]{1,0:T(8,128)(2,1)}, u32[]{:S(2)}, u32[]{:S(2)}) collective-permute-start(bf16[1024,1152]{1,0:T(8,128)(2,1)} %get-tuple-element.241.refs_1_.refs_0_), channel_id=1, source_target_pairs={{0,2},{1,3},{2,0},{3,1},{4,6},{5,7},{6,4},{7,5}} | collective-permute-start | bytes 7077896 | tf_op jit(solution)/shard_map/ppermute | solution.py:31
  473.5 170.3 %collective-permute-start.36 = (bf16[2,288,768]{2,1,0:T(8,128)(2,1)}, bf16[2,288,768]{2,1,0:T(8,128)(2,1)}, u32[]{:S(2)}, u32[]{:S(2)}) collective-permute-start(bf16[2,288,768]{2,1,0:T(8,128)(2,1)} %get-tuple-element.274.refs_8_), channel_id=1, source_target_pairs={{0,2},{1,3},{2,0},{3,1},{4,6},{5,7},{6,4},{7,5}} | collective-permute-start | bytes 2654216 | tf_op jit(solution)/shard_map/ppermute | solution.py:31
  508.8 158.0 %collective-permute-start.19 = (bf16[768,1152]{1,0:T(8,128)(2,1)}, bf16[768,1152]{1,0:T(8,128)(2,1)}, u32[]{:S(2)}, u32[]{:S(2)}) collective-permute-start(bf16[768,1152]{1,0:T(8,128)(2,1)} %get-tuple-element.262), channel_id=1, source_target_pairs={{0,2},{1,3},{2,0},{3,1},{4,6},{5,7},{6,4},{7,5}} | collective-permute-start | bytes 5308424 | tf_op jit(solution)/shard_map/ppermute | solution.py:31
  643.3 79.4 %collective-permute-start.18 = (bf16[1152,1152]{1,0:T(8,128)(2,1)}, bf16[1152,1152]{1,0:T(8,128)(2,1)}, u32[]{:S(2)}, u32[]{:S(2)}) collective-permute-start(bf16[1152,1152]{1,0:T(8,128)(2,1)} %get-tuple-element.261), channel_id=1, source_target_pairs={{0,1},{1,0},{2,3},{3,2},{4,5},{5,4},{6,7},{7,6}} | collective-permute-start | bytes 7962632 | tf_op jit(solution)/shard_map/ppermute | solution.py:31
  651.1 53.6 %collective-permute-start.45 = (bf16[384,1152]{1,0:T(8,128)(2,1)}, bf16[384,1152]{1,0:T(8,128)(2,1)}, u32[]{:S(2)}, u32[]{:S(2)}) collective-permute-start(bf16[384,1152]{1,0:T(8,128)(2,1)} %get-tuple-element.277.refs_20_), channel_id=1, source_target_pairs={{0,2},{1,3},{2,0},{3,1},{4,6},{5,7},{6,4},{7,5}} | collective-permute-start | bytes 2654216 | tf_op jit(solution)/shard_map/ppermute | solution.py:31
  666.8 55.9 %collective-permute-start.42 = (bf16[2,288,768]{2,1,0:T(8,128)(2,1)}, bf16[2,288,768]{2,1,0:T(8,128)(2,1)}, u32[]{:S(2)}, u32[]{:S(2)}) collective-permute-start(bf16[2,288,768]{2,1,0:T(8,128)(2,1)} %get-tuple-element.276.refs_16_), channel_id=1, source_target_pairs={{0,2},{1,3},{2,0},{3,1},{4,6},{5,7},{6,4},{7,5}} | collective-permute-start | bytes 2654216 | tf_op jit(solution)/shard_map/ppermute | solution.py:31
  685.7 51.8 %collective-permute-start.44 = (bf16[384,1152]{1,0:T(8,128)(2,1)}, bf16[384,1152]{1,0:T(8,128)(2,1)}, u32[]{:S(2)}, u32[]{:S(2)}) collective-permute-start(bf16[384,1152]{1,0:T(8,128)(2,1)} %get-tuple-element.277.refs_20_), channel_id=1, source_target_pairs={{0,1},{1,0},{2,3},{3,2},{4,5},{5,4},{6,7},{7,6}} | collective-permute-start | bytes 2654216 | tf_op jit(solution)/shard_map/ppermute | solution.py:31
  685.8 52.1 %collective-permute-start.40 = (bf16[2,288,768]{2,1,0:T(8,128)(2,1)}, bf16[2,288,768]{2,1,0:T(8,128)(2,1)}, u32[]{:S(2)}, u32[]{:S(2)}) collective-permute-start(bf16[2,288,768]{2,1,0:T(8,128)(2,1)} %collective-permute-done.39.refs_14_), channel_id=1, source_target_pairs={{0,1},{1,0},{2,3},{3,2},{4,5},{5,4},{6,7},{7,6}} | collective-permute-start | bytes 2654216 | tf_op jit(solution)/shard_map/ppermute | solution.py:31
  737.5 67.8 %collective-permute-start.24 = (bf16[2,288,768]{2,1,0:T(8,128)(2,1)}, bf16[2,288,768]{2,1,0:T(8,128)(2,1)}, u32[]{:S(2)}, u32[]{:S(2)}) collective-permute-start(bf16[2,288,768]{2,1,0:T(8,128)(2,1)} %get-tuple-element.270.refs_8_), channel_id=1, source_target_pairs={{0,2},{1,3},{2,0},{3,1},{4,6},{5,7},{6,4},{7,5}} | collective-permute-start | bytes 2654216 | tf_op jit(solution)/shard_map/ppermute | solution.py:31
  802.7 84.1 %collective-permute-start.47 = (bf16[2,288,2304]{2,1,0:T(8,128)(2,1)}, bf16[2,288,2304]{2,1,0:T(8,128)(2,1)}, u32[]{:S(2)}, u32[]{:S(2)}) collective-permute-start(bf16[2,288,2304]{2,1,0:T(8,128)(2,1)} %get-tuple-element.283), channel_id=1, source_target_pairs={{0,1},{1,0},{2,3},{3,2},{4,5},{5,4},{6,7},{7,6}} | collective-permute-start | bytes 7962632 | tf_op jit(solution)/shard_map/ppermute | solution.py:31
  803.3 62.7 %collective-permute-start.33 = (bf16[768,1152]{1,0:T(8,128)(2,1)}, bf16[768,1152]{1,0:T(8,128)(2,1)}, u32[]{:S(2)}, u32[]{:S(2)}) collective-permute-start(bf16[768,1152]{1,0:T(8,128)(2,1)} %get-tuple-element.273.refs_20_), channel_id=1, source_target_pairs={{0,2},{1,3},{2,0},{3,1},{4,6},{5,7},{6,4},{7,5}} | collective-permute-start | bytes 5308424 | tf_op jit(solution)/shard_map/ppermute | solution.py:31
  805.0 58.0 %collective-permute-start.27 = (bf16[2,288,768]{2,1,0:T(8,128)(2,1)}, bf16[2,288,768]{2,1,0:T(8,128)(2,1)S(1)}, u32[]{:S(2)}, u32[]{:S(2)}) collective-permute-start(bf16[2,288,768]{2,1,0:T(8,128)(2,1)} %get-tuple-element.271.refs_12_), channel_id=1, source_target_pairs={{0,2},{1,3},{2,0},{3,1},{4,6},{5,7},{6,4},{7,5}} | collective-permute-start | bytes 2654216 | tf_op jit(solution)/shard_map/ppermute | solution.py:31
  805.3 58.7 %collective-permute-start.25 = (bf16[2,288,768]{2,1,0:T(8,128)(2,1)}, bf16[2,288,768]{2,1,0:T(8,128)(2,1)S(1)}, u32[]{:S(2)}, u32[]{:S(2)}) collective-permute-start(bf16[2,288,768]{2,1,0:T(8,128)(2,1)} %collective-permute-done.24.refs_10_), channel_id=1, source_target_pairs={{0,1},{1,0},{2,3},{3,2},{4,5},{5,4},{6,7},{7,6}} | collective-permute-start | bytes 2654216 | tf_op jit(solution)/shard_map/ppermute | solution.py:31
  809.3 56.4 %collective-permute-start.26 = (bf16[2,288,768]{2,1,0:T(8,128)(2,1)}, bf16[2,288,768]{2,1,0:T(8,128)(2,1)S(1)}, u32[]{:S(2)}, u32[]{:S(2)}) collective-permute-start(bf16[2,288,768]{2,1,0:T(8,128)(2,1)} %get-tuple-element.271.refs_12_), channel_id=1, source_target_pairs={{0,1},{1,0},{2,3},{3,2},{4,5},{5,4},{6,7},{7,6}} | collective-permute-start | bytes 2654216 | tf_op jit(solution)/shard_map/ppermute | solution.py:31
  866.7 83.3 %collective-permute-start.21 = (bf16[1152,1152]{1,0:T(8,128)(2,1)}, bf16[1152,1152]{1,0:T(8,128)(2,1)}, u32[]{:S(2)}, u32[]{:S(2)}) collective-permute-start(bf16[1152,1152]{1,0:T(8,128)(2,1)} %get-tuple-element.269.refs_8_), channel_id=1, source_target_pairs={{0,2},{1,3},{2,0},{3,1},{4,6},{5,7},{6,4},{7,5}} | collective-permute-start | bytes 7962632 | tf_op jit(solution)/shard_map/ppermute | solution.py:31
  950.1 60.3 %collective-permute-start.57 = (bf16[2,288,2304]{2,1,0:T(8,128)(2,1)}, bf16[2,288,2304]{2,1,0:T(8,128)(2,1)}, u32[]{:S(2)}, u32[]{:S(2)}) collective-permute-start(bf16[2,288,2304]{2,1,0:T(8,128)(2,1)} %get-tuple-element.308.refs_0_), channel_id=1, source_target_pairs={{0,2},{1,3},{2,0},{3,1},{4,6},{5,7},{6,4},{7,5}} | collective-permute-start | bytes 7962632 | tf_op jit(solution)/shard_map/ppermute | solution.py:31
  993.7 58.4 %collective-permute-start.56 = (bf16[2,288,2304]{2,1,0:T(8,128)(2,1)}, bf16[2,288,2304]{2,1,0:T(8,128)(2,1)}, u32[]{:S(2)}, u32[]{:S(2)}) collective-permute-start(bf16[2,288,2304]{2,1,0:T(8,128)(2,1)} %get-tuple-element.308.refs_0_), channel_id=1, source_target_pairs={{0,1},{1,0},{2,3},{3,2},{4,5},{5,4},{6,7},{7,6}} | collective-permute-start | bytes 7962632 | tf_op jit(solution)/shard_map/ppermute | solution.py:31
  1010.4 60.3 %collective-permute-start.58 = (bf16[2,288,2304]{2,1,0:T(8,128)(2,1)}, bf16[2,288,2304]{2,1,0:T(8,128)(2,1)}, u32[]{:S(2)}, u32[]{:S(2)}) collective-permute-start(bf16[2,288,2304]{2,1,0:T(8,128)(2,1)} %collective-permute-done.57.refs_2_), channel_id=1, source_target_pairs={{0,1},{1,0},{2,3},{3,2},{4,5},{5,4},{6,7},{7,6}} | collective-permute-start | bytes 7962632 | tf_op jit(solution)/shard_map/ppermute | solution.py:31
  1017.6 53.0 %collective-permute-start.51 = (bf16[2,288,768]{2,1,0:T(8,128)(2,1)}, bf16[2,288,768]{2,1,0:T(8,128)(2,1)}, u32[]{:S(2)}, u32[]{:S(2)}) collective-permute-start(bf16[2,288,768]{2,1,0:T(8,128)(2,1)} %get-tuple-element.306.refs_0_), channel_id=1, source_target_pairs={{0,2},{1,3},{2,0},{3,1},{4,6},{5,7},{6,4},{7,5}} | collective-permute-start | bytes 2654216 | tf_op jit(solution)/shard_map/ppermute | solution.py:31
  1017.9 62.3 %collective-permute-start.53 = (bf16[2,288,1536]{2,1,0:T(8,128)(2,1)}, bf16[2,288,1536]{2,1,0:T(8,128)(2,1)}, u32[]{:S(2)}, u32[]{:S(2)}) collective-permute-start(bf16[2,288,1536]{2,1,0:T(8,128)(2,1)} %get-tuple-element.307.refs_0_), channel_id=1, source_target_pairs={{0,1},{1,0},{2,3},{3,2},{4,5},{5,4},{6,7},{7,6}} | collective-permute-start | bytes 5308424 | tf_op jit(solution)/shard_map/ppermute | solution.py:31
  (39 other events, 722.8 us)

commit v5 on v4

--- a/solution.py
+++ b/solution.py
@@ -693,9 +693,11 @@
         results, t = alone(place, t, (2 * span[2],), [into(0, span, own, came)])
         new0[name] = took(results, "into")
 
-    for name, q in (("a", 4), ("c", 8), ("e", 8)):
-        grid = (8 // q + 2,)
-        jobs = [copying(grid, q, into_pieces(0, spans[name], new0[name]))]
+    here, there = slice(4), slice(4, None)
+    for name, q, part in (("a", 4, slice(None)), ("c", 8, slice(None)), ("e", 4, here), ("e", 4, there)):
+        pieces = list(into_pieces(0, spans[name], new0[name]))[part]
+        grid = (len(pieces) // q + 2,)
+        jobs = [copying(grid, q, pieces)]
         results, t = call(nothing, place, t, [], [], grid, jobs=jobs)
         copied(results, ("gate", "up", "down")[: len(results)])
     held, o_down = (weights_out["gate"], weights_out["up"]), weights_out["down"]

time: 1100 us -> 1100 us (level)
    pallas_call x35 -> x36, Pallas kernels: 743 us -> 746 us  [call(): pl.pallas_call(kernel, grid_spec=pltpu.PrefetchScalarGridSpec(num_scalar_...]
where the time goes in v5:
time: 1100 us
  Pallas kernels  746 us (68%)
  waiting for transfers between devices  316 us (29%)
  starting transfers between devices  29.9 us (3%)
    pallas_call x36, Pallas kernels, call(): pl.pallas_call(kernel, grid_spec=pltpu.PrefetchScalarGridSpec(num_scalar_...  746 us
    ppermute x59, waiting for transfers between devices, over(): return lax.ppermute(array, 'dp', pairs)  316 us
    ppermute x59, starting transfers between devices, over(): return lax.ppermute(array, 'dp', pairs)  29.9 us
  transfers between devices with their start and end apart: 59, of which 20 were waited for; matrix products, arithmetic and copies ran while one was open for 0% of the time, Pallas kernels for 52%

profile of v5, /device:TPU:0, one launch (start us, length us, event | category | flops | bytes accessed | tf_op | source)
XLA Modules:
  0.0 1095.1 jit_solution(326175256834730303)
XLA Ops:
  1.3 91.0 %shard_map.178 = (f32[4096,4608]{1,0:T(8,128)}, f32[4096,4608]{1,0:T(8,128)}, bf16[4096,2304]{1,0:T(8,128)(2,1)}, bf16[1152,4096]{1,0:T(8,128)(2,1)}, bf16[2048,...) custom-call(s32[2]{0:T(128)} %pad_add_fusion.place_ref, bf16[2048,1152]{1,0:T(8,128)(2,1)} %bitcast.12, ...), custom_call_target="tpu_custom_call" | custom-call | flops 10871635968 | bytes 10871635968 | tf_op jit(solution)/shard_map/pallas_call | solution.py:91
  92.3 33.6 %shard_map.179 = (bf16[2,2048,4608]{2,1,0:T(8,128)(2,1)}, f32[2,2,288,768]{3,2,1,0:T(8,128)}, bf16[2,2,288,768]{3,2,1,0:T(8,128)(2,1)}, f32[2,384,1152]{2,1,0:T(...) custom-call(s32[2]{0:T(128)} %pad_add_fusion.place_ref, bf16[2048,1152]{1,0:T(8,128)(2,1)} %get-tuple-element.171.refs_0_, ...), custom_call_target="tpu_custom_call" | custom-call | flops 10871635968 | bytes 10871635968 | tf_op jit(solution)/shard_map/pallas_call | solution.py:91
  136.6 33.9 %shard_map.181 = (bf16[2,2048,4608]{2,1,0:T(8,128)(2,1)}, f32[2,2,288,768]{3,2,1,0:T(8,128)}, bf16[2,2,288,768]{3,2,1,0:T(8,128)(2,1)}, f32[2,384,1152]{2,1,0:T(...) custom-call(s32[2]{0:T(128)} %pad_add_fusion.place_ref, ...), custom_call_target="tpu_custom_call", output_to_operand_aliasing={{0}: (6, {}), {3}: (7, {}), {4}: (8, {})} | custom-call | flops 10871635968 | bytes 10871635968 | tf_op jit(solution)/shard_map/pallas_call | solution.py:91
  181.3 33.9 %shard_map.184 = (bf16[2,2048,4608]{2,1,0:T(8,128)(2,1)}, f32[2,2,288,768]{3,2,1,0:T(8,128)}, bf16[2,2,288,768]{3,2,1,0:T(8,128)(2,1)}, f32[2,768,1152]{2,1,0:T(...) custom-call(s32[2]{0:T(128)} %pad_add_fusion.place_ref, ...), custom_call_target="tpu_custom_call", output_to_operand_aliasing={{0}: (6, {})} | custom-call | flops 10871635968 | bytes 10871635968 | tf_op jit(solution)/shard_map/pallas_call | solution.py:91
  226.3 33.8 %shard_map.187 = (bf16[2,2048,4608]{2,1,0:T(8,128)(2,1)}, f32[2,2,288,768]{3,2,1,0:T(8,128)}, bf16[2,2,288,768]{3,2,1,0:T(8,128)(2,1)}, f32[2,768,1152]{2,1,0:T(...) custom-call(s32[2]{0:T(128)} %pad_add_fusion.place_ref, ...), custom_call_target="tpu_custom_call", output_to_operand_aliasing={{0}: (6, {}), {3}: (7, {}), {4}: (8, {})} | custom-call | flops 10871635968 | bytes 10871635968 | tf_op jit(solution)/shard_map/pallas_call | solution.py:91
  288.9 33.6 %shard_map.191 = (bf16[2,2048,4608]{2,1,0:T(8,128)(2,1)}, f32[2,2,288,768]{3,2,1,0:T(8,128)}, bf16[2,2,288,768]{3,2,1,0:T(8,128)(2,1)}, f32[2,768,1152]{2,1,0:T(...) custom-call(s32[2]{0:T(128)} %pad_add_fusion.place_ref, ...), custom_call_target="tpu_custom_call", output_to_operand_aliasing={{0}: (6, {}), {3}: (7, {}), {4}: (8, {})} | custom-call | flops 10871635968 | bytes 10871635968 | tf_op jit(solution)/shard_map/pallas_call | solution.py:91
  331.5 33.3 %shard_map.194 = (bf16[2,2048,4608]{2,1,0:T(8,128)(2,1)}, f32[2,2,288,768]{3,2,1,0:T(8,128)}, bf16[2,2,288,768]{3,2,1,0:T(8,128)(2,1)}, f32[2,768,1152]{2,1,0:T(...) custom-call(s32[2]{0:T(128)} %pad_add_fusion.place_ref, ...), custom_call_target="tpu_custom_call", output_to_operand_aliasing={{0}: (6, {}), {3}: (7, {}), {4}: (8, {})} | custom-call | flops 10871635968 | bytes 10871635968 | tf_op jit(solution)/shard_map/pallas_call | solution.py:91
  368.0 20.8 %collective-permute-done.13.refs_2_ = bf16[2,288,768]{2,1,0:T(8,128)(2,1)} collective-permute-done((bf16[2,288,768]{2,1,0:T(8,128)(2,1)}, bf16[2,288,768]{2,1,0:T(8,128)(2,1)}, u32[]{:S(2)}, u32[]{:S(2)}) %collective-permute-start.13) | collective-permute-done | bytes 884768 | tf_op jit(solution)/shard_map/ppermute | solution.py:31
  400.0 35.8 %shard_map.197 = (bf16[1024,1152]{1,0:T(8,128)(2,1)}, s32[8,128]{1,0:T(8,128)}) custom-call(s32[2]{0:T(128)} %pad_add_fusion.place_ref, bf16[2,2048,4608]{2,1,0:T(8,128)(2,1)} %get-tuple-element.230.refs_0_, bf16[2,1152,4608]{2,1,0:T(8,128)(2,1)} %refs_2_.27, bf16[2,1152,4608]{2,1,0:T(8,128)(2,1)} %refs_3_.37, ...), custom_call_target="tpu_custom_call" | custom-call | flops 10871635968 | bytes 10871635968 | tf_op jit(solution)/shard_map/pallas_call | solution.py:91
  435.7 35.9 %shard_map.198 = (bf16[1024,1152]{1,0:T(8,128)(2,1)}, s32[8,128]{1,0:T(8,128)}) custom-call(s32[2]{0:T(128)} %pad_add_fusion.place_ref, bf16[2,2048,4608]{2,1,0:T(8,128)(2,1)} %get-tuple-element.230.refs_0_, bf16[2,1152,4608]{2,1,0:T(8,128)(2,1)} %refs_2_.27, bf16[2,1152,4608]{2,1,0:T(8,128)(2,1)} %refs_3_.37, ...), custom_call_target="tpu_custom_call" | custom-call | flops 10871635968 | bytes 10871635968 | tf_op jit(solution)/shard_map/pallas_call | solution.py:91
  475.7 33.2 %collective-permute-done.17.refs_2_ = bf16[2,288,768]{2,1,0:T(8,128)(2,1)} collective-permute-done((bf16[2,288,768]{2,1,0:T(8,128)(2,1)}, bf16[2,288,768]{2,1,0:T(8,128)(2,1)}, u32[]{:S(2)}, u32[]{:S(2)}) %collective-permute-start.17) | collective-permute-done | bytes 884768 | tf_op jit(solution)/shard_map/ppermute | solution.py:31
  514.7 63.0 %shard_map.200 = (f32[4096,4608]{1,0:T(8,128)}, f32[4096,4608]{1,0:T(8,128)}, bf16[4096,2304]{1,0:T(8,128)(2,1)}, bf16[1152,4096]{1,0:T(8,128)(2,1)}, s32[8,128]{1,0:T(8,128)}) custom-call(s32[2]{0:T(128)} %pad_add_fusion.place_ref, ...), custom_call_target="tpu_custom_call", output_to_operand_aliasing={{0}: (4, {}), {1}: (5, {}), {2}: (6, {}), {3}: (7, {})} | custom-call | flops 10871635968 | bytes 10871635968 | tf_op jit(solution)/shard_map/pallas_call | solution.py:91
  577.7 32.3 %collective-permute-done.14.refs_3_.refs_2_ = bf16[1024,1152]{1,0:T(8,128)(2,1)} collective-permute-done((bf16[1024,1152]{1,0:T(8,128)(2,1)}, bf16[1024,1152]{1,0:T(8,128)(2,1)}, u32[]{:S(2)}, u32[]{:S(2)}) %collective-permute-start.14) | collective-permute-done | bytes 2359328 | tf_op jit(solution)/shard_map/ppermute | solution.py:31
  610.0 33.4 %shard_map.201 = (f32[1152,1152]{1,0:T(8,128)}, bf16[1152,1152]{1,0:T(8,128)(2,1)}, s32[8,128]{1,0:T(8,128)}) custom-call(s32[2]{0:T(128)} %pad_add_fusion.place_ref, bf16[4096,2304]{1,0:T(8,128)(2,1)} %get-tuple-element.261.refs_0_, bf16[1024,1152]{1,0:T(8,128)(2,1)} %get-tuple-element.244.refs_1_.refs_0_, ...), custom_call_target="tpu_custom_call" | custom-call | flops 10871635968 | bytes 10871635968 | tf_op jit(solution)/shard_map/pallas_call | solution.py:91
  686.3 18.4 %collective-permute-done.45.refs_22_ = bf16[384,1152]{1,0:T(8,128)(2,1)} collective-permute-done((bf16[384,1152]{1,0:T(8,128)(2,1)}, bf16[384,1152]{1,0:T(8,128)(2,1)}, u32[]{:S(2)}, u32[]{:S(2)}) %collective-permute-start.45) | collective-permute-done | bytes 884768 | tf_op jit(solution)/shard_map/ppermute | solution.py:31
  704.8 18.0 %collective-permute-done.42.refs_18_ = bf16[2,288,768]{2,1,0:T(8,128)(2,1)} collective-permute-done((bf16[2,288,768]{2,1,0:T(8,128)(2,1)}, bf16[2,288,768]{2,1,0:T(8,128)(2,1)}, u32[]{:S(2)}, u32[]{:S(2)}) %collective-permute-start.42) | collective-permute-done | bytes 884768 | tf_op jit(solution)/shard_map/ppermute | solution.py:31
  737.9 64.9 %shard_map.204 = (f32[2,288,2304]{2,1,0:T(8,128)}, bf16[2,288,2304]{2,1,0:T(8,128)(2,1)}, bf16[2,1152,4608]{2,1,0:T(8,128)(2,1)}, bf16[2,1152,4608]{2,1,0:T(8,12...) custom-call(s32[2]{0:T(128)} %pad_add_fusion.place_ref, ...), custom_call_target="tpu_custom_call" | custom-call | flops 10871635968 | bytes 10871635968 | tf_op jit(solution)/shard_map/pallas_call | solution.py:91
  809.5 53.5 %collective-permute-done.27.refs_14_ = bf16[2,288,768]{2,1,0:T(8,128)(2,1)S(1)} collective-permute-done((bf16[2,288,768]{2,1,0:T(8,128)(2,1)}, bf16[2,288,768]{2,1,0:T(8,128)(2,1)S(1)}, u32[]{:S(2)}, u32[]{:S(2)}) %collective-permute-start.27) | collective-permute-done | bytes 884768 | tf_op jit(solution)/shard_map/ppermute | solution.py:31
  868.2 18.7 %collective-permute-done.30.refs_18_ = bf16[2,288,768]{2,1,0:T(8,128)(2,1)} collective-permute-done((bf16[2,288,768]{2,1,0:T(8,128)(2,1)}, bf16[2,288,768]{2,1,0:T(8,128)(2,1)}, u32[]{:S(2)}, u32[]{:S(2)}) %collective-permute-start.30) | collective-permute-done | bytes 884768 | tf_op jit(solution)/shard_map/ppermute | solution.py:31
  900.9 48.6 %shard_map.206 = (f32[2,288,1536]{2,1,0:T(8,128)}, bf16[2,288,1536]{2,1,0:T(8,128)(2,1)}, bf16[2,1152,4608]{2,1,0:T(8,128)(2,1)}, bf16[2,1152,4608]{2,1,0:T(8,12...) custom-call(s32[2]{0:T(128)} %pad_add_fusion.place_ref, ...), custom_call_target="tpu_custom_call", output_to_operand_aliasing={{2}: (25, {}), {3}: (26, {}), {4}: (27, {})} | custom-call | flops 10871635968 | bytes 10871635968 | tf_op jit(solution)/shard_map/pallas_call | solution.py:91
  963.0 30.4 %shard_map.208 = (f32[2,288,768]{2,1,0:T(8,128)}, bf16[2,288,768]{2,1,0:T(8,128)(2,1)}, bf16[2,4608,1152]{2,1,0:T(8,128)(2,1)}, s32[8,128]{1,0:T(8,128)}) custom-call(s32[2]{0:T(128)} %pad_add_fusion.place_ref, bf16[1024,1152]{1,0:T(8,128)(2,1)} %get-tuple-element.244.refs_1_.refs_0_, ...), custom_call_target="tpu_custom_call", output_to_operand_aliasing={{2}: (13, {})} | custom-call | flops 10871635968 | bytes 10871635968 | tf_op jit(solution)/shard_map/pallas_call | solution.py:91
  994.0 16.4 %collective-permute-done.57.refs_2_ = bf16[2,288,2304]{2,1,0:T(8,128)(2,1)} collective-permute-done((bf16[2,288,2304]{2,1,0:T(8,128)(2,1)}, bf16[2,288,2304]{2,1,0:T(8,128)(2,1)}, u32[]{:S(2)}, u32[]{:S(2)}) %collective-permute-start.57) | collective-permute-done | bytes 2654240 | tf_op jit(solution)/shard_map/ppermute | solution.py:31
  1017.9 34.3 %collective-permute-done.54.refs_2_ = bf16[2,288,1536]{2,1,0:T(8,128)(2,1)} collective-permute-done((bf16[2,288,1536]{2,1,0:T(8,128)(2,1)}, bf16[2,288,1536]{2,1,0:T(8,128)(2,1)}, u32[]{:S(2)}, u32[]{:S(2)}) %collective-permute-start.54) | collective-permute-done | bytes 1769504 | tf_op jit(solution)/shard_map/ppermute | solution.py:31
  1052.7 18.0 %collective-permute-done.50.refs_0_ = bf16[2,288,768]{2,1,0:T(8,128)(2,1)} collective-permute-done((bf16[2,288,768]{2,1,0:T(8,128)(2,1)}, bf16[2,288,768]{2,1,0:T(8,128)(2,1)}, u32[]{:S(2)}, u32[]{:S(2)}) %collective-permute-start.50) | collective-permute-done | bytes 884768 | tf_op jit(solution)/shard_map/ppermute | solution.py:31
  (139 shorter events, 225.1 us)
Async XLA Ops:
  270.6 51.9 %collective-permute-start.10 = (bf16[2,288,768]{2,1,0:T(8,128)(2,1)}, bf16[2,288,768]{2,1,0:T(8,128)(2,1)}, u32[]{:S(2)}, u32[]{:S(2)}) collective-permute-start(bf16[2,288,768]{2,1,0:T(8,128)(2,1)} %get-tuple-element.222), channel_id=1, source_target_pairs={{0,2},{1,3},{2,0},{3,1},{4,6},{5,7},{6,4},{7,5}} | collective-permute-start | bytes 2654216 | tf_op jit(solution)/shard_map/ppermute | solution.py:31
  366.0 148.7 %collective-permute-start.16 = (bf16[2048,1152]{1,0:T(8,128)(2,1)}, bf16[2048,1152]{1,0:T(8,128)(2,1)}, u32[]{:S(2)}, u32[]{:S(2)}) collective-permute-start(bf16[2048,1152]{1,0:T(8,128)(2,1)} %bitcast.13), channel_id=1, source_target_pairs={{0,2},{1,3},{2,0},{3,1},{4,6},{5,7},{6,4},{7,5}} | collective-permute-start | bytes 14155784 | tf_op jit(solution)/shard_map/ppermute | solution.py:31
  400.0 108.9 %collective-permute-start.17 = (bf16[2,288,768]{2,1,0:T(8,128)(2,1)}, bf16[2,288,768]{2,1,0:T(8,128)(2,1)}, u32[]{:S(2)}, u32[]{:S(2)}) collective-permute-start(bf16[2,288,768]{2,1,0:T(8,128)(2,1)} %get-tuple-element.251), channel_id=1, source_target_pairs={{0,2},{1,3},{2,0},{3,1},{4,6},{5,7},{6,4},{7,5}} | collective-permute-start | bytes 2654216 | tf_op jit(solution)/shard_map/ppermute | solution.py:31
  471.7 106.0 %collective-permute-start.15 = (bf16[1024,1152]{1,0:T(8,128)(2,1)}, bf16[1024,1152]{1,0:T(8,128)(2,1)}, u32[]{:S(2)}, u32[]{:S(2)}) collective-permute-start(bf16[1024,1152]{1,0:T(8,128)(2,1)} %get-tuple-element.246.refs_2_.refs_1_), channel_id=1, source_target_pairs={{0,2},{1,3},{2,0},{3,1},{4,6},{5,7},{6,4},{7,5}} | collective-permute-start | bytes 7077896 | tf_op jit(solution)/shard_map/ppermute | solution.py:31
  473.7 136.3 %collective-permute-start.14 = (bf16[1024,1152]{1,0:T(8,128)(2,1)}, bf16[1024,1152]{1,0:T(8,128)(2,1)}, u32[]{:S(2)}, u32[]{:S(2)}) collective-permute-start(bf16[1024,1152]{1,0:T(8,128)(2,1)} %get-tuple-element.244.refs_1_.refs_0_), channel_id=1, source_target_pairs={{0,2},{1,3},{2,0},{3,1},{4,6},{5,7},{6,4},{7,5}} | collective-permute-start | bytes 7077896 | tf_op jit(solution)/shard_map/ppermute | solution.py:31
  473.7 170.2 %collective-permute-start.36 = (bf16[2,288,768]{2,1,0:T(8,128)(2,1)}, bf16[2,288,768]{2,1,0:T(8,128)(2,1)}, u32[]{:S(2)}, u32[]{:S(2)}) collective-permute-start(bf16[2,288,768]{2,1,0:T(8,128)(2,1)} %get-tuple-element.277.refs_8_), channel_id=1, source_target_pairs={{0,2},{1,3},{2,0},{3,1},{4,6},{5,7},{6,4},{7,5}} | collective-permute-start | bytes 2654216 | tf_op jit(solution)/shard_map/ppermute | solution.py:31
  508.9 158.0 %collective-permute-start.19 = (bf16[768,1152]{1,0:T(8,128)(2,1)}, bf16[768,1152]{1,0:T(8,128)(2,1)}, u32[]{:S(2)}, u32[]{:S(2)}) collective-permute-start(bf16[768,1152]{1,0:T(8,128)(2,1)} %get-tuple-element.265), channel_id=1, source_target_pairs={{0,2},{1,3},{2,0},{3,1},{4,6},{5,7},{6,4},{7,5}} | collective-permute-start | bytes 5308424 | tf_op jit(solution)/shard_map/ppermute | solution.py:31
  643.4 79.4 %collective-permute-start.18 = (bf16[1152,1152]{1,0:T(8,128)(2,1)}, bf16[1152,1152]{1,0:T(8,128)(2,1)}, u32[]{:S(2)}, u32[]{:S(2)}) collective-permute-start(bf16[1152,1152]{1,0:T(8,128)(2,1)} %get-tuple-element.264), channel_id=1, source_target_pairs={{0,1},{1,0},{2,3},{3,2},{4,5},{5,4},{6,7},{7,6}} | collective-permute-start | bytes 7962632 | tf_op jit(solution)/shard_map/ppermute | solution.py:31
  651.2 53.5 %collective-permute-start.45 = (bf16[384,1152]{1,0:T(8,128)(2,1)}, bf16[384,1152]{1,0:T(8,128)(2,1)}, u32[]{:S(2)}, u32[]{:S(2)}) collective-permute-start(bf16[384,1152]{1,0:T(8,128)(2,1)} %get-tuple-element.280.refs_20_), channel_id=1, source_target_pairs={{0,2},{1,3},{2,0},{3,1},{4,6},{5,7},{6,4},{7,5}} | collective-permute-start | bytes 2654216 | tf_op jit(solution)/shard_map/ppermute | solution.py:31
  666.9 55.9 %collective-permute-start.42 = (bf16[2,288,768]{2,1,0:T(8,128)(2,1)}, bf16[2,288,768]{2,1,0:T(8,128)(2,1)}, u32[]{:S(2)}, u32[]{:S(2)}) collective-permute-start(bf16[2,288,768]{2,1,0:T(8,128)(2,1)} %get-tuple-element.279.refs_16_), channel_id=1, source_target_pairs={{0,2},{1,3},{2,0},{3,1},{4,6},{5,7},{6,4},{7,5}} | collective-permute-start | bytes 2654216 | tf_op jit(solution)/shard_map/ppermute | solution.py:31
  685.8 51.8 %collective-permute-start.44 = (bf16[384,1152]{1,0:T(8,128)(2,1)}, bf16[384,1152]{1,0:T(8,128)(2,1)}, u32[]{:S(2)}, u32[]{:S(2)}) collective-permute-start(bf16[384,1152]{1,0:T(8,128)(2,1)} %get-tuple-element.280.refs_20_), channel_id=1, source_target_pairs={{0,1},{1,0},{2,3},{3,2},{4,5},{5,4},{6,7},{7,6}} | collective-permute-start | bytes 2654216 | tf_op jit(solution)/shard_map/ppermute | solution.py:31
  685.8 52.1 %collective-permute-start.40 = (bf16[2,288,768]{2,1,0:T(8,128)(2,1)}, bf16[2,288,768]{2,1,0:T(8,128)(2,1)}, u32[]{:S(2)}, u32[]{:S(2)}) collective-permute-start(bf16[2,288,768]{2,1,0:T(8,128)(2,1)} %collective-permute-done.39.refs_14_), channel_id=1, source_target_pairs={{0,1},{1,0},{2,3},{3,2},{4,5},{5,4},{6,7},{7,6}} | collective-permute-start | bytes 2654216 | tf_op jit(solution)/shard_map/ppermute | solution.py:31
  737.6 67.8 %collective-permute-start.24 = (bf16[2,288,768]{2,1,0:T(8,128)(2,1)}, bf16[2,288,768]{2,1,0:T(8,128)(2,1)}, u32[]{:S(2)}, u32[]{:S(2)}) collective-permute-start(bf16[2,288,768]{2,1,0:T(8,128)(2,1)} %get-tuple-element.273.refs_8_), channel_id=1, source_target_pairs={{0,2},{1,3},{2,0},{3,1},{4,6},{5,7},{6,4},{7,5}} | collective-permute-start | bytes 2654216 | tf_op jit(solution)/shard_map/ppermute | solution.py:31
  802.8 84.1 %collective-permute-start.47 = (bf16[2,288,2304]{2,1,0:T(8,128)(2,1)}, bf16[2,288,2304]{2,1,0:T(8,128)(2,1)}, u32[]{:S(2)}, u32[]{:S(2)}) collective-permute-start(bf16[2,288,2304]{2,1,0:T(8,128)(2,1)} %get-tuple-element.286), channel_id=1, source_target_pairs={{0,1},{1,0},{2,3},{3,2},{4,5},{5,4},{6,7},{7,6}} | collective-permute-start | bytes 7962632 | tf_op jit(solution)/shard_map/ppermute | solution.py:31
  803.3 62.7 %collective-permute-start.33 = (bf16[768,1152]{1,0:T(8,128)(2,1)}, bf16[768,1152]{1,0:T(8,128)(2,1)}, u32[]{:S(2)}, u32[]{:S(2)}) collective-permute-start(bf16[768,1152]{1,0:T(8,128)(2,1)} %get-tuple-element.276.refs_20_), channel_id=1, source_target_pairs={{0,2},{1,3},{2,0},{3,1},{4,6},{5,7},{6,4},{7,5}} | collective-permute-start | bytes 5308424 | tf_op jit(solution)/shard_map/ppermute | solution.py:31
  805.1 58.0 %collective-permute-start.27 = (bf16[2,288,768]{2,1,0:T(8,128)(2,1)}, bf16[2,288,768]{2,1,0:T(8,128)(2,1)S(1)}, u32[]{:S(2)}, u32[]{:S(2)}) collective-permute-start(bf16[2,288,768]{2,1,0:T(8,128)(2,1)} %get-tuple-element.274.refs_12_), channel_id=1, source_target_pairs={{0,2},{1,3},{2,0},{3,1},{4,6},{5,7},{6,4},{7,5}} | collective-permute-start | bytes 2654216 | tf_op jit(solution)/shard_map/ppermute | solution.py:31
  805.4 58.7 %collective-permute-start.25 = (bf16[2,288,768]{2,1,0:T(8,128)(2,1)}, bf16[2,288,768]{2,1,0:T(8,128)(2,1)S(1)}, u32[]{:S(2)}, u32[]{:S(2)}) collective-permute-start(bf16[2,288,768]{2,1,0:T(8,128)(2,1)} %collective-permute-done.24.refs_10_), channel_id=1, source_target_pairs={{0,1},{1,0},{2,3},{3,2},{4,5},{5,4},{6,7},{7,6}} | collective-permute-start | bytes 2654216 | tf_op jit(solution)/shard_map/ppermute | solution.py:31
  809.4 56.4 %collective-permute-start.26 = (bf16[2,288,768]{2,1,0:T(8,128)(2,1)}, bf16[2,288,768]{2,1,0:T(8,128)(2,1)S(1)}, u32[]{:S(2)}, u32[]{:S(2)}) collective-permute-start(bf16[2,288,768]{2,1,0:T(8,128)(2,1)} %get-tuple-element.274.refs_12_), channel_id=1, source_target_pairs={{0,1},{1,0},{2,3},{3,2},{4,5},{5,4},{6,7},{7,6}} | collective-permute-start | bytes 2654216 | tf_op jit(solution)/shard_map/ppermute | solution.py:31
  866.8 83.3 %collective-permute-start.21 = (bf16[1152,1152]{1,0:T(8,128)(2,1)}, bf16[1152,1152]{1,0:T(8,128)(2,1)}, u32[]{:S(2)}, u32[]{:S(2)}) collective-permute-start(bf16[1152,1152]{1,0:T(8,128)(2,1)} %get-tuple-element.272.refs_8_), channel_id=1, source_target_pairs={{0,2},{1,3},{2,0},{3,1},{4,6},{5,7},{6,4},{7,5}} | collective-permute-start | bytes 7962632 | tf_op jit(solution)/shard_map/ppermute | solution.py:31
  950.1 60.3 %collective-permute-start.57 = (bf16[2,288,2304]{2,1,0:T(8,128)(2,1)}, bf16[2,288,2304]{2,1,0:T(8,128)(2,1)}, u32[]{:S(2)}, u32[]{:S(2)}) collective-permute-start(bf16[2,288,2304]{2,1,0:T(8,128)(2,1)} %get-tuple-element.311.refs_0_), channel_id=1, source_target_pairs={{0,2},{1,3},{2,0},{3,1},{4,6},{5,7},{6,4},{7,5}} | collective-permute-start | bytes 7962632 | tf_op jit(solution)/shard_map/ppermute | solution.py:31
  993.6 58.6 %collective-permute-start.56 = (bf16[2,288,2304]{2,1,0:T(8,128)(2,1)}, bf16[2,288,2304]{2,1,0:T(8,128)(2,1)}, u32[]{:S(2)}, u32[]{:S(2)}) collective-permute-start(bf16[2,288,2304]{2,1,0:T(8,128)(2,1)} %get-tuple-element.311.refs_0_), channel_id=1, source_target_pairs={{0,1},{1,0},{2,3},{3,2},{4,5},{5,4},{6,7},{7,6}} | collective-permute-start | bytes 7962632 | tf_op jit(solution)/shard_map/ppermute | solution.py:31
  1010.3 60.3 %collective-permute-start.58 = (bf16[2,288,2304]{2,1,0:T(8,128)(2,1)}, bf16[2,288,2304]{2,1,0:T(8,128)(2,1)}, u32[]{:S(2)}, u32[]{:S(2)}) collective-permute-start(bf16[2,288,2304]{2,1,0:T(8,128)(2,1)} %collective-permute-done.57.refs_2_), channel_id=1, source_target_pairs={{0,1},{1,0},{2,3},{3,2},{4,5},{5,4},{6,7},{7,6}} | collective-permute-start | bytes 7962632 | tf_op jit(solution)/shard_map/ppermute | solution.py:31
  1017.6 53.1 %collective-permute-start.50 = (bf16[2,288,768]{2,1,0:T(8,128)(2,1)}, bf16[2,288,768]{2,1,0:T(8,128)(2,1)}, u32[]{:S(2)}, u32[]{:S(2)}) collective-permute-start(bf16[2,288,768]{2,1,0:T(8,128)(2,1)} %get-tuple-element.309.refs_0_), channel_id=1, source_target_pairs={{0,2},{1,3},{2,0},{3,1},{4,6},{5,7},{6,4},{7,5}} | collective-permute-start | bytes 2654216 | tf_op jit(solution)/shard_map/ppermute | solution.py:31
  1017.9 62.3 %collective-permute-start.53 = (bf16[2,288,1536]{2,1,0:T(8,128)(2,1)}, bf16[2,288,1536]{2,1,0:T(8,128)(2,1)}, u32[]{:S(2)}, u32[]{:S(2)}) collective-permute-start(bf16[2,288,1536]{2,1,0:T(8,128)(2,1)} %get-tuple-element.310.refs_0_), channel_id=1, source_target_pairs={{0,1},{1,0},{2,3},{3,2},{4,5},{5,4},{6,7},{7,6}} | collective-permute-start | bytes 5308424 | tf_op jit(solution)/shard_map/ppermute | solution.py:31
  (39 other events, 726.5 us)
